TPU v7x, 8 devices: a whole 2x2x1 slice. The times are simulated.
8 devices in a mesh: dp: 8 (over z, y, x, core).
Axes of the slice: x: 2, y: 2, z: 1, core: 2. Of those that a mesh axis runs over, the one named last changes fastest.
Arguments:
- tokens: bfloat16 [8192, 1024], P('dp')
- w_one: bfloat16 [1024, 512], replicated
- w_two: bfloat16 [512, 256], replicated
- wi_one: bfloat16 [256, 512], replicated
- wi_two: bfloat16 [512, 256], replicated
- item_table: bfloat16 [262144, 256], P('dp')
- cand_ids: int32 [4096], replicated
- log_q: float32 [4096], replicated
- targets: int32 [8192], P('dp')
Outputs:
- output 1: float32 [], replicated
- output 2: float32 [262144, 256], P('dp')
- output 3: float32 [1024, 512], replicated
- output 4: float32 [512, 256], replicated
- output 5: float32 [256, 512], replicated
- output 6: float32 [512, 256], replicated
All inputs are finite; a program needn't handle non-finite values.
Results may differ from a plain program's by a relative error of at most 0.00982284.
Values are sent between devices in bfloat16 or wider.
A program may use at most 1 GiB of HBM per device.

v0:
```python
import math
import jax
import jax.numpy as jnp
from jax import lax
from jax.sharding import PartitionSpec as P

SCORE_GAIN = 3.0
HIT_VALUE = -1e9


def tower_fwd(row_block, w_in, w_out):
    pre_act = jnp.dot(row_block, w_in, preferred_element_type=jnp.float32)
    hidden = jax.nn.gelu(pre_act).astype(jnp.bfloat16)
    tower_out = jnp.dot(hidden, w_out, preferred_element_type=jnp.float32).astype(jnp.bfloat16)
    return pre_act, hidden, tower_out


def tower_back(row_block, w_out, pre_act, hidden, grad_out):
    dw_out = jnp.einsum("nf,nd->fd", hidden, grad_out, preferred_element_type=jnp.float32)
    grad_hidden = jnp.einsum("nd,fd->nf", grad_out, w_out, preferred_element_type=jnp.float32)
    gelu_back = jax.vjp(jax.nn.gelu, pre_act)[1]
    grad_pre = gelu_back(grad_hidden)[0].astype(jnp.bfloat16)
    dw_in = jnp.einsum("ne,nf->ef", row_block, grad_pre, preferred_element_type=jnp.float32)
    return grad_pre, dw_in, dw_out


def owned_rows(table_loc, row_ids, row_base):
    local_ids = row_ids - row_base
    num_rows = table_loc.shape[0]
    is_owned = (local_ids >= 0) & (local_ids < num_rows)
    picked = jnp.take(table_loc, jnp.clip(local_ids, 0, num_rows - 1), axis=0)
    return jnp.where(is_owned[:, None], picked, 0)


def loss_grads(query, targ_vec, cand_vec, log_q, targ_ids, cand_ids, tok_total):
    logit_scale = SCORE_GAIN / math.sqrt(query.shape[1])
    z_targ = jnp.einsum("td,td->t", query, targ_vec, preferred_element_type=jnp.float32) * logit_scale
    z_cand = jnp.einsum("td,sd->ts", query, cand_vec, preferred_element_type=jnp.float32) * logit_scale - log_q[None, :]
    z_cand = jnp.where(targ_ids[:, None] == cand_ids[None, :], HIT_VALUE, z_cand)
    row_max = jnp.maximum(z_targ, jnp.max(z_cand, axis=1))
    e_targ = jnp.exp(z_targ - row_max)
    e_cand = jnp.exp(z_cand - row_max[:, None])
    denom_sum = e_targ + jnp.sum(e_cand, axis=1)
    loss_sum = jnp.sum(jnp.log(denom_sum) + row_max - z_targ)
    dz_targ = ((e_targ / denom_sum - 1.0) / tok_total).astype(jnp.bfloat16).astype(jnp.float32)
    dz_cand = (e_cand / denom_sum[:, None] / tok_total).astype(jnp.bfloat16)
    d_query = ((dz_targ[:, None] * targ_vec.astype(jnp.float32) + jnp.einsum("ts,sd->td", dz_cand, cand_vec, preferred_element_type=jnp.float32)) * logit_scale).astype(jnp.bfloat16)
    d_targ_vec = (logit_scale * dz_targ[:, None] * query.astype(jnp.float32)).astype(jnp.bfloat16)
    return loss_sum, d_query, d_targ_vec, dz_cand, logit_scale


def solution(mesh):
    num_dev = mesh.shape["dp"]

    def local_step(tokens, w_one, w_two, wi_one, wi_two, table_loc, cand_ids, log_q, targ_loc):
        my_index = lax.axis_index("dp")
        rows_loc = table_loc.shape[0]
        row_base = my_index * rows_loc
        tok_total = tokens.shape[0] * num_dev
        cand_mine = lax.psum_scatter(owned_rows(table_loc, cand_ids, row_base), "dp", scatter_dimension=0, tiled=True)
        c_pre, c_hidden, cand_vec_mine = tower_fwd(cand_mine, wi_one, wi_two)
        cand_vec = lax.all_gather(cand_vec_mine, "dp", axis=0, tiled=True)
        targ_all = lax.all_gather(targ_loc, "dp", axis=0, tiled=True)
        targ_raw = lax.psum_scatter(owned_rows(table_loc, targ_all, row_base), "dp", scatter_dimension=0, tiled=True)
        t_pre, t_hidden, targ_vec = tower_fwd(targ_raw, wi_one, wi_two)
        q_pre, q_hidden, query = tower_fwd(tokens, w_one, w_two)
        loss_sum, d_query, d_targ_vec, dz_cand, logit_scale = loss_grads(query, targ_vec, cand_vec, log_q, targ_loc, cand_ids, tok_total)
        d_cand_part = jnp.einsum("ts,td->sd", dz_cand, query, preferred_element_type=jnp.float32)
        d_cand_vec = (lax.psum_scatter(d_cand_part, "dp", scatter_dimension=0, tiled=True) * logit_scale).astype(jnp.bfloat16)
        dw_one, dw_two = tower_back(tokens, w_two, q_pre, q_hidden, d_query)[1:]
        t_grad_pre, dwi_one_t, dwi_two_t = tower_back(targ_raw, wi_two, t_pre, t_hidden, d_targ_vec)
        c_grad_pre, dwi_one_c, dwi_two_c = tower_back(cand_mine, wi_two, c_pre, c_hidden, d_cand_vec)
        d_targ_raw = jnp.einsum("nf,df->nd", t_grad_pre, wi_one, preferred_element_type=jnp.float32).astype(jnp.bfloat16)
        d_cand_raw = jnp.einsum("nf,df->nd", c_grad_pre, wi_one, preferred_element_type=jnp.float32).astype(jnp.bfloat16)
        weight_grads = lax.psum((dw_one, dw_two, dwi_one_t + dwi_one_c, dwi_two_t + dwi_two_c), "dp")
        back_cand = lax.all_gather(d_cand_raw, "dp", axis=0, tiled=True)
        back_targ = lax.all_gather(d_targ_raw, "dp", axis=0, tiled=True)
        local_ids = jnp.concatenate([cand_ids, targ_all]) - row_base
        local_ids = jnp.where((local_ids >= 0) & (local_ids < rows_loc), local_ids, rows_loc)
        d_table = jax.ops.segment_sum(jnp.concatenate([back_cand, back_targ]).astype(jnp.float32), local_ids, num_segments=rows_loc)
        loss = lax.psum(loss_sum, "dp") / tok_total
        return (loss, d_table) + tuple(weight_grads)

    return jax.shard_map(local_step, mesh=mesh, in_specs=(P("dp", None), P(), P(), P(), P(), P("dp", None), P(), P(), P("dp")), out_specs=(P(), P("dp", None), P(), P(), P(), P()), check_vma=False)
```

profile of v0, /device:TPU:0, one launch (start us, length us, event | category | flops | bytes accessed | tf_op | source)
XLA Modules:
  0.0 461.8 jit_solution(7788711792755021978)
XLA Ops:
  7.2 0.0 reduce-scatter.6.cloned.1.call-start
  7.2 0.9 compare_and_fusion.3
  8.1 0.7 fusion.44
  8.8 23.9 %gather_fusion.1 = bf16[4096,256]{1,0:T(8,128)(2,1)} fusion(bf16[32768,256]{1,0:T(8,128)(2,1)} %param.14, s32[4096]{0:T(1024)S(1)} %fusion.44), kind=kCustom, calls=%fused_computation.1 | custom fusion | bytes 4210688 | tf_op jit(solution)/shard_map/jit(_take)/gather | solution.py:31
  32.7 5.7 %select_select_fusion.1 = bf16[4096,256]{1,0:T(8,128)(2,1)} fusion(bf16[4096,256]{1,0:T(8,128)(2,1)} %gather_fusion.1, pred[4096]{0:T(1024)(128)(4,1)S(1)} %get-tuple-element.33, pred[4096]{0:T(1024)(128)(4,1)S(1)} %get-tuple-element.32), kind=kLoop, calls=%fused_computation.33 | loop fusion | flops 2097152 | bytes 4202496 | tf_op jit(solution)/shard_map/jit(_where)/select_n | solution.py:32
  38.5 0.0 reduce-scatter.4.cloned.1.call-start
  38.5 0.6 copy-done.21
  39.1 13.8 %all_gather.12 = s32[8192]{0:T(1024)S(1)} all-gather(s32[1024]{0:T(1024)S(1)} %copy-done.21), channel_id=1, replica_groups=mesh['dp'=8] {'dp'}, dimensions={0}, use_global_device_ids=true | all-gather | bytes 36864 | tf_op jit(solution)/shard_map/all_gather | solution.py:63
  53.0 39.1 %gather_fusion = bf16[8192,256]{1,0:T(8,128)(2,1)} fusion(bf16[32768,256]{1,0:T(8,128)(2,1)} %param.14, s32[8192]{0:T(1024)S(1)} %fusion.43), kind=kCustom, calls=%fused_computation | custom fusion | bytes 8421376 | tf_op jit(solution)/shard_map/jit(_take)/gather | solution.py:31
  92.1 9.7 %select_select_fusion = bf16[8192,256]{1,0:T(8,128)(2,1)} fusion(bf16[8192,256]{1,0:T(8,128)(2,1)} %gather_fusion, pred[8192]{0:T(1024)(128)(4,1)S(1)} %get-tuple-element.31, pred[8192]{0:T(1024)(128)(4,1)S(1)} %get-tuple-element.30), kind=kLoop, calls=%fused_computation.14 | loop fusion | flops 4194304 | bytes 8404992 | tf_op jit(solution)/shard_map/jit(_where)/select_n | solution.py:32
  101.8 0.0 reduce-scatter.4.cloned.1.call-update
  101.8 0.0 all-gather.4.cloned.1.call-start
  101.8 0.0 reduce-scatter.6.cloned.1.call-done
  101.9 0.8 copy-done.2
  102.7 1.2 fusion.57
  104.0 1.1 copy-done.8
  105.0 1.2 convolution_convert_fusion.4
  106.2 0.0 all-gather.4.cloned.1.call-update
  106.2 0.3 reduce-scatter.8.cloned.1.call-start
  106.6 4.1 multiply_convert_fusion.2
  110.7 1.2 convolution_convert_fusion.2
  112.0 32.4 %reduce-scatter.4.cloned.1.call-done = bf16[1024,256]{1,0:T(8,128)(2,1)} async-done(((bf16[8192,256]{1,0:T(8,128)(2,1)}), bf16[1024,256]{1,0:T(8,128)(2,1)}) %reduce-scatter.4.cloned.1.call-update) | async-done | bytes 524304 | tf_op jit(solution)/shard_map/reduce_scatter | solution.py:64
  144.4 1.5 fusion.56
  145.9 1.3 copy-done.3
  147.3 1.7 fusion.25
  149.0 19.8 %all-gather.4.cloned.1.call-done = bf16[4096,256]{1,0:T(8,128)(2,1)} async-done(((bf16[512,256]{1,0:T(8,128)(2,1)}), bf16[4096,256]{1,0:T(8,128)(2,1)}) %all-gather.4.cloned.1.call-update) | async-done | bytes 2097168 | tf_op jit(solution)/shard_map/all_gather | solution.py:62
  168.8 5.7 %fusion.4 = (f32[1024]{0:T(1024)S(1)}, f32[1024,4096]{1,0:T(8,128)S(1)}) fusion(f32[4096]{0:T(1024)S(1)} %copy-done.20, s32[4096]{0:T(1024)S(1)} %copy-done.18, s32[1024]{0:T(1024)S(1)} %copy-done.21, bf16[1024,256]{1,0:T(8,128)(2,1)} %convolution_convert_fusion.2, bf16[4096,256]{1,0:T(8,128)(2,1)} %all-gather.4.cloned.1.call-done), kind=kOutput, calls=%fused_computation.10 | convolution fusion | flops 2168454144 | bytes 19439616 | tf_op jit(solution)/shard_map/td,sd->ts/dot_general | solution.py:38
  174.5 6.0 %fusion.2 = f32[1024]{0:T(1024)S(1)} fusion(f32[1024,4096]{1,0:T(8,128)S(1)} %get-tuple-element.41, f32[1024]{0:T(1024)S(1)} %multiply_maximum_fusion, f32[4096]{0:T(1024)S(1)} %copy-done.20, s32[4096]{0:T(1024)S(1)} %copy-done.18, s32[1024]{0:T(1024)S(1)} %copy-done.21), kind=kLoop, calls=%fused_computation.8 | loop fusion | flops 25164800 | bytes 16822272 | tf_op jit(solution)/shard_map/reduce_sum | solution.py:43
  180.5 0.6 fusion.46
  181.1 7.5 %multiply_convert_fusion = bf16[1024,4096]{1,0:T(8,128)(2,1)S(1)} fusion(f32[1024,4096]{1,0:T(8,128)S(1)} %get-tuple-element.41, f32[1024]{0:T(1024)S(1)} %get-tuple-element.34, f32[1024]{0:T(1024)S(1)} %multiply_maximum_fusion, f32[4096]{0:T(1024)S(1)} %copy-done.20, s32[4096]{0:T(1024)S(1)} %copy-done.18, s32[1024]{0:T(1024)S(1)} %copy-done.21), kind=kLoop, calls=%fused_computation.3 | loop fusion | flops 33554432 | bytes 25210880 | tf_op jit(solution)/shard_map/convert_element_type | solution.py:46
  188.6 3.4 copy-done.1
  192.0 4.6 fusion.58
  196.6 0.0 reduce-scatter.8.cloned.1.call-update
  196.7 0.0 all-reduce.3.cloned.1.call-start
  196.7 6.4 %fusion.24 = bf16[1024,256]{1,0:T(8,128)(2,1)S(1)} fusion(bf16[1024,4096]{1,0:T(8,128)(2,1)} %copy-done.1, bf16[4096,256]{1,0:T(8,128)(2,1)} %all-gather.4.cloned.1.call-done, bf16[1024,256]{1,0:T(8,128)(2,1)} %get-tuple-element.43, f32[1024]{0:T(1024)S(1)} %get-tuple-element.37), kind=kOutput, calls=%fused_computation.44 | convolution fusion | flops 2148794368 | bytes 11538432 | tf_op jit(solution)/shard_map/ts,sd->td/dot_general | solution.py:47
  203.2 1.3 fusion.59
  204.5 0.7 copy-done.4
  205.2 2.1 fusion.21
  207.3 5.8 %convolution_bitcast_fusion = f32[1024,512]{0,1:T(8,128)} fusion(bf16[1024,1024]{1,0:T(8,128)(2,1)S(1)} %copy-done, f32[1024,512]{1,0:T(8,128)} %get-tuple-element.39, bf16[1024,256]{1,0:T(8,128)(2,1)} %copy-done.27, bf16[512,256]{1,0:T(8,128)(2,1)} %param.11), kind=kOutput, calls=%fused_computation.36 | convolution fusion | flops 1352663040 | bytes 7077888 | tf_op jit(solution)/shard_map/ne,nf->ef/dot_general | solution.py:23
  213.0 26.2 %reduce-scatter.8.cloned.1.call-done = f32[512,256]{1,0:T(8,128)} async-done(((f32[4096,256]{1,0:T(8,128)}), f32[512,256]{1,0:T(8,128)}) %reduce-scatter.8.cloned.1.call-update) | async-done | bytes 524304 | tf_op jit(solution)/shard_map/reduce_scatter | solution.py:69
  239.3 2.1 fusion.42
  241.3 0.1 copy-done.14
  241.4 1.8 convolution_add_fusion.1
  243.2 0.9 fusion.33
  244.1 0.8 copy-done.7
  244.9 0.3 fusion.60
  245.2 1.3 convolution_add_fusion.2
  246.5 0.0 all-reduce.3.cloned.1.call-update
  246.5 0.0 all-gather.8.cloned.1.call-start
  246.5 1.3 convolution_convert_fusion
  247.8 0.0 all-gather.8.cloned.1.call-update
  247.8 0.0 all-gather.6.cloned.1.call-start
  247.9 2.1 convolution_convert_fusion.3
  250.0 0.0 all-gather.6.cloned.1.call-update
  250.0 0.1 and_select_fusion
  250.1 23.1 %psum.35 = f32[]{:T(128)} all-reduce(f32[]{:T(128)} %get-tuple-element.35), channel_id=1, replica_groups=mesh['dp'=8] {'dp'}, use_global_device_ids=true, to_apply=%region_5.6 | all-reduce | flops 1 | bytes 8 | tf_op jit(solution)/shard_map/psum | solution.py:81
  273.8 37.4 %all-reduce.3.cloned.1.call-done = (f32[1024,512]{0,1:T(8,128)}, f32[512,256]{1,0:T(8,128)}, f32[256,512]{1,0:T(8,128)}, f32[512,256]{1,0:T(8,128)}) async-done(((f32[1024,512]{0,1:T(8,128)}, f32[512,256]{1,0:T(8,128)}, f32[256,512]{1,0:T(8,128)}, f32[512,256]{1,0:T(8,128)}), (f32[1024,512]{0,1:T(8,128)}, f32[512,256]{1,0:T(8,128)}, f32[256,512]{1,0:T(8,128)}, ...) | async-done | bytes 3670032 | tf_op jit(solution)/shard_map/psum | solution.py:75
  311.2 2.9 copy.17
  314.1 30.2 %all-gather.8.cloned.1.call-done = bf16[8192,256]{1,0:T(8,128)(2,1)} async-done(((bf16[1024,256]{1,0:T(8,128)(2,1)}), bf16[8192,256]{1,0:T(8,128)(2,1)}) %all-gather.8.cloned.1.call-update) | async-done | bytes 4194320 | tf_op jit(solution)/shard_map/all_gather | solution.py:77
  344.3 23.8 %all-gather.6.cloned.1.call-done = bf16[4096,256]{1,0:T(8,128)(2,1)} async-done(((bf16[512,256]{1,0:T(8,128)(2,1)}), bf16[4096,256]{1,0:T(8,128)(2,1)}) %all-gather.6.cloned.1.call-update) | async-done | bytes 2097168 | tf_op jit(solution)/shard_map/all_gather | solution.py:76
  368.1 83.2 %scatter_custom_fusion = f32[32768,256]{1,0:T(8,128)} fusion(s32[12288]{0:T(1024)S(1)} %bitcast.38, f32[]{:T(128)} %constant.34.clone.1, bf16[8192,256]{1,0:T(8,128)(2,1)} %all-gather.8.cloned.1.call-done, bf16[]{:T(256)} %constant.46, bf16[4096,256]{1,0:T(8,128)(2,1)} %all-gather.6.cloned.1.call-done), kind=kCustom, calls=%fused_computation.4 | custom fusion | flops 15728640 | bytes 39845896 | tf_op jit(solution)/shard_map/scatter-add | solution.py:80
  451.3 0.8 copy.27
  452.1 0.8 copy.28
  452.9 0.8 copy.29
  (52 shorter events, 0.2 us)
Async XLA Ops:
  7.2 99.4 %copy-start = (bf16[1024,1024]{1,0:T(8,128)(2,1)S(1)}, bf16[1024,1024]{1,0:T(8,128)(2,1)}, u32[]{:S(2)}) copy-start(bf16[1024,1024]{1,0:T(8,128)(2,1)} %param.9) | copy-start | bytes 6291460
  7.2 94.7 %reduce-scatter.6.cloned.1.call-start = ((), (), s32[]{:S(2)}) async-start(), calls=%async_computation.4 | async-start | bytes 2359296 | tf_op jit(solution)/shard_map/reduce_scatter | solution.py:60
  38.5 0.7 copy-start.21
  38.5 105.9 %reduce-scatter.4.cloned.1.call-start = ((), (), s32[]{:S(2)}) async-start(), calls=%async_computation.3 | async-start | bytes 4718592 | tf_op jit(solution)/shard_map/reduce_scatter | solution.py:64
  101.8 1.0 copy-start.2
  101.8 3.3 copy-start.23
  101.8 67.0 %all-gather.4.cloned.1.call-start = ((), (), s32[]{:S(2)}) async-start(), calls=%async_computation.5 | async-start | bytes 2359296 | tf_op jit(solution)/shard_map/all_gather | solution.py:62
  103.9 1.1 copy-start.8
  106.2 133.0 %reduce-scatter.8.cloned.1.call-start = ((), (), s32[]{:S(2)}) async-start(), calls=%async_computation.6 | async-start | bytes 4718592 | tf_op jit(solution)/shard_map/reduce_scatter | solution.py:69
  106.6 4.2 copy-start.19
  144.4 2.9 copy-start.11
  144.4 2.9 copy-start.24
  145.9 1.4 copy-start.3
  147.3 21.5 %copy-start.18 = (s32[4096]{0:T(1024)S(1)}, s32[4096]{0:T(1024)}, u32[]{:S(2)}) copy-start(s32[4096]{0:T(1024)} %param.15) | copy-start | bytes 49156
  147.3 21.5 %copy-start.20 = (f32[4096]{0:T(1024)S(1)}, f32[4096]{0:T(1024)}, u32[]{:S(2)}) copy-start(f32[4096]{0:T(1024)} %param.16) | copy-start | bytes 49156
  181.1 10.9 %copy-start.12 = (bf16[1024,256]{1,0:T(8,128)(2,1)S(1)}, bf16[1024,256]{1,0:T(8,128)(2,1)}, u32[]{:S(2)}) copy-start(bf16[1024,256]{1,0:T(8,128)(2,1)} %convolution_convert_fusion.2) | copy-start | bytes 1572868
  188.6 3.4 copy-start.1
  196.7 114.5 %all-reduce.3.cloned.1.call-start = ((), (), s32[]{:S(2)}) async-start(), calls=%async_computation.9 | async-start | bytes 7340032 | tf_op jit(solution)/shard_map/psum | solution.py:75
  196.7 7.8 %copy-start.13 = (bf16[1024,256]{1,0:T(8,128)(2,1)S(1)}, bf16[1024,256]{1,0:T(8,128)(2,1)}, u32[]{:S(2)}) copy-start(bf16[1024,256]{1,0:T(8,128)(2,1)} %convolution_convert_fusion.2) | copy-start | bytes 1572868
  203.2 4.1 copy-start.27
  203.2 2.0 copy-start.4
  203.2 2.0 copy-start.25
  239.2 2.1 copy-start.5
  239.3 2.1 copy-start.14
  241.4 1.8 copy-start.9
  241.4 1.8 copy-start.22
  241.4 1.8 copy-start.26
  243.2 1.7 copy-start.10
  243.2 2.0 copy-start.6
  244.1 0.8 copy-start.7
  246.5 97.8 %all-gather.8.cloned.1.call-start = ((), (), s32[]{:S(2)}) async-start(), calls=%async_computation.8 | async-start | bytes 4718592 | tf_op jit(solution)/shard_map/all_gather | solution.py:77
  247.8 120.3 %all-gather.6.cloned.1.call-start = ((), (), s32[]{:S(2)}) async-start(), calls=%async_computation.7 | async-start | bytes 2359296 | tf_op jit(solution)/shard_map/all_gather | solution.py:76
  368.1 83.2 %copy-start.17 = (f32[512,256]{1,0:T(8,128)S(1)}, f32[512,256]{1,0:T(8,128)}, u32[]{:S(2)}) copy-start(f32[512,256]{1,0:T(8,128)} %get-tuple-element.47) | copy-start | bytes 1572868
  368.1 84.0 %copy-start.16 = (f32[256,512]{1,0:T(8,128)S(1)}, f32[256,512]{1,0:T(8,128)}, u32[]{:S(2)}) copy-start(f32[256,512]{1,0:T(8,128)} %get-tuple-element.48) | copy-start | bytes 1572868
  451.3 1.6 copy-start.15
Sparse Core Ops, SparseCore 0:
  38.6 35.3 reduce-scatter.5
  101.9 42.4 reduce-scatter.3
  146.8 21.9 all-gather.3
  196.8 42.4 reduce-scatter.7
  246.6 64.5 all-reduce.2
  313.4 30.8 all-gather.7
  346.1 21.9 all-gather.5
where the time goes:
time: 468 us; the launch traced here: 462 us
  waiting for transfers between devices  170 us (36%)
  other arithmetic  114 us (24%)
  local copies, waits for them, and re-layouts  77.1 us (16%)
  matrix products  46.5 us (10%)
  blocking collectives  36.8 us (8%)
  between operations  16.4 us (4%)
    scatter-add x1, other arithmetic, local_step(): jax.ops.segment_sum(jnp.concatenate([back_cand, back_targ]).astype(jnp.fl...  83.2 us
    gather x2, local copies, waits for them, and re-layouts, owned_rows(): picked = jnp.take(table_loc, jnp.clip(local_ids, 0, num_rows - 1), axis=0)  63 us
    psum x1, waiting for transfers between devices, local_step(): lax.psum((dw_one, dw_two, dwi_one_t + dwi_one_c, dwi_two_t + dwi_two_c),...  37.4 us
    reduce_scatter x1, waiting for transfers between devices, local_step(): lax.psum_scatter(owned_rows(table_loc, targ_all, row_base), 'dp', scatter...  32.4 us
    all_gather x1, waiting for transfers between devices, local_step(): back_targ = lax.all_gather(d_targ_raw, 'dp', axis=0, tiled=True)  30.2 us
    reduce_scatter x1, waiting for transfers between devices, local_step(): lax.psum_scatter(d_cand_part, 'dp', scatter_dimension=0, tiled=True)  26.2 us
    all_gather x1, waiting for transfers between devices, local_step(): back_cand = lax.all_gather(d_cand_raw, 'dp', axis=0, tiled=True)  23.8 us
    psum x1, blocking collectives, local_step(): loss = lax.psum(loss_sum, 'dp') / tok_total  23.1 us
  transfers between devices with their start and end apart: 7, of which 6 were waited for; matrix products, arithmetic and copies ran while one was open for 18% of the time, Pallas kernels for 0%

commit v1 on v0

--- a/solution.py
+++ b/solution.py
@@ -1,7 +1,10 @@
+import functools
 import math
 import jax
 import jax.numpy as jnp
 from jax import lax
+from jax.experimental import pallas as pl
+from jax.experimental.pallas import tpu as pltpu
 from jax.sharding import PartitionSpec as P
 
 SCORE_GAIN = 3.0
@@ -32,21 +35,161 @@
     return jnp.where(is_owned[:, None], picked, 0)
 
 
-def loss_grads(query, targ_vec, cand_vec, log_q, targ_ids, cand_ids, tok_total):
-    logit_scale = SCORE_GAIN / math.sqrt(query.shape[1])
-    z_targ = jnp.einsum("td,td->t", query, targ_vec, preferred_element_type=jnp.float32) * logit_scale
-    z_cand = jnp.einsum("td,sd->ts", query, cand_vec, preferred_element_type=jnp.float32) * logit_scale - log_q[None, :]
-    z_cand = jnp.where(targ_ids[:, None] == cand_ids[None, :], HIT_VALUE, z_cand)
-    row_max = jnp.maximum(z_targ, jnp.max(z_cand, axis=1))
-    e_targ = jnp.exp(z_targ - row_max)
-    e_cand = jnp.exp(z_cand - row_max[:, None])
-    denom_sum = e_targ + jnp.sum(e_cand, axis=1)
-    loss_sum = jnp.sum(jnp.log(denom_sum) + row_max - z_targ)
-    dz_targ = ((e_targ / denom_sum - 1.0) / tok_total).astype(jnp.bfloat16).astype(jnp.float32)
-    dz_cand = (e_cand / denom_sum[:, None] / tok_total).astype(jnp.bfloat16)
-    d_query = ((dz_targ[:, None] * targ_vec.astype(jnp.float32) + jnp.einsum("ts,sd->td", dz_cand, cand_vec, preferred_element_type=jnp.float32)) * logit_scale).astype(jnp.bfloat16)
-    d_targ_vec = (logit_scale * dz_targ[:, None] * query.astype(jnp.float32)).astype(jnp.bfloat16)
-    return loss_sum, d_query, d_targ_vec, dz_cand, logit_scale
+GROUP = 16
+BATCH = 128
+
+
+def scatter_body(ids_s, ids_v, cand_ref, targ_ref, out_ref, acc, g2, sem):
+    rows = out_ref.shape[0]
+    width = out_ref.shape[1]
+    n_cand = cand_ref.shape[0]
+    n_all = n_cand + targ_ref.shape[0]
+    zero_rows = 256
+
+    @pl.loop(0, rows // zero_rows)
+    def _(i):
+        acc[pl.ds(i * zero_rows, zero_rows), :] = jnp.zeros((zero_rows, width), jnp.float32)
+
+    row_i = lax.broadcasted_iota(jnp.int32, (BATCH, BATCH), 0) // GROUP
+    col_i = lax.broadcasted_iota(jnp.int32, (BATCH, BATCH), 1) // GROUP
+    same_group = row_i == col_i
+
+    def one_batch(b, src, src_base):
+        idr = jnp.broadcast_to(ids_v[pl.ds(b, 1), :], (BATCH, BATCH))
+        same = jnp.where((idr == idr.T) & same_group, 1.0, 0.0).astype(jnp.bfloat16)
+        g2[...] = jnp.dot(same, src[pl.ds(pl.multiple_of(b * BATCH - src_base, BATCH), BATCH), :], preferred_element_type=jnp.float32)
+        for g in range(BATCH // GROUP):
+            idx = [ids_s[b * BATCH + g * GROUP + r] for r in range(GROUP)]
+            old = [acc[pl.ds(idx[r], 1), :] for r in range(GROUP)]
+            new = [old[r] + g2[g * GROUP + r : g * GROUP + r + 1, :] for r in range(GROUP)]
+            for r in range(GROUP):
+                acc[pl.ds(idx[r], 1), :] = new[r]
+
+    @pl.loop(0, n_cand // BATCH)
+    def _(b):
+        one_batch(b, cand_ref, 0)
+
+    @pl.loop(n_cand // BATCH, n_all // BATCH)
+    def _(b):
+        one_batch(b, targ_ref, n_cand)
+
+    n_out = 8
+    step = rows // n_out
+    copies = [pltpu.make_async_copy(acc.at[pl.ds(i * step, step)], out_ref.at[pl.ds(i * step, step)], sem) for i in range(n_out)]
+    for c in copies:
+        c.start()
+    for c in copies:
+        c.wait()
+
+
+def scatter_rows(local_ids, back_cand, back_targ, rows_loc):
+    n_all = local_ids.shape[0]
+    width = back_cand.shape[1]
+    return pl.pallas_call(
+        scatter_body,
+        out_shape=jax.ShapeDtypeStruct((rows_loc, width), jnp.float32),
+        in_specs=[pl.BlockSpec(memory_space=pltpu.SMEM), pl.BlockSpec(memory_space=pltpu.VMEM), pl.BlockSpec(memory_space=pltpu.VMEM), pl.BlockSpec(memory_space=pltpu.VMEM)],
+        out_specs=pl.BlockSpec(memory_space=pl.ANY),
+        scratch_shapes=[pltpu.VMEM((rows_loc + 8, width), jnp.float32), pltpu.VMEM((BATCH, width), jnp.float32), pltpu.SemaphoreType.DMA],
+        compiler_params=pltpu.CompilerParams(vmem_limit_bytes=56 * 1024 * 1024),
+        name="scatter_rows",
+    )(local_ids, local_ids.reshape(n_all // BATCH, BATCH), back_cand, back_targ)
+
+
+TOK_BLK = 256
+CHUNK = 512
+
+
+def softmax_body(tok_total, h_ref, v_ref, u_ref, ut_ref, lq_ref, cid_ref, tid_ref, loss_ref, dh_ref, dv_ref, du_ref, z_s, dz_s):
+    step = pl.program_id(0)
+    n_cand, width = u_ref.shape
+    scale = SCORE_GAIN / math.sqrt(width)
+    h = h_ref[...]
+    hf = h.astype(jnp.float32)
+    vf = v_ref[...].astype(jnp.float32)
+    ht = hf.T.astype(jnp.bfloat16)
+    zt = jnp.sum(hf * vf, axis=1, keepdims=True) * scale
+    zt = jnp.broadcast_to(zt, (TOK_BLK, 128)).T[0:1, :]
+    tid = tid_ref[0]
+    m8 = jnp.broadcast_to(zt, (8, TOK_BLK))
+    n_chunk = n_cand // CHUNK
+
+    def z_chunk(i, m8):
+        off = pl.multiple_of(i * CHUNK, CHUNK)
+        z = jnp.dot(u_ref[pl.ds(off, CHUNK), :], ht, preferred_element_type=jnp.float32) * scale
+        lq = lq_ref[pl.ds(off, CHUNK), :]
+        cid = cid_ref[pl.ds(off, CHUNK), :]
+        z = z - jnp.concatenate([lq] * (TOK_BLK // 128), axis=1)
+        z = jnp.where(jnp.concatenate([cid] * (TOK_BLK // 128), axis=1) == tid, HIT_VALUE, z)
+        z_s[pl.ds(off, CHUNK), :] = z
+        return jnp.maximum(m8, jnp.max(z.reshape(CHUNK // 8, 8, TOK_BLK), axis=0))
+
+    m8 = lax.fori_loop(0, n_chunk, z_chunk, m8)
+    m = jnp.max(m8, axis=0, keepdims=True)
+
+    def e_chunk(i, s8):
+        off = pl.multiple_of(i * CHUNK, CHUNK)
+        e = jnp.exp(z_s[pl.ds(off, CHUNK), :] - m)
+        z_s[pl.ds(off, CHUNK), :] = e
+        return s8 + jnp.sum(e.reshape(CHUNK // 8, 8, TOK_BLK), axis=0)
+
+    s8 = lax.fori_loop(0, n_chunk, e_chunk, jnp.zeros((8, TOK_BLK), jnp.float32))
+    et = jnp.exp(zt - m)
+    den = et + jnp.sum(s8, axis=0, keepdims=True)
+    part = jnp.sum(jnp.log(den) + m - zt, axis=1, keepdims=True)
+    dzt = ((et / den - 1.0) / tok_total).astype(jnp.bfloat16).astype(jnp.float32)
+    inv = 1.0 / den / tok_total
+
+    @pl.when(step == 0)
+    def _():
+        loss_ref[...] = jnp.zeros_like(loss_ref)
+        du_ref[...] = jnp.zeros_like(du_ref)
+
+    loss_ref[...] += jnp.broadcast_to(part, loss_ref.shape)
+
+    def dz_chunk(i, dht):
+        off = pl.multiple_of(i * CHUNK, CHUNK)
+        dz = (z_s[pl.ds(off, CHUNK), :] * inv).astype(jnp.bfloat16)
+        du_ref[pl.ds(off, CHUNK), :] += jnp.dot(dz, h, preferred_element_type=jnp.float32)
+        return dht + jnp.dot(ut_ref[:, pl.ds(off, CHUNK)], dz, preferred_element_type=jnp.float32)
+
+    dht = lax.fori_loop(0, n_chunk, dz_chunk, jnp.zeros((width, TOK_BLK), jnp.float32))
+    dzt_c = jnp.broadcast_to(dzt, (128, TOK_BLK)).T[:, 0:1]
+    dh_ref[...] = ((dzt_c * vf + dht.T) * scale).astype(jnp.bfloat16)
+    dv_ref[...] = (scale * dzt_c * hf).astype(jnp.bfloat16)
+
+
+def softmax_grads(query, targ_vec, cand_vec, log_q, targ_ids, cand_ids, tok_total):
+    n_tok, width = query.shape
+    n_cand = cand_vec.shape[0]
+    steps = n_tok // TOK_BLK
+    whole = lambda s: (0, 0)
+    lq_b = jnp.broadcast_to(log_q[:, None], (n_cand, 128))
+    cid_b = jnp.broadcast_to(cand_ids[:, None], (n_cand, 128))
+    return pl.pallas_call(
+        functools.partial(softmax_body, tok_total),
+        grid=(steps,),
+        out_shape=(jax.ShapeDtypeStruct((8, 128), jnp.float32), jax.ShapeDtypeStruct((n_tok, width), jnp.bfloat16), jax.ShapeDtypeStruct((n_tok, width), jnp.bfloat16), jax.ShapeDtypeStruct((n_cand, width), jnp.float32)),
+        in_specs=[
+            pl.BlockSpec((TOK_BLK, width), lambda s: (s, 0)),
+            pl.BlockSpec((TOK_BLK, width), lambda s: (s, 0)),
+            pl.BlockSpec((n_cand, width), whole),
+            pl.BlockSpec((width, n_cand), whole),
+            pl.BlockSpec((n_cand, 128), whole),
+            pl.BlockSpec((n_cand, 128), whole),
+            pl.BlockSpec((1, 1, TOK_BLK), lambda s: (s, 0, 0)),
+        ],
+        out_specs=(
+            pl.BlockSpec((8, 128), whole),
+            pl.BlockSpec((TOK_BLK, width), lambda s: (s, 0)),
+            pl.BlockSpec((TOK_BLK, width), lambda s: (s, 0)),
+            pl.BlockSpec((n_cand, width), whole),
+        ),
+        scratch_shapes=[pltpu.VMEM((n_cand, TOK_BLK), jnp.float32), pltpu.VMEM((8, 128), jnp.bfloat16)],
+        compiler_params=pltpu.CompilerParams(vmem_limit_bytes=48 * 1024 * 1024, dimension_semantics=("arbitrary",)),
+        cost_estimate=pl.CostEstimate(flops=6 * n_tok * n_cand * width, bytes_accessed=16 << 20, transcendentals=n_tok * n_cand),
+        name="softmax_grads",
+    )(query, targ_vec, cand_vec, cand_vec.T, lq_b, cid_b, targ_ids.reshape(steps, 1, TOK_BLK))
 
 
 def solution(mesh):
@@ -64,8 +207,9 @@
         targ_raw = lax.psum_scatter(owned_rows(table_loc, targ_all, row_base), "dp", scatter_dimension=0, tiled=True)
         t_pre, t_hidden, targ_vec = tower_fwd(targ_raw, wi_one, wi_two)
         q_pre, q_hidden, query = tower_fwd(tokens, w_one, w_two)
-        loss_sum, d_query, d_targ_vec, dz_cand, logit_scale = loss_grads(query, targ_vec, cand_vec, log_q, targ_loc, cand_ids, tok_total)
-        d_cand_part = jnp.einsum("ts,td->sd", dz_cand, query, preferred_element_type=jnp.float32)
+        logit_scale = SCORE_GAIN / math.sqrt(query.shape[1])
+        loss_part, d_query, d_targ_vec, d_cand_part = softmax_grads(query, targ_vec, cand_vec, log_q, targ_loc, cand_ids, tok_total)
+        loss_sum = loss_part[0, 0]
         d_cand_vec = (lax.psum_scatter(d_cand_part, "dp", scatter_dimension=0, tiled=True) * logit_scale).astype(jnp.bfloat16)
         dw_one, dw_two = tower_back(tokens, w_two, q_pre, q_hidden, d_query)[1:]
         t_grad_pre, dwi_one_t, dwi_two_t = tower_back(targ_raw, wi_two, t_pre, t_hidden, d_targ_vec)
@@ -77,7 +221,7 @@
         back_targ = lax.all_gather(d_targ_raw, "dp", axis=0, tiled=True)
         local_ids = jnp.concatenate([cand_ids, targ_all]) - row_base
         local_ids = jnp.where((local_ids >= 0) & (local_ids < rows_loc), local_ids, rows_loc)
-        d_table = jax.ops.segment_sum(jnp.concatenate([back_cand, back_targ]).astype(jnp.float32), local_ids, num_segments=rows_loc)
+        d_table = scatter_rows(local_ids, back_cand, back_targ, rows_loc)
         loss = lax.psum(loss_sum, "dp") / tok_total
         return (loss, d_table) + tuple(weight_grads)
 

time: 468 us -> 446 us (0.953); the launches traced: 462 us -> 445 us
  other arithmetic: 114 us -> 18.3 us
  Pallas kernels: 0 us -> 83.7 us
  matrix products: 46.5 us -> 31.9 us
  local copies, waits for them, and re-layouts: 77.1 us -> 84.2 us
    pallas_call x0 -> x2, Pallas kernels: none -> 83.7 us  [the longest x1 55.8 us: scatter_rows(): pl.pallas_call(scatter_body, out_shape=jax.ShapeDtypeStruct((rows_loc, wi...]
    scatter-add x1 -> x0, other arithmetic: 83.2 us -> none  [local_step(): jax.ops.segment_sum(jnp.concatenate([back_cand, back_targ]).astype(jnp.fl...]
    dot_general x3 -> x0, matrix products: 16.7 us -> none  [the longest x1 6.45 us: loss_grads(): jnp.einsum('ts,sd->td', dz_cand, cand_vec, preferred_element_type=jnp.flo...]
    convert_element_type x1 -> x0, other arithmetic: 7.52 us -> none  [loss_grads(): dz_cand = (e_cand / denom_sum[:, None] / tok_total).astype(jnp.bfloat16)]
    reduce_sum x1 -> x0, other arithmetic: 6.01 us -> none  [loss_grads(): denom_sum = e_targ + jnp.sum(e_cand, axis=1)]
    broadcast_in_dim x0 -> x2, local copies, waits for them, and re-layouts: none -> 4.92 us  [the longest x1 2.94 us: softmax_grads(): cid_b = jnp.broadcast_to(cand_ids[:, None], (n_cand, 128))]
    unnamed x60 -> x56, local copies, waits for them, and re-layouts: 14.1 us -> 11.7 us
where the time goes in v1:
time: 446 us; the launch traced here: 445 us
  waiting for transfers between devices  173 us (39%)
  local copies, waits for them, and re-layouts  84.2 us (19%)
  Pallas kernels  83.7 us (19%)
  blocking collectives  36.6 us (8%)
  matrix products  31.9 us (7%)
  other arithmetic  18.3 us (4%)
  between operations  16.2 us (4%)
    gather x2, local copies, waits for them, and re-layouts, owned_rows(): picked = jnp.take(table_loc, jnp.clip(local_ids, 0, num_rows - 1), axis=0)  63 us
    pallas_call x1, Pallas kernels, scatter_rows(): pl.pallas_call(scatter_body, out_shape=jax.ShapeDtypeStruct((rows_loc, wi...  55.8 us
    psum x1, waiting for transfers between devices, local_step(): lax.psum((dw_one, dw_two, dwi_one_t + dwi_one_c, dwi_two_t + dwi_two_c),...  36.2 us
    reduce_scatter x1, waiting for transfers between devices, local_step(): lax.psum_scatter(owned_rows(table_loc, targ_all, row_base), 'dp', scatter...  32.3 us
    all_gather x1, waiting for transfers between devices, local_step(): back_targ = lax.all_gather(d_targ_raw, 'dp', axis=0, tiled=True)  30.2 us
    reduce_scatter x1, waiting for transfers between devices, local_step(): lax.psum_scatter(d_cand_part, 'dp', scatter_dimension=0, tiled=True)  30 us
    pallas_call x1, Pallas kernels, softmax_grads(): pl.pallas_call(functools.partial(softmax_body, tok_total), grid=(steps,),...  27.9 us
    all_gather x1, waiting for transfers between devices, local_step(): back_cand = lax.all_gather(d_cand_raw, 'dp', axis=0, tiled=True)  23.8 us
  transfers between devices with their start and end apart: 7, of which 6 were waited for; matrix products, arithmetic and copies ran while one was open for 18% of the time, Pallas kernels for 0%

profile of v1, /device:TPU:0, one launch (start us, length us, event | category | flops | bytes accessed | tf_op | source)
XLA Modules:
  0.0 444.6 jit_solution(16518289349189657901)
XLA Ops:
  7.2 0.0 reduce-scatter.6.cloned.1.call-start
  7.2 0.9 compare_and_fusion.3
  8.1 0.7 fusion.31
  8.8 23.9 %gather_fusion.1 = bf16[4096,256]{1,0:T(8,128)(2,1)} fusion(bf16[32768,256]{1,0:T(8,128)(2,1)} %param.14, s32[4096]{0:T(1024)S(1)} %fusion.31), kind=kCustom, calls=%fused_computation.1 | custom fusion | bytes 4210688 | tf_op jit(solution)/shard_map/jit(_take)/gather | solution.py:34
  32.7 5.7 %select_select_fusion.1 = bf16[4096,256]{1,0:T(8,128)(2,1)} fusion(bf16[4096,256]{1,0:T(8,128)(2,1)} %gather_fusion.1, pred[4096]{0:T(1024)(128)(4,1)S(1)} %get-tuple-element.33, pred[4096]{0:T(1024)(128)(4,1)S(1)} %get-tuple-element.32), kind=kLoop, calls=%fused_computation.21 | loop fusion | flops 2097152 | bytes 4202496 | tf_op jit(solution)/shard_map/jit(_where)/select_n | solution.py:35
  38.5 0.0 reduce-scatter.6.cloned.1.call-update
  38.5 0.0 reduce-scatter.4.cloned.1.call-start
  38.5 0.6 copy-done.2
  39.1 13.8 %all_gather.12 = s32[8192]{0:T(1024)S(1)} all-gather(s32[1024]{0:T(1024)S(1)} %copy-done.2), channel_id=1, replica_groups=mesh['dp'=8] {'dp'}, dimensions={0}, use_global_device_ids=true | all-gather | bytes 36864 | tf_op jit(solution)/shard_map/all_gather | solution.py:206
  53.0 39.1 %gather_fusion = bf16[8192,256]{1,0:T(8,128)(2,1)} fusion(bf16[32768,256]{1,0:T(8,128)(2,1)} %param.14, s32[8192]{0:T(1024)S(1)} %fusion.30), kind=kCustom, calls=%fused_computation | custom fusion | bytes 8421376 | tf_op jit(solution)/shard_map/jit(_take)/gather | solution.py:34
  92.1 9.7 %select_select_fusion = bf16[8192,256]{1,0:T(8,128)(2,1)} fusion(bf16[8192,256]{1,0:T(8,128)(2,1)} %gather_fusion, pred[8192]{0:T(1024)(128)(4,1)S(1)} %get-tuple-element.31, pred[8192]{0:T(1024)(128)(4,1)S(1)} %get-tuple-element.30), kind=kLoop, calls=%fused_computation.2 | loop fusion | flops 4194304 | bytes 8404992 | tf_op jit(solution)/shard_map/jit(_where)/select_n | solution.py:35
  101.8 0.0 reduce-scatter.4.cloned.1.call-update
  101.8 0.0 all-gather.4.cloned.1.call-start
  101.8 0.0 reduce-scatter.6.cloned.1.call-done
  101.9 0.8 copy-done.7
  102.7 1.2 fusion.41
  104.0 1.0 copy-done.13
  105.0 1.3 convolution_convert_fusion.4
  106.2 0.0 all-gather.4.cloned.1.call-update
  106.3 0.2 reduce-scatter.8.cloned.1.call-start
  106.5 4.1 multiply_convert_fusion.1
  110.6 1.0 copy-done.12
  111.6 0.4 convolution_convert_fusion.2.h_ref
  112.1 32.3 %reduce-scatter.4.cloned.1.call-done = bf16[1024,256]{1,0:T(8,128)(2,1)} async-done(((bf16[8192,256]{1,0:T(8,128)(2,1)}), bf16[1024,256]{1,0:T(8,128)(2,1)}) %reduce-scatter.4.cloned.1.call-update) | async-done | bytes 524304 | tf_op jit(solution)/shard_map/reduce_scatter | solution.py:207
  144.4 1.5 fusion.40
  145.9 1.4 copy-done.8
  147.2 1.6 convolution_convert_fusion.1.v_ref
  148.8 20.2 %all-gather.4.cloned.1.call-done = bf16[4096,256]{0,1:T(8,128)(2,1)} async-done(((bf16[512,256]{0,1:T(8,128)(2,1)}), bf16[4096,256]{0,1:T(8,128)(2,1)}) %all-gather.4.cloned.1.call-update) | async-done | bytes 2097168 | tf_op jit(solution)/shard_map/all_gather | solution.py:205
  169.1 4.1 copy.19.u_ref
  173.2 2.0 broadcast_in_dim.74.lq_ref
  175.2 2.9 broadcast_in_dim.75.cid_ref
  178.1 27.9 %softmax_grads.1 = (f32[8,128]{1,0:T(8,128)S(1)}, bf16[1024,256]{1,0:T(8,128)(2,1)S(1)}, bf16[1024,256]{1,0:T(8,128)(2,1)S(1)}, f32[4096,256]{1,0:T(8,128)}) custom-call(bf16[1024,256]{1,0:T(8,128)(2,1)S(1)} %convolution_convert_fusion.2.h_ref, bf16[1024,256]{1,0:T(8,128)(2,1)S(1)} %copy-done.5, bf16[4096,256]{1,0:T(8,128)(2,1)S(1)} %copy-done.1, ...), custom_call_target="tpu_custom_call" | custom-call | flops 6442450944 | bytes 16777216 | tf_op jit(solution)/shard_map/softmax_grads/pallas_call | solution.py:169
  206.0 0.8 copy-done.3
  206.8 0.0 reduce-scatter.8.cloned.1.call-update
  206.9 0.3 all-reduce.3.cloned.1.call-start
  207.2 2.5 fusion.42
  209.7 4.1 fusion.13
  213.8 5.7 %convolution_bitcast_fusion = f32[1024,512]{0,1:T(8,128)} fusion(bf16[1024,1024]{1,0:T(8,128)(2,1)S(1)} %copy-done, f32[1024,512]{1,0:T(8,128)} %get-tuple-element.35, bf16[1024,256]{1,0:T(8,128)(2,1)S(1)} %get-tuple-element.13, bf16[512,256]{1,0:T(8,128)(2,1)} %param.11), kind=kOutput, calls=%fused_computation.24 | convolution fusion | flops 1352663040 | bytes 7077888 | tf_op jit(solution)/shard_map/ne,nf->ef/dot_general | solution.py:26
  219.5 30.0 %reduce-scatter.8.cloned.1.call-done = f32[512,256]{1,0:T(8,128)} async-done(((f32[4096,256]{1,0:T(8,128)}), f32[512,256]{1,0:T(8,128)}) %reduce-scatter.8.cloned.1.call-update) | async-done | bytes 524304 | tf_op jit(solution)/shard_map/reduce_scatter | solution.py:213
  249.5 2.1 fusion.28
  251.6 1.6 convolution_add_fusion
  253.2 0.9 fusion.21
  254.1 0.8 copy-done.11
  254.9 0.3 fusion.43
  255.2 1.3 convolution_add_fusion.1
  256.5 0.0 all-reduce.3.cloned.1.call-update
  256.5 0.0 all-gather.8.cloned.1.call-start
  256.6 1.3 convolution_convert_fusion
  257.8 0.0 all-gather.8.cloned.1.call-update
  257.9 0.0 all-gather.6.cloned.1.call-start
  257.9 2.1 convolution_convert_fusion.3
  260.0 0.0 all-gather.6.cloned.1.call-update
  260.0 0.6 bitcast_select_fusion.ids_v
  260.6 0.6 and_select_fusion.ids_s
  261.3 0.5 slice.3
  261.8 22.8 %psum.35 = f32[]{:T(128)} all-reduce(f32[]{:T(128)} %bitcast.2), channel_id=1, replica_groups=mesh['dp'=8] {'dp'}, use_global_device_ids=true, to_apply=%region_2.3 | all-reduce | flops 1 | bytes 8 | tf_op jit(solution)/shard_map/psum | solution.py:225
  285.3 36.2 %all-reduce.3.cloned.1.call-done = (f32[1024,512]{0,1:T(8,128)}, f32[512,256]{1,0:T(8,128)}, f32[256,512]{1,0:T(8,128)}, f32[512,256]{1,0:T(8,128)}) async-done(((f32[1024,512]{0,1:T(8,128)}, f32[512,256]{1,0:T(8,128)}, f32[256,512]{1,0:T(8,128)}, f32[512,256]{1,0:T(8,128)}), (f32[1024,512]{0,1:T(8,128)}, f32[512,256]{1,0:T(8,128)}, f32[256,512]{1,0:T(8,128)}, ...) | async-done | bytes 3670032 | tf_op jit(solution)/shard_map/psum | solution.py:219
  321.5 2.9 copy.20
  324.3 30.2 %all-gather.8.cloned.1.call-done.targ_ref = bf16[8192,256]{1,0:T(8,128)(2,1)} async-done(((bf16[1024,256]{1,0:T(8,128)(2,1)}), bf16[8192,256]{1,0:T(8,128)(2,1)}) %all-gather.8.cloned.1.call-update) | async-done | bytes 4194320 | tf_op jit(solution)/shard_map/all_gather | solution.py:221
  354.6 23.8 %all-gather.6.cloned.1.call-done.cand_ref = bf16[4096,256]{1,0:T(8,128)(2,1)} async-done(((bf16[512,256]{1,0:T(8,128)(2,1)}), bf16[4096,256]{1,0:T(8,128)(2,1)}) %all-gather.6.cloned.1.call-update) | async-done | bytes 2097168 | tf_op jit(solution)/shard_map/all_gather | solution.py:220
  378.4 55.8 %scatter_rows.1 = f32[32768,256]{1,0:T(8,128)} custom-call(s32[12288]{0:T(1024)} %and_select_fusion.ids_s, s32[96,128]{1,0:T(8,128)} %bitcast_select_fusion.ids_v, bf16[4096,256]{1,0:T(8,128)(2,1)} %all-gather.6.cloned.1.call-done.cand_ref, bf16[8192,256]{1,0:T(8,128)(2,1)} %all-gather.8.cloned.1.call-done.targ_ref), custom_call_target="tpu_custom_call" | custom-call | tf_op jit(solution)/shard_map/scatter_rows/pallas_call | solution.py:88
  434.2 0.8 copy.26
  435.0 0.8 copy.27
  435.8 0.8 copy.28
  (47 shorter events, 0.1 us)
Async XLA Ops:
  7.2 99.3 %copy-start = (bf16[1024,1024]{1,0:T(8,128)(2,1)S(1)}, bf16[1024,1024]{1,0:T(8,128)(2,1)}, u32[]{:S(2)}) copy-start(bf16[1024,1024]{1,0:T(8,128)(2,1)} %param.9) | copy-start | bytes 6291460
  7.2 94.7 %reduce-scatter.6.cloned.1.call-start = ((), (), s32[]{:S(2)}) async-start(), calls=%async_computation.4 | async-start | bytes 2359296 | tf_op jit(solution)/shard_map/reduce_scatter | solution.py:203
  38.5 0.7 copy-start.2
  38.5 105.9 %reduce-scatter.4.cloned.1.call-start = ((), (), s32[]{:S(2)}) async-start(), calls=%async_computation.3 | async-start | bytes 4718592 | tf_op jit(solution)/shard_map/reduce_scatter | solution.py:207
  101.8 1.0 copy-start.7
  101.8 3.2 copy-start.23
  101.8 67.3 %all-gather.4.cloned.1.call-start = ((), (), s32[]{:S(2)}) async-start(), calls=%async_computation.5 | async-start | bytes 2359296 | tf_op jit(solution)/shard_map/all_gather | solution.py:205
  103.9 1.0 copy-start.13
  106.3 5.3 %copy-start.20 = (bf16[512,256]{1,0:T(8,128)(2,1)S(1)}, bf16[512,256]{1,0:T(8,128)(2,1)}, u32[]{:S(2)}) copy-start(bf16[512,256]{1,0:T(8,128)(2,1)} %param.11) | copy-start | bytes 786436
  106.3 143.2 %reduce-scatter.8.cloned.1.call-start = ((), (), s32[]{:S(2)}) async-start(), calls=%async_computation.6 | async-start | bytes 4718592 | tf_op jit(solution)/shard_map/reduce_scatter | solution.py:213
  110.6 1.0 copy-start.12
  145.8 1.4 copy-start.8
  148.8 24.3 %copy-start.21 = (f32[4096]{0:T(1024)S(1)}, f32[4096]{0:T(1024)}, u32[]{:S(2)}) copy-start(f32[4096]{0:T(1024)} %param.16) | copy-start | bytes 49156
  173.1 2.0 copy-start.19
  173.2 4.9 %copy-start.1 = (bf16[4096,256]{1,0:T(8,128)(2,1)S(1)}, bf16[4096,256]{1,0:T(8,128)(2,1)}, u32[]{:S(2)}) copy-start(bf16[4096,256]{1,0:T(8,128)(2,1)} %copy.19.u_ref) | copy-start | bytes 6291460
  173.2 4.9 %copy-start.5 = (bf16[1024,256]{1,0:T(8,128)(2,1)S(1)}, bf16[1024,256]{1,0:T(8,128)(2,1)}, u32[]{:S(2)}) copy-start(bf16[1024,256]{1,0:T(8,128)(2,1)} %convolution_convert_fusion.1.v_ref) | copy-start | bytes 1572868
  206.0 0.8 copy-start.3
  206.9 2.8 copy-start.4
  206.9 114.6 %all-reduce.3.cloned.1.call-start = ((), (), s32[]{:S(2)}) async-start(), calls=%async_computation.9 | async-start | bytes 7340032 | tf_op jit(solution)/shard_map/psum | solution.py:219
  207.1 2.6 copy-start.24
  249.5 2.1 copy-start.9
  251.5 1.7 copy-start.14
  251.5 1.7 copy-start.22
  251.5 1.7 copy-start.25
  253.2 1.7 copy-start.15
  253.2 2.0 copy-start.6
  253.2 2.0 copy-start.10
  254.1 0.8 copy-start.11
  256.5 98.0 %all-gather.8.cloned.1.call-start = ((), (), s32[]{:S(2)}) async-start(), calls=%async_computation.8 | async-start | bytes 4718592 | tf_op jit(solution)/shard_map/all_gather | solution.py:221
  257.9 120.5 %all-gather.6.cloned.1.call-start = ((), (), s32[]{:S(2)}) async-start(), calls=%async_computation.7 | async-start | bytes 2359296 | tf_op jit(solution)/shard_map/all_gather | solution.py:220
  324.3 109.8 %copy-start.18 = (f32[512,256]{1,0:T(8,128)S(1)}, f32[512,256]{1,0:T(8,128)}, u32[]{:S(2)}) copy-start(f32[512,256]{1,0:T(8,128)} %get-tuple-element.39) | copy-start | bytes 1572868
  324.3 110.7 %copy-start.17 = (f32[256,512]{1,0:T(8,128)S(1)}, f32[256,512]{1,0:T(8,128)}, u32[]{:S(2)}) copy-start(f32[256,512]{1,0:T(8,128)} %get-tuple-element.40) | copy-start | bytes 1572868
  434.2 1.6 copy-start.16
Sparse Core Ops, SparseCore 0:
  38.6 35.3 reduce-scatter.5
  101.9 42.4 reduce-scatter.3
  146.8 22.2 all-gather.3
  207.0 42.4 reduce-scatter.7
  256.6 64.7 all-reduce.2
  323.7 30.8 all-gather.7
  356.4 21.9 all-gather.5

commit v2 on v1

v2 whole, which is shorter than its diff:
```python
import functools
import math
import jax
import jax.numpy as jnp
from jax import lax
from jax.experimental import pallas as pl
from jax.experimental.pallas import tpu as pltpu
from jax.sharding import PartitionSpec as P

SCORE_GAIN = 3.0
HIT_VALUE = -1e9


def tower_fwd(row_block, w_in, w_out):
    pre_act = jnp.dot(row_block, w_in, preferred_element_type=jnp.float32)
    hidden = jax.nn.gelu(pre_act).astype(jnp.bfloat16)
    tower_out = jnp.dot(hidden, w_out, preferred_element_type=jnp.float32).astype(jnp.bfloat16)
    return pre_act, hidden, tower_out


def over_rows(a, b):
    return lax.dot_general(a, b, (((0,), (0,)), ((), ())), preferred_element_type=jnp.float32)


def by_transpose(a, b):
    return lax.dot_general(a, b, (((1,), (1,)), ((), ())), preferred_element_type=jnp.float32)


def tower_back(row_block, w_out, pre_act, hidden, grad_out):
    dw_out = over_rows(hidden, grad_out)
    grad_hidden = by_transpose(grad_out, w_out)
    gelu_back = jax.vjp(jax.nn.gelu, pre_act)[1]
    grad_pre = gelu_back(grad_hidden)[0].astype(jnp.bfloat16)
    dw_in = over_rows(row_block, grad_pre)
    return grad_pre, dw_in, dw_out


GROUP = 16
BATCH = 128
STAGE_ROWS = 2048
OUT_ROWS = 1024


def pick_body(ids_s, table, cand_out, targ_out, wide, stage, rows_f, stage_sem):
    rows_loc, width = table.shape
    lane = width // 2
    n_stage = rows_loc // STAGE_ROWS

    def stage_copy(i, slot):
        return pltpu.make_async_copy(table.at[pl.ds(i * STAGE_ROWS, STAGE_ROWS)], stage.at[slot], stage_sem.at[slot])

    for i in range(3):
        stage_copy(i, i).start()
    wide[pl.ds(2 * rows_loc, 8), :] = jnp.zeros((8, lane), jnp.float32)

    @pl.loop(0, n_stage)
    def _(i):
        slot = i % 4

        @pl.when(i + 3 < n_stage)
        def _():
            stage_copy(i + 3, (i + 3) % 4).start()

        stage_copy(i, slot).wait()

        @pl.loop(0, STAGE_ROWS // 128)
        def _(j):
            block = stage[slot, pl.ds(pl.multiple_of(j * 128, 128), 128), :].astype(jnp.float32)
            base = pl.multiple_of((i * STAGE_ROWS + j * 128) * 2, 256)
            wide[pl.ds(base, 128, 2), :] = block[:, :lane]
            wide[pl.ds(base + 1, 128, 2), :] = block[:, lane:]

    def fill(out, first):
        @pl.loop(0, out.shape[0] // BATCH)
        def _(b):
            for r in range(BATCH):
                at = pl.multiple_of(ids_s[first + b * BATCH + r], 2)
                rows_f[pl.ds(2 * r, 2), :] = wide[pl.ds(at, 2), :]
            rows = pl.ds(pl.multiple_of(b * BATCH, BATCH), BATCH)
            out[rows, :lane] = rows_f[pl.ds(0, BATCH, 2), :].astype(jnp.bfloat16)
            out[rows, lane:] = rows_f[pl.ds(1, BATCH, 2), :].astype(jnp.bfloat16)

    fill(cand_out, 0)
    fill(targ_out, cand_out.shape[0])


def pick_rows(ids_two, table_loc, n_cand):
    rows_loc, width = table_loc.shape
    n_targ = ids_two.shape[0] - n_cand
    vmem = pl.BlockSpec(memory_space=pltpu.VMEM)
    return pl.pallas_call(
        pick_body,
        out_shape=(jax.ShapeDtypeStruct((n_cand, width), jnp.bfloat16), jax.ShapeDtypeStruct((n_targ, width), jnp.bfloat16)),
        in_specs=[pl.BlockSpec(memory_space=pltpu.SMEM), pl.BlockSpec(memory_space=pl.ANY)],
        out_specs=(vmem, vmem),
        scratch_shapes=[
            pltpu.VMEM((2 * rows_loc + 8, width // 2), jnp.float32),
            pltpu.VMEM((4, STAGE_ROWS, width), jnp.bfloat16),
            pltpu.VMEM((2 * BATCH, width // 2), jnp.float32),
            pltpu.SemaphoreType.DMA((4,)),
        ],
        compiler_params=pltpu.CompilerParams(vmem_limit_bytes=50 * 1024 * 1024),
        name="pick_rows",
    )(ids_two, table_loc)


def scatter_body(ids_s, ids_v, cand_ref, targ_ref, out_ref, acc, g2, out_stage, sem):
    rows, width = out_ref.shape
    lane = width // 2
    n_cand = cand_ref.shape[0]
    n_all = n_cand + targ_ref.shape[0]

    @pl.loop(0, 2 * rows // 512)
    def _(i):
        acc[pl.ds(pl.multiple_of(i * 512, 512), 512), :] = jnp.zeros((512, lane), jnp.float32)

    row_i = lax.broadcasted_iota(jnp.int32, (BATCH, BATCH), 0) // GROUP
    col_i = lax.broadcasted_iota(jnp.int32, (BATCH, BATCH), 1) // GROUP
    same_group = row_i == col_i

    def one_batch(b, src, src_base):
        idr = jnp.broadcast_to(ids_v[pl.ds(b, 1), :], (BATCH, BATCH))
        same = jnp.where((idr == idr.T) & same_group, 1.0, 0.0).astype(jnp.bfloat16)
        part = jnp.dot(same, src[pl.ds(pl.multiple_of(b * BATCH - src_base, BATCH), BATCH), :], preferred_element_type=jnp.float32)
        g2[pl.ds(0, BATCH, 2), :] = part[:, :lane]
        g2[pl.ds(1, BATCH, 2), :] = part[:, lane:]
        for g in range(BATCH // GROUP):
            idx = [pl.multiple_of(ids_s[b * BATCH + g * GROUP + r], 2) for r in range(GROUP)]
            new = [acc[pl.ds(idx[r], 2), :] + g2[pl.ds(2 * (g * GROUP + r), 2), :] for r in range(GROUP)]
            for r in range(GROUP):
                acc[pl.ds(idx[r], 2), :] = new[r]

    @pl.loop(0, n_cand // BATCH)
    def _(b):
        one_batch(b, cand_ref, 0)

    @pl.loop(n_cand // BATCH, n_all // BATCH)
    def _(b):
        one_batch(b, targ_ref, n_cand)

    n_out = rows // OUT_ROWS

    def out_copy(i, slot):
        return pltpu.make_async_copy(out_stage.at[slot], out_ref.at[pl.ds(i * OUT_ROWS, OUT_ROWS)], sem.at[slot])

    @pl.loop(0, n_out)
    def _(i):
        slot = i % 4

        @pl.when(i >= 4)
        def _():
            out_copy(i - 4, slot).wait()

        @pl.loop(0, OUT_ROWS // 128)
        def _(j):
            base = pl.multiple_of((i * OUT_ROWS + j * 128) * 2, 256)
            here = pl.ds(pl.multiple_of(j * 128, 128), 128)
            out_stage[slot, here, :lane] = acc[pl.ds(base, 128, 2), :]
            out_stage[slot, here, lane:] = acc[pl.ds(base + 1, 128, 2), :]

        out_copy(i, slot).start()

    for i in range(n_out - 4, n_out):
        out_copy(i, i % 4).wait()


def scatter_rows(ids_two, back_cand, back_targ, rows_loc):
    n_all = ids_two.shape[0]
    width = back_cand.shape[1]
    vmem = pl.BlockSpec(memory_space=pltpu.VMEM)
    return pl.pallas_call(
        scatter_body,
        out_shape=jax.ShapeDtypeStruct((rows_loc, width), jnp.float32),
        in_specs=[pl.BlockSpec(memory_space=pltpu.SMEM), vmem, vmem, vmem],
        out_specs=pl.BlockSpec(memory_space=pl.ANY),
        scratch_shapes=[
            pltpu.VMEM((2 * rows_loc + 8, width // 2), jnp.float32),
            pltpu.VMEM((2 * BATCH, width // 2), jnp.float32),
            pltpu.VMEM((4, OUT_ROWS, width), jnp.float32),
            pltpu.SemaphoreType.DMA((4,)),
        ],
        compiler_params=pltpu.CompilerParams(vmem_limit_bytes=52 * 1024 * 1024),
        cost_estimate=pl.CostEstimate(flops=60_000_000_000, bytes_accessed=40 << 20, transcendentals=0),
        name="scatter_rows",
    )(ids_two, ids_two.reshape(n_all // BATCH, BATCH), back_cand, back_targ)


TOK_BLK = 256
CHUNK = 512


def softmax_body(tok_total, h_ref, v_ref, u_ref, ut_ref, lq_ref, cid_ref, tid_ref, loss_ref, dh_ref, dv_ref, du_ref, z_s, dz_s):
    step = pl.program_id(0)
    n_cand, width = u_ref.shape
    scale = SCORE_GAIN / math.sqrt(width)
    h = h_ref[...]
    hf = h.astype(jnp.float32)
    vf = v_ref[...].astype(jnp.float32)
    ht = hf.T.astype(jnp.bfloat16)
    zt = jnp.sum(hf * vf, axis=1, keepdims=True) * scale
    zt = jnp.broadcast_to(zt, (TOK_BLK, 128)).T[0:1, :]
    tid = tid_ref[0]
    m8 = jnp.broadcast_to(zt, (8, TOK_BLK))
    n_chunk = n_cand // CHUNK

    def z_chunk(i, m8):
        off = pl.multiple_of(i * CHUNK, CHUNK)
        z = jnp.dot(u_ref[pl.ds(off, CHUNK), :], ht, preferred_element_type=jnp.float32) * scale
        lq = lq_ref[pl.ds(off, CHUNK), :]
        cid = cid_ref[pl.ds(off, CHUNK), :]
        z = z - jnp.concatenate([lq] * (TOK_BLK // 128), axis=1)
        z = jnp.where(jnp.concatenate([cid] * (TOK_BLK // 128), axis=1) == tid, HIT_VALUE, z)
        z_s[pl.ds(off, CHUNK), :] = z
        return jnp.maximum(m8, jnp.max(z.reshape(CHUNK // 8, 8, TOK_BLK), axis=0))

    m8 = lax.fori_loop(0, n_chunk, z_chunk, m8)
    m = jnp.max(m8, axis=0, keepdims=True)

    def e_chunk(i, s8):
        off = pl.multiple_of(i * CHUNK, CHUNK)
        e = jnp.exp(z_s[pl.ds(off, CHUNK), :] - m)
        z_s[pl.ds(off, CHUNK), :] = e
        return s8 + jnp.sum(e.reshape(CHUNK // 8, 8, TOK_BLK), axis=0)

    s8 = lax.fori_loop(0, n_chunk, e_chunk, jnp.zeros((8, TOK_BLK), jnp.float32))
    et = jnp.exp(zt - m)
    den = et + jnp.sum(s8, axis=0, keepdims=True)
    part = jnp.sum(jnp.log(den) + m - zt, axis=1, keepdims=True)
    dzt = ((et / den - 1.0) / tok_total).astype(jnp.bfloat16).astype(jnp.float32)
    inv = 1.0 / den / tok_total

    @pl.when(step == 0)
    def _():
        loss_ref[...] = jnp.zeros_like(loss_ref)
        du_ref[...] = jnp.zeros_like(du_ref)

    loss_ref[...] += jnp.broadcast_to(part, loss_ref.shape)

    def dz_chunk(i, dht):
        off = pl.multiple_of(i * CHUNK, CHUNK)
        dz = (z_s[pl.ds(off, CHUNK), :] * inv).astype(jnp.bfloat16)
        du_ref[pl.ds(off, CHUNK), :] += jnp.dot(dz, h, preferred_element_type=jnp.float32)
        return dht + jnp.dot(ut_ref[:, pl.ds(off, CHUNK)], dz, preferred_element_type=jnp.float32)

    dht = lax.fori_loop(0, n_chunk, dz_chunk, jnp.zeros((width, TOK_BLK), jnp.float32))
    dzt_c = jnp.broadcast_to(dzt, (128, TOK_BLK)).T[:, 0:1]
    dh_ref[...] = ((dzt_c * vf + dht.T) * scale).astype(jnp.bfloat16)
    dv_ref[...] = (scale * dzt_c * hf).astype(jnp.bfloat16)


def softmax_grads(query, targ_vec, cand_vec, log_q, targ_ids, cand_ids, tok_total):
    n_tok, width = query.shape
    n_cand = cand_vec.shape[0]
    steps = n_tok // TOK_BLK
    whole = lambda s: (0, 0)
    lq_b = jnp.broadcast_to(log_q[:, None], (n_cand, 128))
    cid_b = jnp.broadcast_to(cand_ids[:, None], (n_cand, 128))
    return pl.pallas_call(
        functools.partial(softmax_body, tok_total),
        grid=(steps,),
        out_shape=(jax.ShapeDtypeStruct((8, 128), jnp.float32), jax.ShapeDtypeStruct((n_tok, width), jnp.bfloat16), jax.ShapeDtypeStruct((n_tok, width), jnp.bfloat16), jax.ShapeDtypeStruct((n_cand, width), jnp.float32)),
        in_specs=[
            pl.BlockSpec((TOK_BLK, width), lambda s: (s, 0)),
            pl.BlockSpec((TOK_BLK, width), lambda s: (s, 0)),
            pl.BlockSpec((n_cand, width), whole),
            pl.BlockSpec((width, n_cand), whole),
            pl.BlockSpec((n_cand, 128), whole),
            pl.BlockSpec((n_cand, 128), whole),
            pl.BlockSpec((1, 1, TOK_BLK), lambda s: (s, 0, 0)),
        ],
        out_specs=(
            pl.BlockSpec((8, 128), whole),
            pl.BlockSpec((TOK_BLK, width), lambda s: (s, 0)),
            pl.BlockSpec((TOK_BLK, width), lambda s: (s, 0)),
            pl.BlockSpec((n_cand, width), whole),
        ),
        scratch_shapes=[pltpu.VMEM((n_cand, TOK_BLK), jnp.float32), pltpu.VMEM((8, 128), jnp.bfloat16)],
        compiler_params=pltpu.CompilerParams(vmem_limit_bytes=48 * 1024 * 1024, dimension_semantics=("arbitrary",)),
        cost_estimate=pl.CostEstimate(flops=6 * n_tok * n_cand * width, bytes_accessed=16 << 20, transcendentals=n_tok * n_cand),
        name="softmax_grads",
    )(query, targ_vec, cand_vec, cand_vec.T, lq_b, cid_b, targ_ids.reshape(steps, 1, TOK_BLK))


MESH = pl.DeviceIdType.MESH


def my_place():
    me = lax.axis_index("dp")
    return me, me // 4, (me // 2) % 2, me % 2


def peer_of(place, dy, dx, dc):
    me, y, x, c = place
    return me + dy * (4 - 8 * y) + dx * (2 - 4 * x) + dc * (1 - 2 * c)


def meet(place):
    barrier = pltpu.get_barrier_semaphore()
    for k in range(1, 8):
        pl.semaphore_signal(barrier, inc=1, device_id=(peer_of(place, k // 4, (k // 2) % 2, k % 2),), device_id_type=MESH)
    pl.semaphore_wait(barrier, 7)


def push(src, dst, send_sem, recv_sem, peer):
    copy = pltpu.make_async_remote_copy(src_ref=src, dst_ref=dst, send_sem=send_sem, recv_sem=recv_sem, device_id=(peer,), device_id_type=MESH)
    copy.start()
    return copy


class Reduce:
    def __init__(self, place, data, in_one, mid, in_xa, in_yb, part_a, part_b, in_ya, in_xb, send_sem, recv_sem):
        self.place, self.data = place, data
        self.in_one, self.mid, self.in_xa, self.in_yb = in_one, mid, in_xa, in_yb
        self.part_a, self.part_b, self.in_ya, self.in_xb = part_a, part_b, in_ya, in_xb
        self.send_sem, self.recv_sem = send_sem, recv_sem
        self.half = data.shape[3] // 2
        self.copies = []

    def push(self, k, src, dst, dy, dx, dc):
        copy = push(src, dst, self.send_sem.at[k], self.recv_sem.at[k], peer_of(self.place, dy, dx, dc))
        self.copies.append(copy)

    def one(self):
        c = self.place[3]
        self.push(0, self.data.at[:, :, 1 - c], self.in_one, 0, 0, 1)

    def two(self):
        _, y, x, c = self.place
        half = self.half
        self.copies[0].wait_recv()
        for i in range(2):
            for j in range(2):
                self.mid[i, j] = self.data[i, j, c] + self.in_one[i, j]
        self.push(1, self.mid.at[:, 1 - x, pl.ds(0, half)], self.in_xa, 0, 1, 0)
        self.push(2, self.mid.at[1 - y, :, pl.ds(half, half)], self.in_yb, 1, 0, 0)

    def three(self):
        _, y, x, c = self.place
        half = self.half
        self.copies[1].wait_recv()
        for i in range(2):
            self.part_a[i] = self.mid[i, x, 0:half] + self.in_xa[i]
        self.push(3, self.part_a.at[1 - y], self.in_ya, 1, 0, 0)
        self.copies[2].wait_recv()
        for i in range(2):
            self.part_b[i] = self.mid[y, i, half : 2 * half] + self.in_yb[i]
        self.push(4, self.part_b.at[1 - x], self.in_xb, 0, 1, 0)

    def last(self):
        _, y, x, c = self.place
        self.copies[3].wait_recv()
        first = self.part_a[y] + self.in_ya[...]
        self.copies[4].wait_recv()
        return first, self.part_b[x] + self.in_xb[...]

    def drain(self):
        for copy in self.copies:
            copy.wait_send()


def reduce_scratch(n, rows, width, dtype):
    half = rows // 2
    return [
        pltpu.VMEM((n, 2, 2, rows, width), dtype),
        pltpu.VMEM((n, 2, 2, rows, width), dtype),
        pltpu.VMEM((n, 2, half, width), dtype),
        pltpu.VMEM((n, 2, half, width), dtype),
        pltpu.VMEM((n, 2, half, width), dtype),
        pltpu.VMEM((n, 2, half, width), dtype),
        pltpu.VMEM((n, half, width), dtype),
        pltpu.VMEM((n, half, width), dtype),
        pltpu.SemaphoreType.DMA((n, 5)),
        pltpu.SemaphoreType.DMA((n, 5)),
    ]


class Gather:
    def __init__(self, place, full, send_sem, recv_sem):
        self.place, self.full = place, full
        self.send_sem, self.recv_sem = send_sem, recv_sem
        self.half = full.shape[3] // 2
        self.copies = []

    def push(self, k, ref, dy, dx, dc):
        copy = push(ref, ref, self.send_sem.at[k], self.recv_sem.at[k], peer_of(self.place, dy, dx, dc))
        self.copies.append(copy)

    def one(self):
        _, y, x, c = self.place
        half = self.half
        self.push(0, self.full.at[y, x, c, pl.ds(0, half)], 0, 1, 0)
        self.push(1, self.full.at[y, x, c, pl.ds(half, half)], 1, 0, 0)

    def two(self):
        _, y, x, c = self.place
        half = self.half
        self.copies[0].wait_recv()
        self.push(2, self.full.at[y, :, c, pl.ds(0, half)], 1, 0, 0)
        self.copies[1].wait_recv()
        self.push(3, self.full.at[:, x, c, pl.ds(half, half)], 0, 1, 0)

    def three(self):
        c = self.place[3]
        self.copies[2].wait_recv()
        self.copies[3].wait_recv()
        self.push(4, self.full.at[:, :, c], 0, 0, 1)

    def last(self):
        self.copies[4].wait_recv()

    def drain(self):
        for copy in self.copies:
            copy.wait_send()


def gather_sems():
    return [pltpu.SemaphoreType.DMA((5,)), pltpu.SemaphoreType.DMA((5,))]


def ids_body(mine, full, send_sem, recv_sem):
    place = my_place()
    meet(place)
    full[place[0]] = mine[...]
    copies = []
    for k in range(1, 8):
        copies.append(push(mine, full.at[place[0]], send_sem.at[k], recv_sem.at[k], peer_of(place, k // 4, (k // 2) % 2, k % 2)))
    for copy in copies:
        copy.wait()


def share_ids(targ_loc):
    vmem = pl.BlockSpec(memory_space=pltpu.VMEM)
    return pl.pallas_call(
        ids_body,
        out_shape=jax.ShapeDtypeStruct((8, 8, 128), jnp.int32),
        in_specs=[vmem],
        out_specs=vmem,
        scratch_shapes=[pltpu.SemaphoreType.DMA((8,)), pltpu.SemaphoreType.DMA((8,))],
        compiler_params=pltpu.CompilerParams(collective_id=0, has_side_effects=True),
        name="share_ids",
    )(targ_loc.reshape(8, 128))


PIECE = 256


def fetch_body(data_c, data_t, wi_one, wi_two, tokens, w_one, w_two, cand_raw, c_pre, c_hid, cand_vec, targ_raw, t_pre, t_hid, targ_vec, q_pre, q_hid, query, in_one, mid, in_xa, in_yb, part_a, part_b, in_ya, in_xb, rs_send, rs_recv, ag_send, ag_recv):
    place = my_place()
    me, y, x, c = place
    half = PIECE // 2
    meet(place)
    reduces = []
    for k in range(6):
        data = data_c.at[:, :, :, pl.ds(k * PIECE, PIECE)] if k < 2 else data_t.at[:, :, :, pl.ds((k - 2) * PIECE, PIECE)]
        reduces.append(Reduce(place, data, in_one.at[k], mid.at[k], in_xa.at[k], in_yb.at[k], part_a.at[k], part_b.at[k], in_ya.at[k], in_xb.at[k], rs_send.at[k], rs_recv.at[k]))
    ag = Gather(place, cand_vec, ag_send, ag_recv)

    def close(k, out, base):
        first, second = reduces[k].last()
        out[base : base + half, :] = first
        out[base + half : base + PIECE, :] = second

    def tower(rows_ref, at, w_in, w_out, pre_ref, hid_ref):
        pre, hid, vec = tower_fwd(rows_ref[at, :], w_in[...], w_out[...])
        pre_ref[at, :] = pre
        hid_ref[at, :] = hid
        return vec

    for k in range(6):
        reduces[k].one()
    reduces[0].two()
    reduces[1].two()
    reduces[2].two()
    query[0:256, :] = tower(tokens, slice(0, 256), w_one, w_two, q_pre, q_hid)
    reduces[0].three()
    reduces[1].three()
    reduces[3].two()
    query[256:512, :] = tower(tokens, slice(256, 512), w_one, w_two, q_pre, q_hid)
    close(0, cand_raw, 0)
    close(1, cand_raw, PIECE)
    cand_vec[y, x, c] = tower(cand_raw, slice(0, 512), wi_one, wi_two, c_pre, c_hid)
    ag.one()
    reduces[2].three()
    reduces[4].two()
    query[512:768, :] = tower(tokens, slice(512, 768), w_one, w_two, q_pre, q_hid)
    ag.two()
    reduces[3].three()
    reduces[5].two()
    query[768:1024, :] = tower(tokens, slice(768, 1024), w_one, w_two, q_pre, q_hid)
    close(2, targ_raw, 0)
    targ_vec[0:256, :] = tower(targ_raw, slice(0, 256), wi_one, wi_two, t_pre, t_hid)
    reduces[4].three()
    ag.three()
    close(3, targ_raw, PIECE)
    targ_vec[256:512, :] = tower(targ_raw, slice(256, 512), wi_one, wi_two, t_pre, t_hid)
    reduces[5].three()
    close(4, targ_raw, 2 * PIECE)
    targ_vec[512:768, :] = tower(targ_raw, slice(512, 768), wi_one, wi_two, t_pre, t_hid)
    close(5, targ_raw, 3 * PIECE)
    targ_vec[768:1024, :] = tower(targ_raw, slice(768, 1024), wi_one, wi_two, t_pre, t_hid)
    ag.last()
    for red in reduces:
        red.drain()
    ag.drain()


def fetch_rows(data_c, data_t, wi_one, wi_two, tokens, w_one, w_two):
    n_mine, width = data_c.shape[3:]
    n_tok = data_t.shape[3]
    ff = wi_one.shape[1]
    vmem = pl.BlockSpec(memory_space=pltpu.VMEM)

    def outs(n):
        return [jax.ShapeDtypeStruct((n, ff), jnp.float32), jax.ShapeDtypeStruct((n, ff), jnp.bfloat16)]

    def rows(n):
        return [jax.ShapeDtypeStruct((n, width), jnp.bfloat16)]

    full = [jax.ShapeDtypeStruct((2, 2, 2, n_mine, width), jnp.bfloat16)]
    return pl.pallas_call(
        fetch_body,
        out_shape=tuple(rows(n_mine) + outs(n_mine) + full + rows(n_tok) + outs(n_tok) + rows(n_tok) + outs(n_tok) + rows(n_tok)),
        in_specs=[vmem] * 7,
        out_specs=(vmem,) * 11,
        scratch_shapes=reduce_scratch(6, PIECE, width, jnp.bfloat16) + gather_sems(),
        compiler_params=pltpu.CompilerParams(vmem_limit_bytes=56 * 1024 * 1024, collective_id=1, has_side_effects=True),
        name="fetch_rows",
    )(data_c, data_t, wi_one, wi_two, tokens, w_one, w_two)


def back_body(d_part, loss_in, d_query, d_targ, tokens, q_pre, q_hid, w_two, targ_raw, t_pre, t_hid, cand_raw, c_pre, c_hid, wi_one, wi_two, back_t, back_c, w_mine, loss_out, *scratch):
    place = my_place()
    me, y, x, c = place
    rs_u, rs_w = scratch[0:10], scratch[10:20]
    at_send, at_recv, ac_send, ac_recv, l_send, l_recv, w_data, l_all = scratch[20:28]
    width = d_query.shape[1]
    scale = SCORE_GAIN / math.sqrt(width)
    meet(place)
    red_u = []
    for k in range(2):
        red_u.append(Reduce(place, d_part.at[:, :, :, pl.ds(k * PIECE, PIECE)], *[s.at[k] for s in rs_u]))
    red_w = Reduce(place, w_data, *[s.at[0] for s in rs_w])
    ag_t = Gather(place, back_t, at_send, at_recv)
    ag_c = Gather(place, back_c, ac_send, ac_recv)
    red_u[0].one()
    red_u[1].one()
    l_all[me] = loss_in[...]
    l_copies = []
    for k in range(1, 8):
        l_copies.append(push(loss_in, l_all.at[me], l_send.at[k], l_recv.at[k], peer_of(place, k // 4, (k // 2) % 2, k % 2)))

    def put(first, value):
        n = value.shape[0] // 8
        for b in range(8):
            w_data[b // 4, (b // 2) % 2, b % 2, first : first + n, :] = value[b * n : (b + 1) * n, :]

    t_q, dwi_one, dwi_two = tower_back(targ_raw[...], wi_two[...], t_pre[...], t_hid[...], d_targ[...])
    back_t[y, x, c] = by_transpose(t_q, wi_one[...]).astype(jnp.bfloat16)
    red_u[0].two()
    red_u[1].two()
    ag_t.one()
    _, dw_one, dw_two = tower_back(tokens[...], w_two[...], q_pre[...], q_hid[...], d_query[...])
    put(0, dw_one[:, :width])
    put(128, dw_one[:, width:])
    put(256, dw_two)
    red_u[0].three()
    red_u[1].three()
    ag_t.two()
    parts = []
    for k in range(2):
        first, second = red_u[k].last()
        parts += [first, second]
    d_cand = (jnp.concatenate(parts, axis=0) * scale).astype(jnp.bfloat16)
    c_q, dwi_one_c, dwi_two_c = tower_back(cand_raw[...], wi_two[...], c_pre[...], c_hid[...], d_cand)
    back_c[y, x, c] = by_transpose(c_q, wi_one[...]).astype(jnp.bfloat16)
    ag_c.one()
    dwi_one = dwi_one + dwi_one_c
    put(320, dwi_one[:, :width])
    put(352, dwi_one[:, width:])
    put(384, dwi_two + dwi_two_c)
    red_w.one()
    for copy in l_copies:
        copy.wait()
    loss_out[...] = jnp.sum(l_all[...], axis=0)
    ag_c.two()
    red_w.two()
    ag_t.three()
    red_w.three()
    ag_c.three()
    first, second = red_w.last()
    half = first.shape[0]
    w_mine[0:half, :] = first
    w_mine[half : 2 * half, :] = second
    ag_t.last()
    ag_c.last()
    for part in red_u + [red_w, ag_t, ag_c]:
        part.drain()


W_ROWS = 448


def back_rows(d_part, loss_part, *rest):
    n_mine, width = d_part.shape[3:]
    n_tok = rest[0].shape[0]
    vmem = pl.BlockSpec(memory_space=pltpu.VMEM)
    sems = [pltpu.SemaphoreType.DMA((8,)), pltpu.SemaphoreType.DMA((8,))]
    return pl.pallas_call(
        back_body,
        out_shape=(
            jax.ShapeDtypeStruct((2, 2, 2, n_tok, width), jnp.bfloat16),
            jax.ShapeDtypeStruct((2, 2, 2, n_mine, width), jnp.bfloat16),
            jax.ShapeDtypeStruct((W_ROWS, width), jnp.float32),
            jax.ShapeDtypeStruct((8, 128), jnp.float32),
        ),
        in_specs=[vmem] * 16,
        out_specs=(vmem,) * 4,
        scratch_shapes=reduce_scratch(2, PIECE, width, jnp.float32) + reduce_scratch(1, W_ROWS, width, jnp.float32) + gather_sems() + gather_sems() + sems + [pltpu.VMEM((2, 2, 2, W_ROWS, width), jnp.float32), pltpu.VMEM((8, 8, 128), jnp.float32)],
        compiler_params=pltpu.CompilerParams(vmem_limit_bytes=60 * 1024 * 1024, collective_id=2, has_side_effects=True),
        name="back_rows",
    )(d_part, loss_part, *rest)


def solution(mesh):
    num_dev = mesh.shape["dp"]

    def local_step(tokens, w_one, w_two, wi_one, wi_two, table_loc, cand_ids, log_q, targ_loc):
        my_index = lax.axis_index("dp")
        rows_loc, width = table_loc.shape
        n_cand = cand_ids.shape[0]
        tok_total = tokens.shape[0] * num_dev
        targ_all = share_ids(targ_loc).reshape(-1)
        local_ids = jnp.concatenate([cand_ids, targ_all]) - my_index * rows_loc
        ids_two = 2 * jnp.where((local_ids >= 0) & (local_ids < rows_loc), local_ids, rows_loc)
        data_c, data_t = pick_rows(ids_two, table_loc, n_cand)
        data_c = data_c.reshape(2, 2, 2, n_cand // 8, width)
        data_t = data_t.reshape(2, 2, 2, tokens.shape[0], width)
        cand_mine, c_pre, c_hid, cand_vec, targ_raw, t_pre, t_hid, targ_vec, q_pre, q_hid, query = fetch_rows(data_c, data_t, wi_one, wi_two, tokens, w_one, w_two)
        cand_vec = cand_vec.reshape(n_cand, width)
        loss_part, d_query, d_targ_vec, d_part = softmax_grads(query, targ_vec, cand_vec, log_q, targ_loc, cand_ids, tok_total)
        back_t, back_c, w_mine, loss = back_rows(d_part.reshape(2, 2, 2, n_cand // 8, width), loss_part, d_query, d_targ_vec, tokens, q_pre, q_hid, w_two, targ_raw, t_pre, t_hid, cand_mine, c_pre, c_hid, wi_one, wi_two)
        w_all = lax.all_gather(w_mine, "dp", axis=0)
        d_table = scatter_rows(ids_two, back_c.reshape(-1, width), back_t.reshape(-1, width), rows_loc)

        def pair(first, n):
            return jnp.concatenate([w_all[:, first : first + n].reshape(8 * n, width), w_all[:, first + n : first + 2 * n].reshape(8 * n, width)], axis=1)

        dw_one = pair(0, 128)
        dw_two = w_all[:, 256:320].reshape(-1, width)
        dwi_one = pair(320, 32)
        dwi_two = w_all[:, 384:448].reshape(-1, width)
        return loss[0, 0] / tok_total, d_table, dw_one, dw_two, dwi_one, dwi_two

    return jax.shard_map(local_step, mesh=mesh, in_specs=(P("dp", None), P(), P(), P(), P(), P("dp", None), P(), P(), P("dp")), out_specs=(P(), P("dp", None), P(), P(), P(), P()), check_vma=False)
```

time: 446 us -> 272 us (0.61)
  waiting for transfers between devices: 173 us -> 0.04 us
  Pallas kernels: 83.7 us -> 233 us
  local copies, waits for them, and re-layouts: 84.2 us -> 18.8 us
  blocking collectives: 36.6 us -> 0 us
  matrix products: 31.9 us -> 0 us
  other arithmetic: 18.3 us -> 3.3 us
    pallas_call x0 -> x4, Pallas kernels: none -> 156 us  [the longest x1 75.2 us: back_rows(): pl.pallas_call(back_body, out_shape=(jax.ShapeDtypeStruct((2, 2, 2, n_tok...]
    all_gather x3 -> x1, waiting for transfers between devices: 74.3 us -> 0.02 us  [local_step(): w_all = lax.all_gather(w_mine, 'dp', axis=0)]
    gather x2 -> x0, local copies, waits for them, and re-layouts: 63 us -> none  [owned_rows(): picked = jnp.take(table_loc, jnp.clip(local_ids, 0, num_rows - 1), axis=0)]
    reduce_scatter x3 -> x0, waiting for transfers between devices: 62.3 us -> none  [the longest x1 32.3 us: local_step(): lax.psum_scatter(owned_rows(table_loc, targ_all, row_base), 'dp', scatter...]
    psum x1 -> x0, waiting for transfers between devices: 36.2 us -> none  [local_step(): lax.psum((dw_one, dw_two, dwi_one_t + dwi_one_c, dwi_two_t + dwi_two_c),...]
    dot_general x16 -> x0, matrix products: 31.9 us -> none  [the longest x3 7.22 us: tower_back(): jnp.einsum('ne,nf->ef', row_block, grad_pre, preferred_element_type=jnp.f...]
    psum x1 -> x0, blocking collectives: 22.8 us -> none  [local_step(): loss = lax.psum(loss_sum, 'dp') / tok_total]
    select_n x4 -> x0, other arithmetic: 16.7 us -> none  [the longest x2 15.4 us: owned_rows(): return jnp.where(is_owned[:, None], picked, 0)]
  transfers between devices with their start and end apart: 7 -> 1, of which waited for: 6 -> 0; matrix products, arithmetic and copies ran while one was open for 18% -> 0% of each run, Pallas kernels for 0% -> 18%
where the time goes in v2:
time: 272 us
  Pallas kernels  233 us (86%)
  local copies, waits for them, and re-layouts  18.8 us (7%)
  between operations  16 us (6%)
  other arithmetic  3.3 us (1%)
    pallas_call x1, Pallas kernels, back_rows(): pl.pallas_call(back_body, out_shape=(jax.ShapeDtypeStruct((2, 2, 2, n_tok...  75.2 us
    pallas_call x1, Pallas kernels, fetch_rows(): pl.pallas_call(fetch_body, out_shape=tuple(rows(n_mine) + outs(n_mine) +...  50 us
    pallas_call x1, Pallas kernels, scatter_rows(): pl.pallas_call(scatter_body, out_shape=jax.ShapeDtypeStruct((rows_loc, wi...  49.8 us
    pallas_call x1, Pallas kernels, softmax_grads(): pl.pallas_call(functools.partial(softmax_body, tok_total), grid=(steps,),...  28 us
    pallas_call x1, Pallas kernels, pick_rows(): pl.pallas_call(pick_body, out_shape=(jax.ShapeDtypeStruct((n_cand, width)...  22.5 us
    pallas_call x1, Pallas kernels, share_ids(): pl.pallas_call(ids_body, out_shape=jax.ShapeDtypeStruct((8, 8, 128), jnp....  7.95 us
  transfers between devices with their start and end apart: 1, of which 0 were waited for; matrix products, arithmetic and copies ran while one was open for 0% of the time, Pallas kernels for 18%

profile of v2, /device:TPU:0, one launch (start us, length us, event | category | flops | bytes accessed | tf_op | source)
XLA Modules:
  0.0 271.5 jit_solution(10515341295089109911)
XLA Ops:
  7.2 0.0 all-gather.3.cloned.1.call-start
  7.2 7.9 %share_ids.1 = s32[8,8,128]{2,1,0:T(8,128)} custom-call(s32[8,128]{1,0:T(8,128)} %bitcast.33), custom_call_target="tpu_custom_call" | custom-call | tf_op jit(solution)/shard_map/share_ids/pallas_call | solution.py:433
  15.2 0.8 select_multiply_fusion.ids_s
  16.0 22.5 %pick_rows.1 = (bf16[4096,256]{1,0:T(8,128)(2,1)S(1)}, bf16[8192,256]{1,0:T(8,128)(2,1)}) custom-call(s32[12288]{0:T(1024)S(1)} %select_multiply_fusion.ids_s, bf16[32768,256]{1,0:T(8,128)(2,1)} %table.1), custom_call_target="tpu_custom_call" | custom-call | tf_op jit(solution)/shard_map/pick_rows/pallas_call | solution.py:91
  38.5 0.0 copy-start
  38.5 1.3 copy-done
  39.8 50.0 %fetch_rows.1 = (bf16[512,256]{1,0:T(8,128)(2,1)}, f32[512,512]{1,0:T(8,128)}, bf16[512,512]{1,0:T(8,128)(2,1)}, bf16[2,2,2,512,256]{4,3,2,1,0:T(8,128)(2,1)}, b...) custom-call(bf16[2,2,2,512,256]{4,3,2,1,0:T(8,128)(2,1)} %bitcast.30, ...), custom_call_target="tpu_custom_call" | custom-call | tf_op jit(solution)/shard_map/fetch_rows/pallas_call | solution.py:520
  89.8 0.0 copy-start.10
  89.8 4.1 %copy.17 = bf16[4096,256]{0,1:T(8,128)(2,1)} copy(bf16[4096,256]{1,0:T(8,128)(2,1)} %bitcast.31) | data formatting | bytes 4194304 | tf_op jit(solution)/shard_map/reshape | solution.py:639
  93.9 0.0 copy-start.9
  93.9 0.0 copy-done.10
  93.9 0.0 copy-start.1
  93.9 0.0 copy-start.5
  93.9 0.0 copy-start.6
  93.9 0.0 copy-start.7
  93.9 1.9 broadcast_in_dim.6.lq_ref
  95.8 0.0 copy-done.9
  95.8 3.0 %broadcast_in_dim.7.cid_ref = s32[4096,128]{1,0:T(8,128)} broadcast(s32[4096]{0:T(1024)S(1)} %copy-done.9), dimensions={0} | broadcast | bytes 2113536 | tf_op jit(solution)/shard_map/broadcast_in_dim | solution.py:257
  98.8 0.0 copy-done.1
  98.8 0.0 copy-done.5
  98.8 0.0 copy-done.6
  98.8 0.0 copy-done.7
  98.9 28.0 %softmax_grads.1 = (f32[8,128]{1,0:T(8,128)S(1)}, bf16[1024,256]{1,0:T(8,128)(2,1)S(1)}, bf16[1024,256]{1,0:T(8,128)(2,1)S(1)}, f32[4096,256]{1,0:T(8,128)}) custom-call(bf16[1024,256]{1,0:T(8,128)(2,1)S(1)} %copy-done.7, bf16[1024,256]{1,0:T(8,128)(2,1)S(1)} %copy-done.6, bf16[4096,256]{1,0:T(8,128)(2,1)S(1)} %bitcast.32, bf16[256,4096]{1,0:T(8,128)(2,1)} %bitcast.42, ...), custom_call_target="tpu_custom_call" | custom-call | flops 6442450944 | bytes 16777216 | tf_op jit(solution)/shard_map/softmax_grads/pallas_call | solution.py:258
  126.9 0.0 copy-start.2
  126.9 0.8 copy-done.2
  127.7 0.0 copy-start.3
  127.7 0.8 copy-done.3
  128.4 0.0 copy-start.4
  128.4 0.6 copy-done.4
  129.0 0.0 copy-start.8
  129.0 75.2 %back_rows.1 = (bf16[2,2,2,1024,256]{4,3,2,1,0:T(8,128)(2,1)}, bf16[2,2,2,512,256]{4,3,2,1,0:T(8,128)(2,1)}, f32[448,256]{1,0:T(8,128)}, f32[8,128]{1,0:T(8,128)}) custom-call(f32[2,2,2,512,256]{4,3,2,1,0:T(8,128)} %bitcast.35, f32[8,128]{1,0:T(8,128)} %copy-done.4, bf16[1024,256]{1,0:T(8,128)(2,1)} %copy-done.2, bf16[1024,256]{1,0:T(8,128)(2,1)} %copy-done.3, ...), custom_call_target="tpu_custom_call" | custom-call | tf_op jit(solution)/shard_map/back_rows/pallas_call | solution.py:608
  204.2 0.0 all-gather.3.cloned.1.call-update
  204.3 1.2 slice.21
  206.1 0.0 copy-done.8
  206.1 49.8 %scatter_rows.1 = f32[32768,256]{1,0:T(8,128)} custom-call(s32[12288]{0:T(1024)S(1)} %select_multiply_fusion.ids_s, s32[96,128]{1,0:T(8,128)S(1)} %fusion.ids_v, bf16[4096,256]{1,0:T(8,128)(2,1)} %bitcast.50, bf16[8192,256]{1,0:T(8,128)(2,1)} %bitcast.49), custom_call_target="tpu_custom_call" | custom-call | flops 60000002048 | bytes 41943040 | tf_op jit(solution)/shard_map/scatter_rows/pallas_call | solution.py:171
  255.9 0.0 all-gather.3.cloned.1.call-done
  256.0 1.7 fusion.4
  257.7 2.3 fusion.2
  260.0 1.1 fusion.3
  261.1 1.6 pad_maximum_fusion
  262.7 0.9 pad_maximum_fusion.1
  (1 shorter events, 0.0 us)
Async XLA Ops:
  7.2 248.8 %all-gather.3.cloned.1.call-start = ((), (), s32[]{:S(2)}) async-start(), calls=%async_computation | async-start | bytes 4128768 | tf_op jit(solution)/shard_map/all_gather | solution.py:642
  38.5 1.3 copy-start
  89.8 4.1 %copy-start.10 = (f32[4096]{0:T(1024)S(1)}, f32[4096]{0:T(1024)}, u32[]{:S(2)}) copy-start(f32[4096]{0:T(1024)} %param.16) | copy-start | bytes 49156
  93.9 2.0 copy-start.9
  93.9 5.0 %copy-start.1 = (bf16[2,2,2,512,256]{4,3,2,1,0:T(8,128)(2,1)S(1)}, bf16[2,2,2,512,256]{4,3,2,1,0:T(8,128)(2,1)}, u32[]{:S(2)}) copy-start(bf16[2,2,2,512,256]{4,3,2,1,0:T(8,128)(2,1)} %get-tuple-element.31) | copy-start | bytes 6291460
  93.9 5.0 %copy-start.5 = (s32[1024]{0:T(1024)S(1)}, s32[1024]{0:T(1024)}, u32[]{:S(2)}) copy-start(s32[1024]{0:T(1024)} %param.17) | copy-start | bytes 12292
  93.9 5.0 %copy-start.6 = (bf16[1024,256]{1,0:T(8,128)(2,1)S(1)}, bf16[1024,256]{1,0:T(8,128)(2,1)}, u32[]{:S(2)}) copy-start(bf16[1024,256]{1,0:T(8,128)(2,1)} %get-tuple-element.30.v_ref) | copy-start | bytes 1572868
  93.9 5.0 %copy-start.7 = (bf16[1024,256]{1,0:T(8,128)(2,1)S(1)}, bf16[1024,256]{1,0:T(8,128)(2,1)}, u32[]{:S(2)}) copy-start(bf16[1024,256]{1,0:T(8,128)(2,1)} %get-tuple-element.29.h_ref) | copy-start | bytes 1572868
  126.9 0.8 copy-start.2
  127.7 0.8 copy-start.3
  128.4 0.6 copy-start.4
  129.0 77.1 %copy-start.8 = (s32[8,8,128]{2,1,0:T(8,128)S(1)}, s32[8,8,128]{2,1,0:T(8,128)}, u32[]{:S(2)}) copy-start(s32[8,8,128]{2,1,0:T(8,128)} %share_ids.1) | copy-start | bytes 98308
Sparse Core Ops, SparseCore 0:
  204.4 28.6 all-gather.2

commit v3 on v2

--- a/solution.py
+++ b/solution.py
@@ -26,17 +26,22 @@
     return lax.dot_general(a, b, (((1,), (1,)), ((), ())), preferred_element_type=jnp.float32)
 
 
+def grad_through(grad_out, w_out, pre_act):
+    grad_hidden = by_transpose(grad_out, w_out)
+    gelu_back = jax.vjp(jax.nn.gelu, pre_act)[1]
+    return gelu_back(grad_hidden)[0].astype(jnp.bfloat16)
+
+
 def tower_back(row_block, w_out, pre_act, hidden, grad_out):
     dw_out = over_rows(hidden, grad_out)
-    grad_hidden = by_transpose(grad_out, w_out)
-    gelu_back = jax.vjp(jax.nn.gelu, pre_act)[1]
-    grad_pre = gelu_back(grad_hidden)[0].astype(jnp.bfloat16)
+    grad_pre = grad_through(grad_out, w_out, pre_act)
     dw_in = over_rows(row_block, grad_pre)
     return grad_pre, dw_in, dw_out
 
 
 GROUP = 16
 BATCH = 128
+SPARE = 256
 STAGE_ROWS = 2048
 OUT_ROWS = 1024
 
@@ -51,7 +56,7 @@
 
     for i in range(3):
         stage_copy(i, i).start()
-    wide[pl.ds(2 * rows_loc, 8), :] = jnp.zeros((8, lane), jnp.float32)
+    wide[pl.ds(2 * rows_loc, 2 * SPARE), :] = jnp.zeros((2 * SPARE, lane), jnp.float32)
 
     @pl.loop(0, n_stage)
     def _(i):
@@ -94,7 +99,7 @@
         in_specs=[pl.BlockSpec(memory_space=pltpu.SMEM), pl.BlockSpec(memory_space=pl.ANY)],
         out_specs=(vmem, vmem),
         scratch_shapes=[
-            pltpu.VMEM((2 * rows_loc + 8, width // 2), jnp.float32),
+            pltpu.VMEM((2 * (rows_loc + SPARE), width // 2), jnp.float32),
             pltpu.VMEM((4, STAGE_ROWS, width), jnp.bfloat16),
             pltpu.VMEM((2 * BATCH, width // 2), jnp.float32),
             pltpu.SemaphoreType.DMA((4,)),
@@ -174,7 +179,7 @@
         in_specs=[pl.BlockSpec(memory_space=pltpu.SMEM), vmem, vmem, vmem],
         out_specs=pl.BlockSpec(memory_space=pl.ANY),
         scratch_shapes=[
-            pltpu.VMEM((2 * rows_loc + 8, width // 2), jnp.float32),
+            pltpu.VMEM((2 * (rows_loc + SPARE), width // 2), jnp.float32),
             pltpu.VMEM((2 * BATCH, width // 2), jnp.float32),
             pltpu.VMEM((4, OUT_ROWS, width), jnp.float32),
             pltpu.SemaphoreType.DMA((4,)),
@@ -186,75 +191,82 @@
 
 
 TOK_BLK = 256
-CHUNK = 512
-
-
-def softmax_body(tok_total, h_ref, v_ref, u_ref, ut_ref, lq_ref, cid_ref, tid_ref, loss_ref, dh_ref, dv_ref, du_ref, z_s, dz_s):
+CHUNK = 256
+SUB = 64
+BACK_CHUNK = 512
+
+
+def softmax_body(tok_total, h_ref, v_ref, u_ref, lq_ref, cid_ref, tid_ref, loss_ref, dh_ref, dv_ref, du_ref, e_s, m_s, ut_s):
     step = pl.program_id(0)
     n_cand, width = u_ref.shape
     scale = SCORE_GAIN / math.sqrt(width)
-    h = h_ref[...]
-    hf = h.astype(jnp.float32)
-    vf = v_ref[...].astype(jnp.float32)
-    ht = hf.T.astype(jnp.bfloat16)
-    zt = jnp.sum(hf * vf, axis=1, keepdims=True) * scale
-    zt = jnp.broadcast_to(zt, (TOK_BLK, 128)).T[0:1, :]
-    tid = tid_ref[0]
-    m8 = jnp.broadcast_to(zt, (8, TOK_BLK))
-    n_chunk = n_cand // CHUNK
-
-    def z_chunk(i, m8):
-        off = pl.multiple_of(i * CHUNK, CHUNK)
-        z = jnp.dot(u_ref[pl.ds(off, CHUNK), :], ht, preferred_element_type=jnp.float32) * scale
-        lq = lq_ref[pl.ds(off, CHUNK), :]
-        cid = cid_ref[pl.ds(off, CHUNK), :]
-        z = z - jnp.concatenate([lq] * (TOK_BLK // 128), axis=1)
-        z = jnp.where(jnp.concatenate([cid] * (TOK_BLK // 128), axis=1) == tid, HIT_VALUE, z)
-        z_s[pl.ds(off, CHUNK), :] = z
-        return jnp.maximum(m8, jnp.max(z.reshape(CHUNK // 8, 8, TOK_BLK), axis=0))
-
-    m8 = lax.fori_loop(0, n_chunk, z_chunk, m8)
-    m = jnp.max(m8, axis=0, keepdims=True)
-
-    def e_chunk(i, s8):
-        off = pl.multiple_of(i * CHUNK, CHUNK)
-        e = jnp.exp(z_s[pl.ds(off, CHUNK), :] - m)
-        z_s[pl.ds(off, CHUNK), :] = e
-        return s8 + jnp.sum(e.reshape(CHUNK // 8, 8, TOK_BLK), axis=0)
-
-    s8 = lax.fori_loop(0, n_chunk, e_chunk, jnp.zeros((8, TOK_BLK), jnp.float32))
-    et = jnp.exp(zt - m)
-    den = et + jnp.sum(s8, axis=0, keepdims=True)
-    part = jnp.sum(jnp.log(den) + m - zt, axis=1, keepdims=True)
-    dzt = ((et / den - 1.0) / tok_total).astype(jnp.bfloat16).astype(jnp.float32)
-    inv = 1.0 / den / tok_total
 
     @pl.when(step == 0)
     def _():
         loss_ref[...] = jnp.zeros_like(loss_ref)
         du_ref[...] = jnp.zeros_like(du_ref)
-
+        for i in range(n_cand // 512):
+            ut_s[:, i * 512 : (i + 1) * 512] = u_ref[i * 512 : (i + 1) * 512, :].T
+
+    h = h_ref[...]
+    hf = h.astype(jnp.float32)
+    vf = v_ref[...].astype(jnp.float32)
+    ht = h.T
+    zt = jnp.sum(hf * vf, axis=1, keepdims=True) * scale
+    zt = jnp.broadcast_to(zt, (TOK_BLK, 128)).T[0:1, :]
+    tid = tid_ref[0]
+    lanes = TOK_BLK // 128
+
+    def forward(i, carry):
+        m8, s8 = carry
+        off = pl.multiple_of(i * CHUNK, CHUNK)
+        z_all = jnp.dot(u_ref[pl.ds(off, CHUNK), :], ht, preferred_element_type=jnp.float32)
+        for k in range(CHUNK // SUB):
+            rows = pl.ds(pl.multiple_of(off + k * SUB, SUB), SUB)
+            lq = jnp.concatenate([lq_ref[rows, :]] * lanes, axis=1)
+            cid = jnp.concatenate([cid_ref[rows, :]] * lanes, axis=1)
+            z = z_all[k * SUB : (k + 1) * SUB] * scale - lq
+            z = jnp.where(cid == tid, HIT_VALUE, z).reshape(SUB // 8, 8, TOK_BLK)
+            m_new = jnp.maximum(m8, jnp.max(z, axis=0))
+            e = jnp.exp(z - m_new[None])
+            s8 = s8 * jnp.exp(m8 - m_new) + jnp.sum(e, axis=0)
+            m8 = m_new
+            e_s[rows, :] = e.reshape(SUB, TOK_BLK)
+            m_s[pl.ds(pl.multiple_of(i * (8 * CHUNK // SUB) + 8 * k, 8), 8), :] = m8
+        return m8, s8
+
+    m8, s8 = lax.fori_loop(0, n_cand // CHUNK, forward, (jnp.broadcast_to(zt, (8, TOK_BLK)), jnp.zeros((8, TOK_BLK), jnp.float32)))
+    m = jnp.max(m8, axis=0, keepdims=True)
+    et = jnp.exp(zt - m)
+    den = et + jnp.sum(s8 * jnp.exp(m8 - m), axis=0, keepdims=True)
+    part = jnp.sum(jnp.log(den) + m - zt, axis=1, keepdims=True)
+    dzt = ((et / den - 1.0) / tok_total).astype(jnp.bfloat16).astype(jnp.float32)
+    inv = 1.0 / den / tok_total
     loss_ref[...] += jnp.broadcast_to(part, loss_ref.shape)
 
-    def dz_chunk(i, dht):
-        off = pl.multiple_of(i * CHUNK, CHUNK)
-        dz = (z_s[pl.ds(off, CHUNK), :] * inv).astype(jnp.bfloat16)
-        du_ref[pl.ds(off, CHUNK), :] += jnp.dot(dz, h, preferred_element_type=jnp.float32)
-        return dht + jnp.dot(ut_ref[:, pl.ds(off, CHUNK)], dz, preferred_element_type=jnp.float32)
-
-    dht = lax.fori_loop(0, n_chunk, dz_chunk, jnp.zeros((width, TOK_BLK), jnp.float32))
+    def backward(i, dht):
+        off = pl.multiple_of(i * BACK_CHUNK, BACK_CHUNK)
+        pieces = []
+        for k in range(BACK_CHUNK // SUB):
+            rows = pl.ds(pl.multiple_of(off + k * SUB, SUB), SUB)
+            m_k = m_s[pl.ds(pl.multiple_of(i * (8 * BACK_CHUNK // SUB) + 8 * k, 8), 8), :]
+            fac = jnp.exp(m_k - m) * inv
+            pieces.append((e_s[rows, :].reshape(SUB // 8, 8, TOK_BLK) * fac[None]).reshape(SUB, TOK_BLK).astype(jnp.bfloat16))
+        dz = jnp.concatenate(pieces, axis=0)
+        du_ref[pl.ds(off, BACK_CHUNK), :] += jnp.dot(dz, h, preferred_element_type=jnp.float32)
+        return dht + jnp.dot(ut_s[:, pl.ds(off, BACK_CHUNK)], dz, preferred_element_type=jnp.float32)
+
+    dht = lax.fori_loop(0, n_cand // BACK_CHUNK, backward, jnp.zeros((width, TOK_BLK), jnp.float32))
     dzt_c = jnp.broadcast_to(dzt, (128, TOK_BLK)).T[:, 0:1]
     dh_ref[...] = ((dzt_c * vf + dht.T) * scale).astype(jnp.bfloat16)
     dv_ref[...] = (scale * dzt_c * hf).astype(jnp.bfloat16)
 
 
-def softmax_grads(query, targ_vec, cand_vec, log_q, targ_ids, cand_ids, tok_total):
+def softmax_grads(query, targ_vec, cand_vec, lq_b, cid_b, targ_ids, tok_total):
     n_tok, width = query.shape
     n_cand = cand_vec.shape[0]
     steps = n_tok // TOK_BLK
     whole = lambda s: (0, 0)
-    lq_b = jnp.broadcast_to(log_q[:, None], (n_cand, 128))
-    cid_b = jnp.broadcast_to(cand_ids[:, None], (n_cand, 128))
     return pl.pallas_call(
         functools.partial(softmax_body, tok_total),
         grid=(steps,),
@@ -263,7 +275,6 @@
             pl.BlockSpec((TOK_BLK, width), lambda s: (s, 0)),
             pl.BlockSpec((TOK_BLK, width), lambda s: (s, 0)),
             pl.BlockSpec((n_cand, width), whole),
-            pl.BlockSpec((width, n_cand), whole),
             pl.BlockSpec((n_cand, 128), whole),
             pl.BlockSpec((n_cand, 128), whole),
             pl.BlockSpec((1, 1, TOK_BLK), lambda s: (s, 0, 0)),
@@ -274,11 +285,11 @@
             pl.BlockSpec((TOK_BLK, width), lambda s: (s, 0)),
             pl.BlockSpec((n_cand, width), whole),
         ),
-        scratch_shapes=[pltpu.VMEM((n_cand, TOK_BLK), jnp.float32), pltpu.VMEM((8, 128), jnp.bfloat16)],
+        scratch_shapes=[pltpu.VMEM((n_cand, TOK_BLK), jnp.float32), pltpu.VMEM((8 * n_cand // SUB, TOK_BLK), jnp.float32), pltpu.VMEM((width, n_cand), jnp.bfloat16)],
         compiler_params=pltpu.CompilerParams(vmem_limit_bytes=48 * 1024 * 1024, dimension_semantics=("arbitrary",)),
         cost_estimate=pl.CostEstimate(flops=6 * n_tok * n_cand * width, bytes_accessed=16 << 20, transcendentals=n_tok * n_cand),
         name="softmax_grads",
-    )(query, targ_vec, cand_vec, cand_vec.T, lq_b, cid_b, targ_ids.reshape(steps, 1, TOK_BLK))
+    )(query, targ_vec, cand_vec, lq_b, cid_b, targ_ids.reshape(steps, 1, TOK_BLK))
 
 
 MESH = pl.DeviceIdType.MESH
@@ -294,11 +305,15 @@
     return me + dy * (4 - 8 * y) + dx * (2 - 4 * x) + dc * (1 - 2 * c)
 
 
-def meet(place):
+def greet(place):
     barrier = pltpu.get_barrier_semaphore()
     for k in range(1, 8):
         pl.semaphore_signal(barrier, inc=1, device_id=(peer_of(place, k // 4, (k // 2) % 2, k % 2),), device_id_type=MESH)
-    pl.semaphore_wait(barrier, 7)
+
+
+def meet(place):
+    greet(place)
+    pl.semaphore_wait(pltpu.get_barrier_semaphore(), 7)
 
 
 def push(src, dst, send_sem, recv_sem, peer):
@@ -417,34 +432,58 @@
     return [pltpu.SemaphoreType.DMA((5,)), pltpu.SemaphoreType.DMA((5,))]
 
 
-def ids_body(mine, full, send_sem, recv_sem):
+def prepare_body(mine, lq_ref, cid_ref, tokens, w_one, w_two, full, lq_out, cid_out, q_pre, q_hid, query, send_sem, recv_sem):
     place = my_place()
-    meet(place)
+    greet(place)
+    for i in range(tokens.shape[0] // 256):
+        at = slice(i * 256, i * 256 + 256)
+        pre, hid, vec = tower_fwd(tokens[at, :], w_one[...], w_two[...])
+        q_pre[at, :] = pre
+        q_hid[at, :] = hid
+        query[at, :] = vec
+    pl.semaphore_wait(pltpu.get_barrier_semaphore(), 7)
     full[place[0]] = mine[...]
     copies = []
     for k in range(1, 8):
         copies.append(push(mine, full.at[place[0]], send_sem.at[k], recv_sem.at[k], peer_of(place, k // 4, (k // 2) % 2, k % 2)))
+
+    @pl.loop(0, lq_ref.shape[0])
+    def _(i):
+        rows = pl.ds(pl.multiple_of(i * 128, 128), 128)
+        lq_out[rows, :] = jnp.broadcast_to(lq_ref[pl.ds(i, 1), :], (128, 128)).T
+        cid_out[rows, :] = jnp.broadcast_to(cid_ref[pl.ds(i, 1), :], (128, 128)).T
+
     for copy in copies:
         copy.wait()
 
 
-def share_ids(targ_loc):
+def prepare(targ_loc, log_q, cand_ids, tokens, w_one, w_two):
+    n_cand = cand_ids.shape[0]
+    n_tok = tokens.shape[0]
+    ff, width = w_two.shape
     vmem = pl.BlockSpec(memory_space=pltpu.VMEM)
     return pl.pallas_call(
-        ids_body,
-        out_shape=jax.ShapeDtypeStruct((8, 8, 128), jnp.int32),
-        in_specs=[vmem],
-        out_specs=vmem,
+        prepare_body,
+        out_shape=(
+            jax.ShapeDtypeStruct((8, 8, 128), jnp.int32),
+            jax.ShapeDtypeStruct((n_cand, 128), jnp.float32),
+            jax.ShapeDtypeStruct((n_cand, 128), jnp.int32),
+            jax.ShapeDtypeStruct((n_tok, ff), jnp.float32),
+            jax.ShapeDtypeStruct((n_tok, ff), jnp.bfloat16),
+            jax.ShapeDtypeStruct((n_tok, width), jnp.bfloat16),
+        ),
+        in_specs=[vmem] * 6,
+        out_specs=(vmem,) * 6,
         scratch_shapes=[pltpu.SemaphoreType.DMA((8,)), pltpu.SemaphoreType.DMA((8,))],
-        compiler_params=pltpu.CompilerParams(collective_id=0, has_side_effects=True),
-        name="share_ids",
-    )(targ_loc.reshape(8, 128))
+        compiler_params=pltpu.CompilerParams(vmem_limit_bytes=40 * 1024 * 1024, collective_id=0, has_side_effects=True),
+        name="prepare",
+    )(targ_loc.reshape(8, 128), log_q.reshape(-1, 128), cand_ids.reshape(-1, 128), tokens, w_one, w_two)
 
 
 PIECE = 256
 
 
-def fetch_body(data_c, data_t, wi_one, wi_two, tokens, w_one, w_two, cand_raw, c_pre, c_hid, cand_vec, targ_raw, t_pre, t_hid, targ_vec, q_pre, q_hid, query, in_one, mid, in_xa, in_yb, part_a, part_b, in_ya, in_xb, rs_send, rs_recv, ag_send, ag_recv):
+def fetch_body(data_c, data_t, wi_one, wi_two, cand_raw, c_pre, c_hid, cand_vec, targ_raw, t_pre, t_hid, targ_vec, in_one, mid, in_xa, in_yb, part_a, part_b, in_ya, in_xb, rs_send, rs_recv, ag_send, ag_recv):
     place = my_place()
     me, y, x, c = place
     half = PIECE // 2
@@ -466,45 +505,42 @@
         hid_ref[at, :] = hid
         return vec
 
+    def targ_tower(k):
+        close(k + 2, targ_raw, k * PIECE)
+        at = slice(k * PIECE, (k + 1) * PIECE)
+        targ_vec[at, :] = tower(targ_raw, at, wi_one, wi_two, t_pre, t_hid)
+
     for k in range(6):
         reduces[k].one()
     reduces[0].two()
     reduces[1].two()
     reduces[2].two()
-    query[0:256, :] = tower(tokens, slice(0, 256), w_one, w_two, q_pre, q_hid)
     reduces[0].three()
     reduces[1].three()
     reduces[3].two()
-    query[256:512, :] = tower(tokens, slice(256, 512), w_one, w_two, q_pre, q_hid)
+    reduces[4].two()
     close(0, cand_raw, 0)
     close(1, cand_raw, PIECE)
     cand_vec[y, x, c] = tower(cand_raw, slice(0, 512), wi_one, wi_two, c_pre, c_hid)
     ag.one()
+    reduces[5].two()
     reduces[2].three()
-    reduces[4].two()
-    query[512:768, :] = tower(tokens, slice(512, 768), w_one, w_two, q_pre, q_hid)
     ag.two()
     reduces[3].three()
-    reduces[5].two()
-    query[768:1024, :] = tower(tokens, slice(768, 1024), w_one, w_two, q_pre, q_hid)
-    close(2, targ_raw, 0)
-    targ_vec[0:256, :] = tower(targ_raw, slice(0, 256), wi_one, wi_two, t_pre, t_hid)
     reduces[4].three()
+    targ_tower(0)
+    reduces[5].three()
+    targ_tower(1)
     ag.three()
-    close(3, targ_raw, PIECE)
-    targ_vec[256:512, :] = tower(targ_raw, slice(256, 512), wi_one, wi_two, t_pre, t_hid)
-    reduces[5].three()
-    close(4, targ_raw, 2 * PIECE)
-    targ_vec[512:768, :] = tower(targ_raw, slice(512, 768), wi_one, wi_two, t_pre, t_hid)
-    close(5, targ_raw, 3 * PIECE)
-    targ_vec[768:1024, :] = tower(targ_raw, slice(768, 1024), wi_one, wi_two, t_pre, t_hid)
+    targ_tower(2)
+    targ_tower(3)
     ag.last()
     for red in reduces:
         red.drain()
     ag.drain()
 
 
-def fetch_rows(data_c, data_t, wi_one, wi_two, tokens, w_one, w_two):
+def fetch_rows(data_c, data_t, wi_one, wi_two):
     n_mine, width = data_c.shape[3:]
     n_tok = data_t.shape[3]
     ff = wi_one.shape[1]
@@ -519,13 +555,13 @@
     full = [jax.ShapeDtypeStruct((2, 2, 2, n_mine, width), jnp.bfloat16)]
     return pl.pallas_call(
         fetch_body,
-        out_shape=tuple(rows(n_mine) + outs(n_mine) + full + rows(n_tok) + outs(n_tok) + rows(n_tok) + outs(n_tok) + rows(n_tok)),
-        in_specs=[vmem] * 7,
-        out_specs=(vmem,) * 11,
+        out_shape=tuple(rows(n_mine) + outs(n_mine) + full + rows(n_tok) + outs(n_tok) + rows(n_tok)),
+        in_specs=[vmem] * 4,
+        out_specs=(vmem,) * 8,
         scratch_shapes=reduce_scratch(6, PIECE, width, jnp.bfloat16) + gather_sems(),
         compiler_params=pltpu.CompilerParams(vmem_limit_bytes=56 * 1024 * 1024, collective_id=1, has_side_effects=True),
         name="fetch_rows",
-    )(data_c, data_t, wi_one, wi_two, tokens, w_one, w_two)
+    )(data_c, data_t, wi_one, wi_two)
 
 
 def back_body(d_part, loss_in, d_query, d_targ, tokens, q_pre, q_hid, w_two, targ_raw, t_pre, t_hid, cand_raw, c_pre, c_hid, wi_one, wi_two, back_t, back_c, w_mine, loss_out, *scratch):
@@ -554,11 +590,13 @@
         for b in range(8):
             w_data[b // 4, (b // 2) % 2, b % 2, first : first + n, :] = value[b * n : (b + 1) * n, :]
 
-    t_q, dwi_one, dwi_two = tower_back(targ_raw[...], wi_two[...], t_pre[...], t_hid[...], d_targ[...])
-    back_t[y, x, c] = by_transpose(t_q, wi_one[...]).astype(jnp.bfloat16)
+    dwi_two = over_rows(t_hid[...], d_targ[...])
     red_u[0].two()
     red_u[1].two()
+    t_q = grad_through(d_targ[...], wi_two[...], t_pre[...])
+    back_t[y, x, c] = by_transpose(t_q, wi_one[...]).astype(jnp.bfloat16)
     ag_t.one()
+    dwi_one = over_rows(targ_raw[...], t_q)
     _, dw_one, dw_two = tower_back(tokens[...], w_two[...], q_pre[...], q_hid[...], d_query[...])
     put(0, dw_one[:, :width])
     put(128, dw_one[:, width:])
@@ -629,15 +667,17 @@
         rows_loc, width = table_loc.shape
         n_cand = cand_ids.shape[0]
         tok_total = tokens.shape[0] * num_dev
-        targ_all = share_ids(targ_loc).reshape(-1)
+        targ_all, lq_b, cid_b, q_pre, q_hid, query = prepare(targ_loc, log_q, cand_ids, tokens, w_one, w_two)
+        targ_all = targ_all.reshape(-1)
         local_ids = jnp.concatenate([cand_ids, targ_all]) - my_index * rows_loc
-        ids_two = 2 * jnp.where((local_ids >= 0) & (local_ids < rows_loc), local_ids, rows_loc)
+        spare = rows_loc + jnp.arange(local_ids.shape[0], dtype=jnp.int32) % SPARE
+        ids_two = 2 * jnp.where((local_ids >= 0) & (local_ids < rows_loc), local_ids, spare)
         data_c, data_t = pick_rows(ids_two, table_loc, n_cand)
         data_c = data_c.reshape(2, 2, 2, n_cand // 8, width)
         data_t = data_t.reshape(2, 2, 2, tokens.shape[0], width)
-        cand_mine, c_pre, c_hid, cand_vec, targ_raw, t_pre, t_hid, targ_vec, q_pre, q_hid, query = fetch_rows(data_c, data_t, wi_one, wi_two, tokens, w_one, w_two)
+        cand_mine, c_pre, c_hid, cand_vec, targ_raw, t_pre, t_hid, targ_vec = fetch_rows(data_c, data_t, wi_one, wi_two)
         cand_vec = cand_vec.reshape(n_cand, width)
-        loss_part, d_query, d_targ_vec, d_part = softmax_grads(query, targ_vec, cand_vec, log_q, targ_loc, cand_ids, tok_total)
+        loss_part, d_query, d_targ_vec, d_part = softmax_grads(query, targ_vec, cand_vec, lq_b, cid_b, targ_loc, tok_total)
         back_t, back_c, w_mine, loss = back_rows(d_part.reshape(2, 2, 2, n_cand // 8, width), loss_part, d_query, d_targ_vec, tokens, q_pre, q_hid, w_two, targ_raw, t_pre, t_hid, cand_mine, c_pre, c_hid, wi_one, wi_two)
         w_all = lax.all_gather(w_mine, "dp", axis=0)
         d_table = scatter_rows(ids_two, back_c.reshape(-1, width), back_t.reshape(-1, width), rows_loc)

time: 272 us -> 279 us (1.026)
  local copies, waits for them, and re-layouts: 18.8 us -> 23.2 us
  Pallas kernels: 233 us -> 237 us
    unnamed x22 -> x36, local copies, waits for them, and re-layouts: 3.52 us -> 17 us
    pallas_call x1, Pallas kernels: 28 us -> 35.6 us  [softmax_grads(): pl.pallas_call(functools.partial(softmax_body, tok_total), grid=(steps,),...]
    broadcast_in_dim x2 -> x0, local copies, waits for them, and re-layouts: 4.92 us -> none  [the longest x1 3.01 us: softmax_grads(): cid_b = jnp.broadcast_to(cand_ids[:, None], (n_cand, 128))]
    pallas_call x1, Pallas kernels: 50 us -> 45.9 us  [fetch_rows(): pl.pallas_call(fetch_body, out_shape=tuple(rows(n_mine) + outs(n_mine) +...]
    reshape x1 -> x0, local copies, waits for them, and re-layouts: 4.07 us -> none  [local_step(): cand_vec = cand_vec.reshape(n_cand, width)]
where the time goes in v3:
time: 279 us; the launch traced here: 278 us
  Pallas kernels  237 us (85%)
  local copies, waits for them, and re-layouts  23.2 us (8%)
  between operations  16 us (6%)
    pallas_call x1, Pallas kernels, back_rows(): pl.pallas_call(back_body, out_shape=(jax.ShapeDtypeStruct((2, 2, 2, n_tok...  75.4 us
    pallas_call x1, Pallas kernels, scatter_rows(): pl.pallas_call(scatter_body, out_shape=jax.ShapeDtypeStruct((rows_loc, wi...  49 us
    pallas_call x1, Pallas kernels, fetch_rows(): pl.pallas_call(fetch_body, out_shape=tuple(rows(n_mine) + outs(n_mine) +...  45.9 us
    pallas_call x1, Pallas kernels, softmax_grads(): pl.pallas_call(functools.partial(softmax_body, tok_total), grid=(steps,),...  35.6 us
    pallas_call x1, Pallas kernels, pick_rows(): pl.pallas_call(pick_body, out_shape=(jax.ShapeDtypeStruct((n_cand, width)...  22.7 us
    unnamed x36, local copies, waits for them, and re-layouts  17 us
    pallas_call x1, Pallas kernels, prepare(): pl.pallas_call(prepare_body, out_shape=(jax.ShapeDtypeStruct((8, 8, 128),...  8.07 us
  transfers between devices with their start and end apart: 1, of which 0 were waited for; matrix products, arithmetic and copies ran while one was open for 0% of the time, Pallas kernels for 18%

profile of v3, /device:TPU:0, one launch (start us, length us, event | category | flops | bytes accessed | tf_op | source)
XLA Modules:
  0.0 278.5 jit_solution(17327295994331373807)
XLA Ops:
  7.2 0.0 all-gather.3.cloned.1.call-start
  7.2 0.0 copy-start
  7.2 1.6 copy-done
  8.8 0.0 copy-start.3
  8.8 0.9 copy-done.3
  9.8 0.0 copy-start.5
  9.8 1.2 copy-done.5
  11.0 0.0 copy-start.8
  11.0 0.7 copy-done.8
  11.7 0.0 copy-start.10
  11.7 0.7 copy-done.10
  12.4 0.0 copy-start.11
  12.4 0.7 copy-done.11
  13.1 8.1 %prepare.1 = (s32[8,8,128]{2,1,0:T(8,128)S(1)}, f32[4096,128]{1,0:T(8,128)S(1)}, s32[4096,128]{1,0:T(8,128)S(1)}, f32[1024,512]{1,0:T(8,128)S(1)}, bf16[1024,512...) custom-call(s32[8,128]{1,0:T(8,128)S(1)} %bitcast.34, f32[32,128]{1,0:T(8,128)S(1)} %bitcast.33, s32[32,128]{1,0:T(8,128)S(1)} %bitcast.30, ...), custom_call_target="tpu_custom_call" | custom-call | tf_op jit(solution)/shard_map/prepare/pallas_call | solution.py:465
  21.2 0.0 copy-start.1
  21.2 1.3 copy-done.1
  22.5 0.0 copy-start.4
  22.5 1.0 copy-done.4
  23.5 0.0 copy-start.14
  23.5 1.3 copy-done.14
  24.9 0.0 copy-start.15
  24.9 1.3 copy-done.15
  26.2 22.7 %pick_rows.1 = (bf16[4096,256]{1,0:T(8,128)(2,1)S(1)}, bf16[8192,256]{1,0:T(8,128)(2,1)}) custom-call(s32[12288]{0:T(1024)S(1)} %fusion.2.ids_s, bf16[32768,256]{1,0:T(8,128)(2,1)} %table.1), custom_call_target="tpu_custom_call" | custom-call | tf_op jit(solution)/shard_map/pick_rows/pallas_call | solution.py:96
  48.8 0.0 copy-start.2
  48.9 1.3 copy-done.2
  50.2 0.0 copy-start.12
  50.2 45.9 %fetch_rows.1 = (bf16[512,256]{1,0:T(8,128)(2,1)}, f32[512,512]{1,0:T(8,128)}, bf16[512,512]{1,0:T(8,128)(2,1)}, bf16[2,2,2,512,256]{4,3,2,1,0:T(8,128)(2,1)}, b...) custom-call(bf16[2,2,2,512,256]{4,3,2,1,0:T(8,128)(2,1)} %bitcast.29, ...), custom_call_target="tpu_custom_call" | custom-call | tf_op jit(solution)/shard_map/fetch_rows/pallas_call | solution.py:556
  96.1 0.0 copy-done.12
  96.1 0.0 copy-start.16
  96.1 1.6 copy-done.16
  97.7 0.0 copy-start.17
  97.7 1.0 copy-done.17
  98.7 35.6 %softmax_grads.1 = (f32[8,128]{1,0:T(8,128)S(1)}, bf16[1024,256]{1,0:T(8,128)(2,1)S(1)}, bf16[1024,256]{1,0:T(8,128)(2,1)S(1)}, f32[4096,256]{1,0:T(8,128)}) custom-call(bf16[1024,256]{1,0:T(8,128)(2,1)S(1)} %get-tuple-element.30.h_ref, bf16[1024,256]{1,0:T(8,128)(2,1)S(1)} %copy-done.17, bf16[4096,256]{1,0:T(8,128)(2,1)S(1)} %bitcast.36, ...), custom_call_target="tpu_custom_call" | custom-call | flops 6442450944 | bytes 16777216 | tf_op jit(solution)/shard_map/softmax_grads/pallas_call | solution.py:270
  134.3 0.0 copy-start.6
  134.3 0.8 copy-done.6
  135.1 0.0 copy-start.7
  135.1 0.8 copy-done.7
  135.9 0.0 copy-start.13
  135.9 0.6 copy-done.13
  136.5 0.0 copy-start.9
  136.5 75.4 %back_rows.1 = (bf16[2,2,2,1024,256]{4,3,2,1,0:T(8,128)(2,1)}, bf16[2,2,2,512,256]{4,3,2,1,0:T(8,128)(2,1)}, f32[448,256]{1,0:T(8,128)}, f32[8,128]{1,0:T(8,128)}) custom-call(f32[2,2,2,512,256]{4,3,2,1,0:T(8,128)} %bitcast.37, f32[8,128]{1,0:T(8,128)} %copy-done.13, bf16[1024,256]{1,0:T(8,128)(2,1)} %copy-done.6, bf16[1024,256]{1,0:T(8,128)(2,1)} %copy-done.7, ...), custom_call_target="tpu_custom_call" | custom-call | tf_op jit(solution)/shard_map/back_rows/pallas_call | solution.py:646
  211.9 0.0 all-gather.3.cloned.1.call-update
  211.9 1.2 slice.21
  213.8 0.0 copy-done.9
  213.8 49.0 %scatter_rows.1 = f32[32768,256]{1,0:T(8,128)} custom-call(s32[12288]{0:T(1024)S(1)} %fusion.2.ids_s, s32[96,128]{1,0:T(8,128)S(1)} %fusion.6.ids_v, bf16[4096,256]{1,0:T(8,128)(2,1)} %bitcast.49, bf16[8192,256]{1,0:T(8,128)(2,1)} %bitcast.48), custom_call_target="tpu_custom_call" | custom-call | flops 60000002048 | bytes 41943040 | tf_op jit(solution)/shard_map/scatter_rows/pallas_call | solution.py:176
  262.9 0.0 all-gather.3.cloned.1.call-done
  262.9 1.7 fusion.13
  264.6 2.3 fusion.11
  266.9 1.1 fusion.12
  268.0 1.6 pad_maximum_fusion
  269.6 0.9 pad_maximum_fusion.1
  (2 shorter events, 0.1 us)
Async XLA Ops:
  7.2 255.7 %all-gather.3.cloned.1.call-start = ((), (), s32[]{:S(2)}) async-start(), calls=%async_computation | async-start | bytes 4128768 | tf_op jit(solution)/shard_map/all_gather | solution.py:682
  7.2 1.6 copy-start
  8.8 0.9 copy-start.3
  9.8 1.2 copy-start.5
  11.0 0.7 copy-start.8
  11.7 0.7 copy-start.10
  12.4 0.7 copy-start.11
  21.2 1.4 copy-start.1
  22.5 1.0 copy-start.4
  23.5 1.3 copy-start.14
  24.9 1.3 copy-start.15
  48.8 1.3 copy-start.2
  50.2 45.9 %copy-start.12 = (s32[1024]{0:T(1024)S(1)}, s32[1024]{0:T(1024)}, u32[]{:S(2)}) copy-start(s32[1024]{0:T(1024)} %param.17) | copy-start | bytes 12292
  96.1 1.6 copy-start.16
  97.7 1.0 copy-start.17
  134.3 0.8 copy-start.6
  135.1 0.8 copy-start.7
  135.9 0.6 copy-start.13
  136.5 77.3 %copy-start.9 = (s32[4096]{0:T(1024)S(1)}, s32[4096]{0:T(1024)}, u32[]{:S(2)}) copy-start(s32[4096]{0:T(1024)} %param.15) | copy-start | bytes 49156
Sparse Core Ops, SparseCore 0:
  212.1 28.5 all-gather.2

commit v4 on v3

--- a/solution.py
+++ b/solution.py
@@ -39,7 +39,7 @@
     return grad_pre, dw_in, dw_out
 
 
-GROUP = 16
+VMEM_LIMIT = 63 * 1024 * 1024
 BATCH = 128
 SPARE = 256
 STAGE_ROWS = 2048
@@ -104,12 +104,12 @@
             pltpu.VMEM((2 * BATCH, width // 2), jnp.float32),
             pltpu.SemaphoreType.DMA((4,)),
         ],
-        compiler_params=pltpu.CompilerParams(vmem_limit_bytes=50 * 1024 * 1024),
+        compiler_params=pltpu.CompilerParams(vmem_limit_bytes=VMEM_LIMIT),
         name="pick_rows",
     )(ids_two, table_loc)
 
 
-def scatter_body(ids_s, ids_v, cand_ref, targ_ref, out_ref, acc, g2, out_stage, sem):
+def scatter_body(ids_s, ids_v, cand_ref, targ_ref, out_ref, acc, g2, new, out_stage, sem):
     rows, width = out_ref.shape
     lane = width // 2
     n_cand = cand_ref.shape[0]
@@ -119,21 +119,18 @@
     def _(i):
         acc[pl.ds(pl.multiple_of(i * 512, 512), 512), :] = jnp.zeros((512, lane), jnp.float32)
 
-    row_i = lax.broadcasted_iota(jnp.int32, (BATCH, BATCH), 0) // GROUP
-    col_i = lax.broadcasted_iota(jnp.int32, (BATCH, BATCH), 1) // GROUP
-    same_group = row_i == col_i
-
     def one_batch(b, src, src_base):
         idr = jnp.broadcast_to(ids_v[pl.ds(b, 1), :], (BATCH, BATCH))
-        same = jnp.where((idr == idr.T) & same_group, 1.0, 0.0).astype(jnp.bfloat16)
+        same = jnp.where(idr == idr.T, 1.0, 0.0).astype(jnp.bfloat16)
         part = jnp.dot(same, src[pl.ds(pl.multiple_of(b * BATCH - src_base, BATCH), BATCH), :], preferred_element_type=jnp.float32)
         g2[pl.ds(0, BATCH, 2), :] = part[:, :lane]
         g2[pl.ds(1, BATCH, 2), :] = part[:, lane:]
-        for g in range(BATCH // GROUP):
-            idx = [pl.multiple_of(ids_s[b * BATCH + g * GROUP + r], 2) for r in range(GROUP)]
-            new = [acc[pl.ds(idx[r], 2), :] + g2[pl.ds(2 * (g * GROUP + r), 2), :] for r in range(GROUP)]
-            for r in range(GROUP):
-                acc[pl.ds(idx[r], 2), :] = new[r]
+        for r in range(BATCH):
+            at = pl.multiple_of(ids_s[b * BATCH + r], 2)
+            new[pl.ds(2 * r, 2), :] = acc[pl.ds(at, 2), :] + g2[pl.ds(2 * r, 2), :]
+        for r in range(BATCH):
+            at = pl.multiple_of(ids_s[b * BATCH + r], 2)
+            acc[pl.ds(at, 2), :] = new[pl.ds(2 * r, 2), :]
 
     @pl.loop(0, n_cand // BATCH)
     def _(b):
@@ -181,115 +178,152 @@
         scratch_shapes=[
             pltpu.VMEM((2 * (rows_loc + SPARE), width // 2), jnp.float32),
             pltpu.VMEM((2 * BATCH, width // 2), jnp.float32),
+            pltpu.VMEM((2 * BATCH, width // 2), jnp.float32),
             pltpu.VMEM((4, OUT_ROWS, width), jnp.float32),
             pltpu.SemaphoreType.DMA((4,)),
         ],
-        compiler_params=pltpu.CompilerParams(vmem_limit_bytes=52 * 1024 * 1024),
+        compiler_params=pltpu.CompilerParams(vmem_limit_bytes=VMEM_LIMIT),
         cost_estimate=pl.CostEstimate(flops=60_000_000_000, bytes_accessed=40 << 20, transcendentals=0),
         name="scatter_rows",
     )(ids_two, ids_two.reshape(n_all // BATCH, BATCH), back_cand, back_targ)
 
 
-TOK_BLK = 256
-CHUNK = 256
+CHUNK = 512
 SUB = 64
-BACK_CHUNK = 512
-
-
-def softmax_body(tok_total, h_ref, v_ref, u_ref, lq_ref, cid_ref, tid_ref, loss_ref, dh_ref, dv_ref, du_ref, e_s, m_s, ut_s):
-    step = pl.program_id(0)
+COLS = 256
+
+
+def logits_pass(u_ref, h, lq_ref, cid_ref, tid, z_a, z_b, e_s, m_s, s_s):
     n_cand, width = u_ref.shape
+    n_tok = h.shape[0]
     scale = SCORE_GAIN / math.sqrt(width)
-
-    @pl.when(step == 0)
-    def _():
-        loss_ref[...] = jnp.zeros_like(loss_ref)
-        du_ref[...] = jnp.zeros_like(du_ref)
-        for i in range(n_cand // 512):
-            ut_s[:, i * 512 : (i + 1) * 512] = u_ref[i * 512 : (i + 1) * 512, :].T
-
-    h = h_ref[...]
+    ht = h.T
+    n_chunk = n_cand // CHUNK
+
+    def multiply(i, z_ref):
+        off = pl.multiple_of(jnp.minimum(i, n_chunk - 1) * CHUNK, CHUNK)
+        z_ref[...] = jnp.dot(u_ref[pl.ds(off, CHUNK), :], ht, preferred_element_type=jnp.float32)
+
+    def absorb(i, z_ref, first):
+        off = pl.multiple_of(i * CHUNK, CHUNK)
+        for col in range(0, n_tok, COLS):
+            cols = slice(col, col + COLS)
+            m8 = m_s[0, :, cols]
+            s8 = s_s[:, cols]
+            for k in range(CHUNK // SUB):
+                rows = pl.ds(pl.multiple_of(off + k * SUB, SUB), SUB)
+                lq = jnp.concatenate([lq_ref[rows, :]] * (COLS // 128), axis=1)
+                cid = jnp.concatenate([cid_ref[rows, :]] * (COLS // 128), axis=1)
+                z = z_ref[k * SUB : (k + 1) * SUB, cols] * scale - lq
+                z = jnp.where(cid == tid[:, cols], HIT_VALUE, z).reshape(SUB // 8, 8, COLS)
+                m_new = jnp.maximum(m8, jnp.max(z, axis=0))
+                e = jnp.exp(z - m_new[None])
+                s8 = s8 * jnp.exp(m8 - m_new) + jnp.sum(e, axis=0)
+                m8 = m_new
+                e_s[rows, cols] = e.reshape(SUB, COLS)
+                m_s[1 + i * (CHUNK // SUB) + k, :, cols] = m8
+            m_s[0, :, cols] = m8
+            s_s[:, cols] = s8
+
+    m_s[0] = jnp.full((8, n_tok), jnp.finfo(jnp.float32).min, jnp.float32)
+    s_s[...] = jnp.zeros_like(s_s)
+    multiply(0, z_a)
+
+    @pl.loop(0, n_chunk // 2)
+    def _(i):
+        multiply(2 * i + 1, z_b)
+        absorb(2 * i, z_a, 0)
+        multiply(2 * i + 2, z_a)
+        absorb(2 * i + 1, z_b, 0)
+
+
+def loss_pass(tok_total, u_ref, ut_s, h, v, e_s, m_s, s_s, fac_s, dz_a, dz_b, dht_s, loss_ref, dh_ref, dv_ref, du_ref):
+    n_cand, width = u_ref.shape
+    n_tok = h.shape[0]
+    scale = SCORE_GAIN / math.sqrt(width)
+    n_chunk = n_cand // CHUNK
     hf = h.astype(jnp.float32)
-    vf = v_ref[...].astype(jnp.float32)
-    ht = h.T
+    vf = v.astype(jnp.float32)
     zt = jnp.sum(hf * vf, axis=1, keepdims=True) * scale
-    zt = jnp.broadcast_to(zt, (TOK_BLK, 128)).T[0:1, :]
-    tid = tid_ref[0]
-    lanes = TOK_BLK // 128
-
-    def forward(i, carry):
-        m8, s8 = carry
-        off = pl.multiple_of(i * CHUNK, CHUNK)
-        z_all = jnp.dot(u_ref[pl.ds(off, CHUNK), :], ht, preferred_element_type=jnp.float32)
-        for k in range(CHUNK // SUB):
-            rows = pl.ds(pl.multiple_of(off + k * SUB, SUB), SUB)
-            lq = jnp.concatenate([lq_ref[rows, :]] * lanes, axis=1)
-            cid = jnp.concatenate([cid_ref[rows, :]] * lanes, axis=1)
-            z = z_all[k * SUB : (k + 1) * SUB] * scale - lq
-            z = jnp.where(cid == tid, HIT_VALUE, z).reshape(SUB // 8, 8, TOK_BLK)
-            m_new = jnp.maximum(m8, jnp.max(z, axis=0))
-            e = jnp.exp(z - m_new[None])
-            s8 = s8 * jnp.exp(m8 - m_new) + jnp.sum(e, axis=0)
-            m8 = m_new
-            e_s[rows, :] = e.reshape(SUB, TOK_BLK)
-            m_s[pl.ds(pl.multiple_of(i * (8 * CHUNK // SUB) + 8 * k, 8), 8), :] = m8
-        return m8, s8
-
-    m8, s8 = lax.fori_loop(0, n_cand // CHUNK, forward, (jnp.broadcast_to(zt, (8, TOK_BLK)), jnp.zeros((8, TOK_BLK), jnp.float32)))
-    m = jnp.max(m8, axis=0, keepdims=True)
+    zt = jnp.broadcast_to(zt, (n_tok, 128)).T[0:1, :]
+    m8 = m_s[0]
+    m = jnp.maximum(zt, jnp.max(m8, axis=0, keepdims=True))
     et = jnp.exp(zt - m)
-    den = et + jnp.sum(s8 * jnp.exp(m8 - m), axis=0, keepdims=True)
+    den = et + jnp.sum(s_s[...] * jnp.exp(m8 - m), axis=0, keepdims=True)
     part = jnp.sum(jnp.log(den) + m - zt, axis=1, keepdims=True)
+    loss_ref[...] = jnp.broadcast_to(part, loss_ref.shape)
     dzt = ((et / den - 1.0) / tok_total).astype(jnp.bfloat16).astype(jnp.float32)
     inv = 1.0 / den / tok_total
-    loss_ref[...] += jnp.broadcast_to(part, loss_ref.shape)
-
-    def backward(i, dht):
-        off = pl.multiple_of(i * BACK_CHUNK, BACK_CHUNK)
-        pieces = []
-        for k in range(BACK_CHUNK // SUB):
-            rows = pl.ds(pl.multiple_of(off + k * SUB, SUB), SUB)
-            m_k = m_s[pl.ds(pl.multiple_of(i * (8 * BACK_CHUNK // SUB) + 8 * k, 8), 8), :]
-            fac = jnp.exp(m_k - m) * inv
-            pieces.append((e_s[rows, :].reshape(SUB // 8, 8, TOK_BLK) * fac[None]).reshape(SUB, TOK_BLK).astype(jnp.bfloat16))
-        dz = jnp.concatenate(pieces, axis=0)
-        du_ref[pl.ds(off, BACK_CHUNK), :] += jnp.dot(dz, h, preferred_element_type=jnp.float32)
-        return dht + jnp.dot(ut_s[:, pl.ds(off, BACK_CHUNK)], dz, preferred_element_type=jnp.float32)
-
-    dht = lax.fori_loop(0, n_cand // BACK_CHUNK, backward, jnp.zeros((width, TOK_BLK), jnp.float32))
-    dzt_c = jnp.broadcast_to(dzt, (128, TOK_BLK)).T[:, 0:1]
-    dh_ref[...] = ((dzt_c * vf + dht.T) * scale).astype(jnp.bfloat16)
+    fac_s[0:8, :] = jnp.broadcast_to(m, (8, n_tok))
+    fac_s[8:16, :] = jnp.broadcast_to(inv, (8, n_tok))
+    for i in range(n_cand // 512):
+        ut_s[:, i * 512 : (i + 1) * 512] = u_ref[i * 512 : (i + 1) * 512, :].T
+
+    def gradient(i, dz_ref):
+        i = jnp.minimum(i, n_chunk - 1)
+        off = pl.multiple_of(i * CHUNK, CHUNK)
+        for col in range(0, n_tok, COLS):
+            cols = slice(col, col + COLS)
+            for k in range(CHUNK // SUB):
+                rows = pl.ds(pl.multiple_of(off + k * SUB, SUB), SUB)
+                fac = jnp.exp(m_s[1 + i * (CHUNK // SUB) + k, :, cols] - fac_s[0:8, cols]) * fac_s[8:16, cols]
+                dz_ref[k * SUB : (k + 1) * SUB, cols] = (e_s[rows, cols].reshape(SUB // 8, 8, COLS) * fac[None]).reshape(SUB, COLS).astype(jnp.bfloat16)
+
+    def spread(i, dz_ref):
+        off = pl.multiple_of(i * CHUNK, CHUNK)
+        du_ref[pl.ds(off, CHUNK), :] = jnp.dot(dz_ref[...], h, preferred_element_type=jnp.float32)
+        dht_s[...] += jnp.dot(ut_s[:, pl.ds(off, CHUNK)], dz_ref[...], preferred_element_type=jnp.float32)
+
+    dht_s[...] = jnp.zeros_like(dht_s)
+    gradient(0, dz_a)
+
+    @pl.loop(0, n_chunk // 2)
+    def _(i):
+        gradient(2 * i + 1, dz_b)
+        spread(2 * i, dz_a)
+        gradient(2 * i + 2, dz_a)
+        spread(2 * i + 1, dz_b)
+
+    dzt_c = jnp.broadcast_to(dzt, (128, n_tok)).T[:, 0:1]
+    dh_ref[...] = ((dzt_c * vf + dht_s[...].T) * scale).astype(jnp.bfloat16)
     dv_ref[...] = (scale * dzt_c * hf).astype(jnp.bfloat16)
+
+
+def softmax_scratch(n_cand, n_tok, width):
+    return [
+        pltpu.VMEM((CHUNK, n_tok), jnp.float32),
+        pltpu.VMEM((CHUNK, n_tok), jnp.float32),
+        pltpu.VMEM((n_cand, n_tok), jnp.float32),
+        pltpu.VMEM((1 + n_cand // SUB, 8, n_tok), jnp.float32),
+        pltpu.VMEM((8, n_tok), jnp.float32),
+        pltpu.VMEM((width, n_cand), jnp.bfloat16),
+        pltpu.VMEM((16, n_tok), jnp.float32),
+        pltpu.VMEM((CHUNK, n_tok), jnp.bfloat16),
+        pltpu.VMEM((CHUNK, n_tok), jnp.bfloat16),
+        pltpu.VMEM((width, n_tok), jnp.float32),
+    ]
+
+
+def softmax_body(tok_total, h_ref, v_ref, u_ref, lq_ref, cid_ref, tid_ref, loss_ref, dh_ref, dv_ref, du_ref, z_a, z_b, e_s, m_s, s_s, ut_s, fac_s, dz_a, dz_b, dht_s):
+    h = h_ref[...]
+    logits_pass(u_ref, h, lq_ref, cid_ref, tid_ref[...], z_a, z_b, e_s, m_s, s_s)
+    loss_pass(tok_total, u_ref, ut_s, h, v_ref[...], e_s, m_s, s_s, fac_s, dz_a, dz_b, dht_s, loss_ref, dh_ref, dv_ref, du_ref)
 
 
 def softmax_grads(query, targ_vec, cand_vec, lq_b, cid_b, targ_ids, tok_total):
     n_tok, width = query.shape
     n_cand = cand_vec.shape[0]
-    steps = n_tok // TOK_BLK
-    whole = lambda s: (0, 0)
+    vmem = pl.BlockSpec(memory_space=pltpu.VMEM)
     return pl.pallas_call(
         functools.partial(softmax_body, tok_total),
-        grid=(steps,),
         out_shape=(jax.ShapeDtypeStruct((8, 128), jnp.float32), jax.ShapeDtypeStruct((n_tok, width), jnp.bfloat16), jax.ShapeDtypeStruct((n_tok, width), jnp.bfloat16), jax.ShapeDtypeStruct((n_cand, width), jnp.float32)),
-        in_specs=[
-            pl.BlockSpec((TOK_BLK, width), lambda s: (s, 0)),
-            pl.BlockSpec((TOK_BLK, width), lambda s: (s, 0)),
-            pl.BlockSpec((n_cand, width), whole),
-            pl.BlockSpec((n_cand, 128), whole),
-            pl.BlockSpec((n_cand, 128), whole),
-            pl.BlockSpec((1, 1, TOK_BLK), lambda s: (s, 0, 0)),
-        ],
-        out_specs=(
-            pl.BlockSpec((8, 128), whole),
-            pl.BlockSpec((TOK_BLK, width), lambda s: (s, 0)),
-            pl.BlockSpec((TOK_BLK, width), lambda s: (s, 0)),
-            pl.BlockSpec((n_cand, width), whole),
-        ),
-        scratch_shapes=[pltpu.VMEM((n_cand, TOK_BLK), jnp.float32), pltpu.VMEM((8 * n_cand // SUB, TOK_BLK), jnp.float32), pltpu.VMEM((width, n_cand), jnp.bfloat16)],
-        compiler_params=pltpu.CompilerParams(vmem_limit_bytes=48 * 1024 * 1024, dimension_semantics=("arbitrary",)),
+        in_specs=[vmem] * 6,
+        out_specs=(vmem,) * 4,
+        scratch_shapes=softmax_scratch(n_cand, n_tok, width),
+        compiler_params=pltpu.CompilerParams(vmem_limit_bytes=VMEM_LIMIT),
         cost_estimate=pl.CostEstimate(flops=6 * n_tok * n_cand * width, bytes_accessed=16 << 20, transcendentals=n_tok * n_cand),
         name="softmax_grads",
-    )(query, targ_vec, cand_vec, lq_b, cid_b, targ_ids.reshape(steps, 1, TOK_BLK))
+    )(query, targ_vec, cand_vec, lq_b, cid_b, targ_ids.reshape(1, n_tok))
 
 
 MESH = pl.DeviceIdType.MESH
@@ -475,7 +509,7 @@
         in_specs=[vmem] * 6,
         out_specs=(vmem,) * 6,
         scratch_shapes=[pltpu.SemaphoreType.DMA((8,)), pltpu.SemaphoreType.DMA((8,))],
-        compiler_params=pltpu.CompilerParams(vmem_limit_bytes=40 * 1024 * 1024, collective_id=0, has_side_effects=True),
+        compiler_params=pltpu.CompilerParams(vmem_limit_bytes=VMEM_LIMIT, collective_id=0, has_side_effects=True),
         name="prepare",
     )(targ_loc.reshape(8, 128), log_q.reshape(-1, 128), cand_ids.reshape(-1, 128), tokens, w_one, w_two)
 
@@ -559,16 +593,16 @@
         in_specs=[vmem] * 4,
         out_specs=(vmem,) * 8,
         scratch_shapes=reduce_scratch(6, PIECE, width, jnp.bfloat16) + gather_sems(),
-        compiler_params=pltpu.CompilerParams(vmem_limit_bytes=56 * 1024 * 1024, collective_id=1, has_side_effects=True),
+        compiler_params=pltpu.CompilerParams(vmem_limit_bytes=VMEM_LIMIT, collective_id=1, has_side_effects=True),
         name="fetch_rows",
     )(data_c, data_t, wi_one, wi_two)
 
 
-def back_body(d_part, loss_in, d_query, d_targ, tokens, q_pre, q_hid, w_two, targ_raw, t_pre, t_hid, cand_raw, c_pre, c_hid, wi_one, wi_two, back_t, back_c, w_mine, loss_out, *scratch):
+def back_body(d_part, loss_in, d_query, d_targ, tokens, q_pre, q_hid, w_two, targ_raw, t_pre, t_hid, cand_raw, c_pre, c_hid, wi_one, wi_two, back_t, back_c, dw_one_out, dw_two_out, dwi_one_out, dwi_two_out, loss_out, *scratch):
     place = my_place()
     me, y, x, c = place
     rs_u, rs_w = scratch[0:10], scratch[10:20]
-    at_send, at_recv, ac_send, ac_recv, l_send, l_recv, w_data, l_all = scratch[20:28]
+    at_send, at_recv, ac_send, ac_recv, aw_send, aw_recv, l_send, l_recv, w_data, w_full, l_all = scratch[20:31]
     width = d_query.shape[1]
     scale = SCORE_GAIN / math.sqrt(width)
     meet(place)
@@ -578,6 +612,7 @@
     red_w = Reduce(place, w_data, *[s.at[0] for s in rs_w])
     ag_t = Gather(place, back_t, at_send, at_recv)
     ag_c = Gather(place, back_c, ac_send, ac_recv)
+    ag_w = Gather(place, w_full, aw_send, aw_recv)
     red_u[0].one()
     red_u[1].one()
     l_all[me] = loss_in[...]
@@ -598,9 +633,8 @@
     ag_t.one()
     dwi_one = over_rows(targ_raw[...], t_q)
     _, dw_one, dw_two = tower_back(tokens[...], w_two[...], q_pre[...], q_hid[...], d_query[...])
-    put(0, dw_one[:, :width])
-    put(128, dw_one[:, width:])
-    put(256, dw_two)
+    dw_one_out[...] = dw_one
+    dw_two_out[...] = dw_two
     red_u[0].three()
     red_u[1].three()
     ag_t.two()
@@ -613,29 +647,38 @@
     back_c[y, x, c] = by_transpose(c_q, wi_one[...]).astype(jnp.bfloat16)
     ag_c.one()
     dwi_one = dwi_one + dwi_one_c
-    put(320, dwi_one[:, :width])
-    put(352, dwi_one[:, width:])
-    put(384, dwi_two + dwi_two_c)
+    put(0, dwi_one[:, :width])
+    put(32, dwi_one[:, width:])
+    put(64, dwi_two + dwi_two_c)
     red_w.one()
     for copy in l_copies:
         copy.wait()
     loss_out[...] = jnp.sum(l_all[...], axis=0)
+    red_w.two()
+    red_w.three()
     ag_c.two()
-    red_w.two()
-    ag_t.three()
-    red_w.three()
-    ag_c.three()
     first, second = red_w.last()
     half = first.shape[0]
-    w_mine[0:half, :] = first
-    w_mine[half : 2 * half, :] = second
+    w_full[y, x, c, 0:half, :] = first
+    w_full[y, x, c, half : 2 * half, :] = second
+    ag_w.one()
+    ag_t.three()
+    ag_w.two()
+    ag_c.three()
+    ag_w.three()
     ag_t.last()
     ag_c.last()
-    for part in red_u + [red_w, ag_t, ag_c]:
+    ag_w.last()
+    for b in range(8):
+        block = w_full.at[b // 4, (b // 2) % 2, b % 2]
+        dwi_one_out[b * 32 : (b + 1) * 32, :width] = block[0:32, :]
+        dwi_one_out[b * 32 : (b + 1) * 32, width:] = block[32:64, :]
+        dwi_two_out[b * 64 : (b + 1) * 64, :] = block[64:128, :]
+    for part in red_u + [red_w, ag_t, ag_c, ag_w]:
         part.drain()
 
 
-W_ROWS = 448
+W_ROWS = 128
 
 
 def back_rows(d_part, loss_part, *rest):
@@ -648,13 +691,16 @@
         out_shape=(
             jax.ShapeDtypeStruct((2, 2, 2, n_tok, width), jnp.bfloat16),
             jax.ShapeDtypeStruct((2, 2, 2, n_mine, width), jnp.bfloat16),
-            jax.ShapeDtypeStruct((W_ROWS, width), jnp.float32),
+            jax.ShapeDtypeStruct((rest[2].shape[1], rest[3].shape[1]), jnp.float32),
+            jax.ShapeDtypeStruct(rest[5].shape, jnp.float32),
+            jax.ShapeDtypeStruct(rest[12].shape, jnp.float32),
+            jax.ShapeDtypeStruct(rest[13].shape, jnp.float32),
             jax.ShapeDtypeStruct((8, 128), jnp.float32),
         ),
         in_specs=[vmem] * 16,
-        out_specs=(vmem,) * 4,
-        scratch_shapes=reduce_scratch(2, PIECE, width, jnp.float32) + reduce_scratch(1, W_ROWS, width, jnp.float32) + gather_sems() + gather_sems() + sems + [pltpu.VMEM((2, 2, 2, W_ROWS, width), jnp.float32), pltpu.VMEM((8, 8, 128), jnp.float32)],
-        compiler_params=pltpu.CompilerParams(vmem_limit_bytes=60 * 1024 * 1024, collective_id=2, has_side_effects=True),
+        out_specs=(vmem,) * 7,
+        scratch_shapes=reduce_scratch(2, PIECE, width, jnp.float32) + reduce_scratch(1, W_ROWS, width, jnp.float32) + gather_sems() + gather_sems() + gather_sems() + sems + [pltpu.VMEM((2, 2, 2, W_ROWS, width), jnp.float32), pltpu.VMEM((2, 2, 2, W_ROWS, width), jnp.float32), pltpu.VMEM((8, 8, 128), jnp.float32)],
+        compiler_params=pltpu.CompilerParams(vmem_limit_bytes=VMEM_LIMIT, collective_id=2, has_side_effects=True),
         name="back_rows",
     )(d_part, loss_part, *rest)
 
@@ -678,17 +724,9 @@
         cand_mine, c_pre, c_hid, cand_vec, targ_raw, t_pre, t_hid, targ_vec = fetch_rows(data_c, data_t, wi_one, wi_two)
         cand_vec = cand_vec.reshape(n_cand, width)
         loss_part, d_query, d_targ_vec, d_part = softmax_grads(query, targ_vec, cand_vec, lq_b, cid_b, targ_loc, tok_total)
-        back_t, back_c, w_mine, loss = back_rows(d_part.reshape(2, 2, 2, n_cand // 8, width), loss_part, d_query, d_targ_vec, tokens, q_pre, q_hid, w_two, targ_raw, t_pre, t_hid, cand_mine, c_pre, c_hid, wi_one, wi_two)
-        w_all = lax.all_gather(w_mine, "dp", axis=0)
+        back_t, back_c, dw_one, dw_two, dwi_one, dwi_two, loss = back_rows(d_part.reshape(2, 2, 2, n_cand // 8, width), loss_part, d_query, d_targ_vec, tokens, q_pre, q_hid, w_two, targ_raw, t_pre, t_hid, cand_mine, c_pre, c_hid, wi_one, wi_two)
+        dw_one, dw_two = lax.psum((dw_one, dw_two), "dp")
         d_table = scatter_rows(ids_two, back_c.reshape(-1, width), back_t.reshape(-1, width), rows_loc)
-
-        def pair(first, n):
-            return jnp.concatenate([w_all[:, first : first + n].reshape(8 * n, width), w_all[:, first + n : first + 2 * n].reshape(8 * n, width)], axis=1)
-
-        dw_one = pair(0, 128)
-        dw_two = w_all[:, 256:320].reshape(-1, width)
-        dwi_one = pair(320, 32)
-        dwi_two = w_all[:, 384:448].reshape(-1, width)
         return loss[0, 0] / tok_total, d_table, dw_one, dw_two, dwi_one, dwi_two
 
     return jax.shard_map(local_step, mesh=mesh, in_specs=(P("dp", None), P(), P(), P(), P(), P("dp", None), P(), P(), P("dp")), out_specs=(P(), P("dp", None), P(), P(), P(), P()), check_vma=False)

time: 279 us -> 254 us (0.910)
  local copies, waits for them, and re-layouts: 23.2 us -> 7.48 us
  Pallas kernels: 237 us -> 228 us
    pallas_call x1, Pallas kernels: 35.6 us -> 20.2 us  [softmax_grads(): pl.pallas_call(functools.partial(softmax_body, tok_total), out_shape=(jax...]
    unnamed x36 -> x14, local copies, waits for them, and re-layouts: 17 us -> 6.29 us
    slice x3 -> x0, local copies, waits for them, and re-layouts: 5.09 us -> none  [the longest x2 2.82 us: pair(): w_all[:, first:first + n].reshape(8 * n, width)]
    pallas_call x1, Pallas kernels: 8.07 us -> 13.1 us  [prepare(): pl.pallas_call(prepare_body, out_shape=(jax.ShapeDtypeStruct((8, 8, 128),...]
    pallas_call x1, Pallas kernels: 49 us -> 53.6 us  [scatter_rows(): pl.pallas_call(scatter_body, out_shape=jax.ShapeDtypeStruct((rows_loc, wi...]
    pallas_call x1, Pallas kernels: 75.4 us -> 71.6 us  [back_rows(): pl.pallas_call(back_body, out_shape=(jax.ShapeDtypeStruct((2, 2, 2, n_tok...]
  transfers between devices with their start and end apart: 1 -> 1, of which waited for: 0 -> 0; matrix products, arithmetic and copies ran while one was open for 0% -> 1% of each run, Pallas kernels for 18% -> 21%
where the time goes in v4:
time: 254 us; the launch traced here: 253 us
  Pallas kernels  228 us (90%)
  between operations  15.9 us (6%)
  local copies, waits for them, and re-layouts  7.48 us (3%)
    pallas_call x1, Pallas kernels, back_rows(): pl.pallas_call(back_body, out_shape=(jax.ShapeDtypeStruct((2, 2, 2, n_tok...  71.6 us
    pallas_call x1, Pallas kernels, scatter_rows(): pl.pallas_call(scatter_body, out_shape=jax.ShapeDtypeStruct((rows_loc, wi...  53.6 us
    pallas_call x1, Pallas kernels, fetch_rows(): pl.pallas_call(fetch_body, out_shape=tuple(rows(n_mine) + outs(n_mine) +...  45.8 us
    pallas_call x1, Pallas kernels, pick_rows(): pl.pallas_call(pick_body, out_shape=(jax.ShapeDtypeStruct((n_cand, width)...  23.5 us
    pallas_call x1, Pallas kernels, softmax_grads(): pl.pallas_call(functools.partial(softmax_body, tok_total), out_shape=(jax...  20.2 us
    pallas_call x1, Pallas kernels, prepare(): pl.pallas_call(prepare_body, out_shape=(jax.ShapeDtypeStruct((8, 8, 128),...  13.1 us
    unnamed x14, local copies, waits for them, and re-layouts  6.29 us
  transfers between devices with their start and end apart: 1, of which 0 were waited for; matrix products, arithmetic and copies ran while one was open for 1% of the time, Pallas kernels for 21%

profile of v4, /device:TPU:0, one launch (start us, length us, event | category | flops | bytes accessed | tf_op | source)
XLA Modules:
  0.0 253.3 jit_solution(11284852305782103132)
XLA Ops:
  7.2 0.0 copy-start.3
  7.2 0.0 all-reduce.3.cloned.1.call-start
  7.2 13.1 %prepare.1 = (s32[8,8,128]{2,1,0:T(8,128)}, f32[4096,128]{1,0:T(8,128)}, s32[4096,128]{1,0:T(8,128)}, f32[1024,512]{1,0:T(8,128)}, bf16[1024,512]{1,0:T(8,128)(2,1)}, /*index=5*/bf16[1024,256]{1,0:T(8,128)(2,1)}) custom-call(s32[8,128]{1,0:T(8,128)} %bitcast.29, f32[32,128]{1,0:T(8,128)} %bitcast.28, s32[32,128]{1,0:T(8,128)} %bitcast.25, ...), custom_call_target="tpu_custom_call" | custom-call | tf_op jit(solution)/shard_map/prepare/pallas_call | solution.py:499
  20.3 0.0 copy-done.3
  20.3 1.4 fusion.2.ids_s
  21.7 23.5 %pick_rows.1 = (bf16[4096,256]{1,0:T(8,128)(2,1)}, bf16[8192,256]{1,0:T(8,128)(2,1)}) custom-call(s32[12288]{0:T(1024)} %fusion.2.ids_s, bf16[32768,256]{1,0:T(8,128)(2,1)} %table.1), custom_call_target="tpu_custom_call" | custom-call | tf_op jit(solution)/shard_map/pick_rows/pallas_call | solution.py:96
  45.2 45.8 %fetch_rows.1 = (bf16[512,256]{1,0:T(8,128)(2,1)}, f32[512,512]{1,0:T(8,128)}, bf16[512,512]{1,0:T(8,128)(2,1)}, bf16[2,2,2,512,256]{4,3,2,1,0:T(8,128)(2,1)}, b...) custom-call(bf16[2,2,2,512,256]{4,3,2,1,0:T(8,128)(2,1)} %bitcast.24, ...), custom_call_target="tpu_custom_call" | custom-call | tf_op jit(solution)/shard_map/fetch_rows/pallas_call | solution.py:590
  91.0 20.2 %softmax_grads.1 = (f32[8,128]{1,0:T(8,128)}, bf16[1024,256]{1,0:T(8,128)(2,1)}, bf16[1024,256]{1,0:T(8,128)(2,1)}, f32[4096,256]{1,0:T(8,128)}) custom-call(bf16[1024,256]{1,0:T(8,128)(2,1)} %get-tuple-element.33.h_ref, bf16[1024,256]{1,0:T(8,128)(2,1)} %get-tuple-element.37.v_ref, bf16[4096,256]{1,0:T(8,128)(2,1)} %bitcast.33, ...), custom_call_target="tpu_custom_call" | custom-call | flops 6442450944 | bytes 16777216 | tf_op jit(solution)/shard_map/softmax_grads/pallas_call | solution.py:317
  111.2 71.6 %back_rows.1 = (bf16[2,2,2,1024,256]{4,3,2,1,0:T(8,128)(2,1)}, bf16[2,2,2,512,256]{4,3,2,1,0:T(8,128)(2,1)}, f32[1024,512]{1,0:T(8,128)}, f32[512,256]{1,0:T(8,1...) custom-call(f32[2,2,2,512,256]{4,3,2,1,0:T(8,128)} %bitcast.22, ...), custom_call_target="tpu_custom_call" | custom-call | tf_op jit(solution)/shard_map/back_rows/pallas_call | solution.py:689
  182.8 0.0 copy-start.4
  182.8 0.0 all-reduce.3.cloned.1.call-update
  182.9 0.7 copy-done.4
  183.6 0.7 fusion.6.ids_v
  184.3 53.6 %scatter_rows.1 = f32[32768,256]{1,0:T(8,128)} custom-call(s32[12288]{0:T(1024)} %fusion.2.ids_s, s32[96,128]{1,0:T(8,128)} %fusion.6.ids_v, bf16[4096,256]{1,0:T(8,128)(2,1)} %bitcast.32, bf16[8192,256]{1,0:T(8,128)(2,1)} %bitcast.31), custom_call_target="tpu_custom_call" | custom-call | flops 60000002048 | bytes 41943040 | tf_op jit(solution)/shard_map/scatter_rows/pallas_call | solution.py:173
  237.9 1.2 slice.3
  239.7 0.0 all-reduce.3.cloned.1.call-done
  239.8 0.0 copy-start.2
  239.8 0.0 copy-start.1
  239.8 3.2 %copy.21 = f32[1024,512]{1,0:T(8,128)} copy(f32[1024,512]{1,0:T(8,128)} %get-tuple-element.70) | data formatting | bytes 4194304
  242.9 0.0 copy-done.2
  242.9 0.0 copy-start
  242.9 0.8 copy.22
  243.7 0.0 copy-done.1
  243.7 0.8 copy.23
  244.5 0.0 copy-done
  244.5 0.8 copy.24
Async XLA Ops:
  7.2 13.2 %copy-start.3 = (s32[4096]{0:T(1024)S(1)}, s32[4096]{0:T(1024)}, u32[]{:S(2)}) copy-start(s32[4096]{0:T(1024)} %param.15) | copy-start | bytes 49156
  7.2 232.6 %all-reduce.3.cloned.1.call-start = ((), (), s32[]{:S(2)}) async-start(), calls=%async_computation | async-start | bytes 5242880 | tf_op jit(solution)/shard_map/psum | solution.py:728
  182.8 0.8 copy-start.4
  239.8 3.2 %copy-start.2 = (f32[512,256]{1,0:T(8,128)S(1)}, f32[512,256]{1,0:T(8,128)}, u32[]{:S(2)}) copy-start(f32[512,256]{1,0:T(8,128)} %get-tuple-element.71) | copy-start | bytes 1572868
  239.8 4.0 %copy-start.1 = (f32[256,512]{1,0:T(8,128)S(1)}, f32[256,512]{1,0:T(8,128)}, u32[]{:S(2)}) copy-start(f32[256,512]{1,0:T(8,128)} %get-tuple-element.72) | copy-start | bytes 1572868
  242.9 1.6 copy-start
Sparse Core Ops, SparseCore 0:
  183.0 53.9 all-reduce.2

commit v5 on v4

--- a/solution.py
+++ b/solution.py
@@ -15,7 +15,7 @@
     pre_act = jnp.dot(row_block, w_in, preferred_element_type=jnp.float32)
     hidden = jax.nn.gelu(pre_act).astype(jnp.bfloat16)
     tower_out = jnp.dot(hidden, w_out, preferred_element_type=jnp.float32).astype(jnp.bfloat16)
-    return pre_act, hidden, tower_out
+    return tower_out
 
 
 def over_rows(a, b):
@@ -26,24 +26,21 @@
     return lax.dot_general(a, b, (((1,), (1,)), ((), ())), preferred_element_type=jnp.float32)
 
 
-def grad_through(grad_out, w_out, pre_act):
+def tower_back(row_block, w_in, w_out, grad_out):
+    pre_act = jnp.dot(row_block, w_in, preferred_element_type=jnp.float32)
+    hidden, gelu_back = jax.vjp(jax.nn.gelu, pre_act)
     grad_hidden = by_transpose(grad_out, w_out)
-    gelu_back = jax.vjp(jax.nn.gelu, pre_act)[1]
-    return gelu_back(grad_hidden)[0].astype(jnp.bfloat16)
-
-
-def tower_back(row_block, w_out, pre_act, hidden, grad_out):
-    dw_out = over_rows(hidden, grad_out)
-    grad_pre = grad_through(grad_out, w_out, pre_act)
-    dw_in = over_rows(row_block, grad_pre)
-    return grad_pre, dw_in, dw_out
+    return gelu_back(grad_hidden)[0].astype(jnp.bfloat16), hidden.astype(jnp.bfloat16)
 
 
 VMEM_LIMIT = 63 * 1024 * 1024
 BATCH = 128
 SPARE = 256
+GROUP = 16
 STAGE_ROWS = 2048
 OUT_ROWS = 1024
+IN_SLOTS = 12
+OUT_SLOTS = 12
 
 
 def pick_body(ids_s, table, cand_out, targ_out, wide, stage, rows_f, stage_sem):
@@ -54,17 +51,17 @@
     def stage_copy(i, slot):
         return pltpu.make_async_copy(table.at[pl.ds(i * STAGE_ROWS, STAGE_ROWS)], stage.at[slot], stage_sem.at[slot])
 
-    for i in range(3):
+    for i in range(IN_SLOTS - 1):
         stage_copy(i, i).start()
     wide[pl.ds(2 * rows_loc, 2 * SPARE), :] = jnp.zeros((2 * SPARE, lane), jnp.float32)
 
     @pl.loop(0, n_stage)
     def _(i):
-        slot = i % 4
-
-        @pl.when(i + 3 < n_stage)
+        slot = i % IN_SLOTS
+
+        @pl.when(i + IN_SLOTS - 1 < n_stage)
         def _():
-            stage_copy(i + 3, (i + 3) % 4).start()
+            stage_copy(i + IN_SLOTS - 1, (i + IN_SLOTS - 1) % IN_SLOTS).start()
 
         stage_copy(i, slot).wait()
 
@@ -100,37 +97,46 @@
         out_specs=(vmem, vmem),
         scratch_shapes=[
             pltpu.VMEM((2 * (rows_loc + SPARE), width // 2), jnp.float32),
-            pltpu.VMEM((4, STAGE_ROWS, width), jnp.bfloat16),
+            pltpu.VMEM((IN_SLOTS, STAGE_ROWS, width), jnp.bfloat16),
             pltpu.VMEM((2 * BATCH, width // 2), jnp.float32),
-            pltpu.SemaphoreType.DMA((4,)),
+            pltpu.SemaphoreType.DMA((IN_SLOTS,)),
         ],
         compiler_params=pltpu.CompilerParams(vmem_limit_bytes=VMEM_LIMIT),
         name="pick_rows",
     )(ids_two, table_loc)
 
 
-def scatter_body(ids_s, ids_v, cand_ref, targ_ref, out_ref, acc, g2, new, out_stage, sem):
+def scatter_body(ids_s, ids_v, cand_hbm, targ_hbm, out_ref, acc, g2, cand_ref, targ_ref, out_stage, sem, in_sem):
     rows, width = out_ref.shape
     lane = width // 2
     n_cand = cand_ref.shape[0]
     n_all = n_cand + targ_ref.shape[0]
+    in_copies = [pltpu.make_async_copy(cand_hbm, cand_ref, in_sem.at[0]), pltpu.make_async_copy(targ_hbm, targ_ref, in_sem.at[1])]
+    for copy in in_copies:
+        copy.start()
 
     @pl.loop(0, 2 * rows // 512)
     def _(i):
         acc[pl.ds(pl.multiple_of(i * 512, 512), 512), :] = jnp.zeros((512, lane), jnp.float32)
 
+    row_i = lax.broadcasted_iota(jnp.int32, (BATCH, BATCH), 0) // GROUP
+    col_i = lax.broadcasted_iota(jnp.int32, (BATCH, BATCH), 1) // GROUP
+    same_group = row_i == col_i
+
     def one_batch(b, src, src_base):
         idr = jnp.broadcast_to(ids_v[pl.ds(b, 1), :], (BATCH, BATCH))
-        same = jnp.where(idr == idr.T, 1.0, 0.0).astype(jnp.bfloat16)
+        same = jnp.where((idr == idr.T) & same_group, 1.0, 0.0).astype(jnp.bfloat16)
         part = jnp.dot(same, src[pl.ds(pl.multiple_of(b * BATCH - src_base, BATCH), BATCH), :], preferred_element_type=jnp.float32)
         g2[pl.ds(0, BATCH, 2), :] = part[:, :lane]
         g2[pl.ds(1, BATCH, 2), :] = part[:, lane:]
-        for r in range(BATCH):
-            at = pl.multiple_of(ids_s[b * BATCH + r], 2)
-            new[pl.ds(2 * r, 2), :] = acc[pl.ds(at, 2), :] + g2[pl.ds(2 * r, 2), :]
-        for r in range(BATCH):
-            at = pl.multiple_of(ids_s[b * BATCH + r], 2)
-            acc[pl.ds(at, 2), :] = new[pl.ds(2 * r, 2), :]
+        for g in range(BATCH // GROUP):
+            at = [pl.multiple_of(ids_s[b * BATCH + g * GROUP + r], 2) for r in range(GROUP)]
+            new = [acc[pl.ds(at[r], 2), :] + g2[pl.ds(2 * (g * GROUP + r), 2), :] for r in range(GROUP)]
+            for r in range(GROUP):
+                acc[pl.ds(at[r], 2), :] = new[r]
+
+    for copy in in_copies:
+        copy.wait()
 
     @pl.loop(0, n_cand // BATCH)
     def _(b):
@@ -147,11 +153,11 @@
 
     @pl.loop(0, n_out)
     def _(i):
-        slot = i % 4
-
-        @pl.when(i >= 4)
+        slot = i % OUT_SLOTS
+
+        @pl.when(i >= OUT_SLOTS)
         def _():
-            out_copy(i - 4, slot).wait()
+            out_copy(i - OUT_SLOTS, slot).wait()
 
         @pl.loop(0, OUT_ROWS // 128)
         def _(j):
@@ -162,8 +168,8 @@
 
         out_copy(i, slot).start()
 
-    for i in range(n_out - 4, n_out):
-        out_copy(i, i % 4).wait()
+    for i in range(n_out - OUT_SLOTS, n_out):
+        out_copy(i, i % OUT_SLOTS).wait()
 
 
 def scatter_rows(ids_two, back_cand, back_targ, rows_loc):
@@ -173,14 +179,16 @@
     return pl.pallas_call(
         scatter_body,
         out_shape=jax.ShapeDtypeStruct((rows_loc, width), jnp.float32),
-        in_specs=[pl.BlockSpec(memory_space=pltpu.SMEM), vmem, vmem, vmem],
+        in_specs=[pl.BlockSpec(memory_space=pltpu.SMEM), vmem, pl.BlockSpec(memory_space=pl.ANY), pl.BlockSpec(memory_space=pl.ANY)],
         out_specs=pl.BlockSpec(memory_space=pl.ANY),
         scratch_shapes=[
             pltpu.VMEM((2 * (rows_loc + SPARE), width // 2), jnp.float32),
             pltpu.VMEM((2 * BATCH, width // 2), jnp.float32),
-            pltpu.VMEM((2 * BATCH, width // 2), jnp.float32),
-            pltpu.VMEM((4, OUT_ROWS, width), jnp.float32),
-            pltpu.SemaphoreType.DMA((4,)),
+            pltpu.VMEM(back_cand.shape, jnp.bfloat16),
+            pltpu.VMEM(back_targ.shape, jnp.bfloat16),
+            pltpu.VMEM((OUT_SLOTS, OUT_ROWS, width), jnp.float32),
+            pltpu.SemaphoreType.DMA((OUT_SLOTS,)),
+            pltpu.SemaphoreType.DMA((2,)),
         ],
         compiler_params=pltpu.CompilerParams(vmem_limit_bytes=VMEM_LIMIT),
         cost_estimate=pl.CostEstimate(flops=60_000_000_000, bytes_accessed=40 << 20, transcendentals=0),
@@ -304,28 +312,6 @@
     ]
 
 
-def softmax_body(tok_total, h_ref, v_ref, u_ref, lq_ref, cid_ref, tid_ref, loss_ref, dh_ref, dv_ref, du_ref, z_a, z_b, e_s, m_s, s_s, ut_s, fac_s, dz_a, dz_b, dht_s):
-    h = h_ref[...]
-    logits_pass(u_ref, h, lq_ref, cid_ref, tid_ref[...], z_a, z_b, e_s, m_s, s_s)
-    loss_pass(tok_total, u_ref, ut_s, h, v_ref[...], e_s, m_s, s_s, fac_s, dz_a, dz_b, dht_s, loss_ref, dh_ref, dv_ref, du_ref)
-
-
-def softmax_grads(query, targ_vec, cand_vec, lq_b, cid_b, targ_ids, tok_total):
-    n_tok, width = query.shape
-    n_cand = cand_vec.shape[0]
-    vmem = pl.BlockSpec(memory_space=pltpu.VMEM)
-    return pl.pallas_call(
-        functools.partial(softmax_body, tok_total),
-        out_shape=(jax.ShapeDtypeStruct((8, 128), jnp.float32), jax.ShapeDtypeStruct((n_tok, width), jnp.bfloat16), jax.ShapeDtypeStruct((n_tok, width), jnp.bfloat16), jax.ShapeDtypeStruct((n_cand, width), jnp.float32)),
-        in_specs=[vmem] * 6,
-        out_specs=(vmem,) * 4,
-        scratch_shapes=softmax_scratch(n_cand, n_tok, width),
-        compiler_params=pltpu.CompilerParams(vmem_limit_bytes=VMEM_LIMIT),
-        cost_estimate=pl.CostEstimate(flops=6 * n_tok * n_cand * width, bytes_accessed=16 << 20, transcendentals=n_tok * n_cand),
-        name="softmax_grads",
-    )(query, targ_vec, cand_vec, lq_b, cid_b, targ_ids.reshape(1, n_tok))
-
-
 MESH = pl.DeviceIdType.MESH
 
 
@@ -466,66 +452,54 @@
     return [pltpu.SemaphoreType.DMA((5,)), pltpu.SemaphoreType.DMA((5,))]
 
 
-def prepare_body(mine, lq_ref, cid_ref, tokens, w_one, w_two, full, lq_out, cid_out, q_pre, q_hid, query, send_sem, recv_sem):
+def prepare_body(mine, tokens, w_one, w_two, full, query, send_sem, recv_sem):
     place = my_place()
     greet(place)
     for i in range(tokens.shape[0] // 256):
         at = slice(i * 256, i * 256 + 256)
-        pre, hid, vec = tower_fwd(tokens[at, :], w_one[...], w_two[...])
-        q_pre[at, :] = pre
-        q_hid[at, :] = hid
-        query[at, :] = vec
+        query[at, :] = tower_fwd(tokens[at, :], w_one[...], w_two[...])
     pl.semaphore_wait(pltpu.get_barrier_semaphore(), 7)
     full[place[0]] = mine[...]
     copies = []
     for k in range(1, 8):
         copies.append(push(mine, full.at[place[0]], send_sem.at[k], recv_sem.at[k], peer_of(place, k // 4, (k // 2) % 2, k % 2)))
 
-    @pl.loop(0, lq_ref.shape[0])
-    def _(i):
-        rows = pl.ds(pl.multiple_of(i * 128, 128), 128)
-        lq_out[rows, :] = jnp.broadcast_to(lq_ref[pl.ds(i, 1), :], (128, 128)).T
-        cid_out[rows, :] = jnp.broadcast_to(cid_ref[pl.ds(i, 1), :], (128, 128)).T
-
     for copy in copies:
         copy.wait()
 
 
-def prepare(targ_loc, log_q, cand_ids, tokens, w_one, w_two):
-    n_cand = cand_ids.shape[0]
+def prepare(targ_loc, tokens, w_one, w_two):
     n_tok = tokens.shape[0]
-    ff, width = w_two.shape
     vmem = pl.BlockSpec(memory_space=pltpu.VMEM)
     return pl.pallas_call(
         prepare_body,
-        out_shape=(
-            jax.ShapeDtypeStruct((8, 8, 128), jnp.int32),
-            jax.ShapeDtypeStruct((n_cand, 128), jnp.float32),
-            jax.ShapeDtypeStruct((n_cand, 128), jnp.int32),
-            jax.ShapeDtypeStruct((n_tok, ff), jnp.float32),
-            jax.ShapeDtypeStruct((n_tok, ff), jnp.bfloat16),
-            jax.ShapeDtypeStruct((n_tok, width), jnp.bfloat16),
-        ),
-        in_specs=[vmem] * 6,
-        out_specs=(vmem,) * 6,
+        out_shape=(jax.ShapeDtypeStruct((8, 8, 128), jnp.int32), jax.ShapeDtypeStruct((n_tok, w_two.shape[1]), jnp.bfloat16)),
+        in_specs=[vmem] * 4,
+        out_specs=(vmem,) * 2,
         scratch_shapes=[pltpu.SemaphoreType.DMA((8,)), pltpu.SemaphoreType.DMA((8,))],
         compiler_params=pltpu.CompilerParams(vmem_limit_bytes=VMEM_LIMIT, collective_id=0, has_side_effects=True),
         name="prepare",
-    )(targ_loc.reshape(8, 128), log_q.reshape(-1, 128), cand_ids.reshape(-1, 128), tokens, w_one, w_two)
+    )(targ_loc.reshape(8, 128), tokens, w_one, w_two)
 
 
 PIECE = 256
 
 
-def fetch_body(data_c, data_t, wi_one, wi_two, cand_raw, c_pre, c_hid, cand_vec, targ_raw, t_pre, t_hid, targ_vec, in_one, mid, in_xa, in_yb, part_a, part_b, in_ya, in_xb, rs_send, rs_recv, ag_send, ag_recv):
+def score_body(tok_total, c_hbm, t_hbm, wi_one, wi_two, h_ref, lq_ref, cid_ref, tid_ref, cand_raw, targ_raw, loss_ref, dh_ref, dv_ref, du_ref, *scratch):
     place = my_place()
     me, y, x, c = place
     half = PIECE // 2
+    data_c, data_t, in_sem, cand_vec, lq_b, cid_b, rs, ag_send, ag_recv = scratch[0:6] + (scratch[6:16],) + scratch[16:18]
+    z_a, z_b, e_s, m_s, s_s, ut_s, fac_s, dz_a, dz_b, dht_s, u_s = scratch[18:29]
+    n_cand, width = du_ref.shape
+    in_copies = [pltpu.make_async_copy(c_hbm, data_c, in_sem.at[0]), pltpu.make_async_copy(t_hbm, data_t, in_sem.at[1])]
+    for copy in in_copies:
+        copy.start()
     meet(place)
     reduces = []
     for k in range(6):
         data = data_c.at[:, :, :, pl.ds(k * PIECE, PIECE)] if k < 2 else data_t.at[:, :, :, pl.ds((k - 2) * PIECE, PIECE)]
-        reduces.append(Reduce(place, data, in_one.at[k], mid.at[k], in_xa.at[k], in_yb.at[k], part_a.at[k], part_b.at[k], in_ya.at[k], in_xb.at[k], rs_send.at[k], rs_recv.at[k]))
+        reduces.append(Reduce(place, data, *[r.at[k] for r in rs]))
     ag = Gather(place, cand_vec, ag_send, ag_recv)
 
     def close(k, out, base):
@@ -533,18 +507,11 @@
         out[base : base + half, :] = first
         out[base + half : base + PIECE, :] = second
 
-    def tower(rows_ref, at, w_in, w_out, pre_ref, hid_ref):
-        pre, hid, vec = tower_fwd(rows_ref[at, :], w_in[...], w_out[...])
-        pre_ref[at, :] = pre
-        hid_ref[at, :] = hid
-        return vec
-
-    def targ_tower(k):
-        close(k + 2, targ_raw, k * PIECE)
-        at = slice(k * PIECE, (k + 1) * PIECE)
-        targ_vec[at, :] = tower(targ_raw, at, wi_one, wi_two, t_pre, t_hid)
-
-    for k in range(6):
+    in_copies[0].wait()
+    reduces[0].one()
+    reduces[1].one()
+    in_copies[1].wait()
+    for k in range(2, 6):
         reduces[k].one()
     reduces[0].two()
     reduces[1].two()
@@ -552,67 +519,83 @@
     reduces[0].three()
     reduces[1].three()
     reduces[3].two()
-    reduces[4].two()
+
+    @pl.loop(0, n_cand // 128)
+    def _(i):
+        rows = pl.ds(pl.multiple_of(i * 128, 128), 128)
+        lq_b[rows, :] = jnp.broadcast_to(lq_ref[pl.ds(i, 1), :], (128, 128)).T
+        cid_b[rows, :] = jnp.broadcast_to(cid_ref[pl.ds(i, 1), :], (128, 128)).T
+
     close(0, cand_raw, 0)
     close(1, cand_raw, PIECE)
-    cand_vec[y, x, c] = tower(cand_raw, slice(0, 512), wi_one, wi_two, c_pre, c_hid)
+    cand_vec[y, x, c] = tower_fwd(cand_raw[...], wi_one[...], wi_two[...])
     ag.one()
+    reduces[4].two()
     reduces[5].two()
     reduces[2].three()
     ag.two()
     reduces[3].three()
     reduces[4].three()
-    targ_tower(0)
+    ag.three()
     reduces[5].three()
-    targ_tower(1)
-    ag.three()
-    targ_tower(2)
-    targ_tower(3)
     ag.last()
+    n_mine = n_cand // 8
+    for b in range(8):
+        u_s[b * n_mine : (b + 1) * n_mine, :] = cand_vec[b // 4, (b // 2) % 2, b % 2]
+    h = h_ref[...]
+    logits_pass(u_s, h, lq_b, cid_b, tid_ref[...], z_a, z_b, e_s, m_s, s_s)
+    for k in range(4):
+        close(k + 2, targ_raw, k * PIECE)
+    v = tower_fwd(targ_raw[...], wi_one[...], wi_two[...])
+    loss_pass(tok_total, u_s, ut_s, h, v, e_s, m_s, s_s, fac_s, dz_a, dz_b, dht_s, loss_ref, dh_ref, dv_ref, du_ref)
     for red in reduces:
         red.drain()
     ag.drain()
 
 
-def fetch_rows(data_c, data_t, wi_one, wi_two):
+def score(tok_total, data_c, data_t, wi_one, wi_two, query, log_q, cand_ids, targ_loc):
     n_mine, width = data_c.shape[3:]
     n_tok = data_t.shape[3]
-    ff = wi_one.shape[1]
+    n_cand = 8 * n_mine
     vmem = pl.BlockSpec(memory_space=pltpu.VMEM)
-
-    def outs(n):
-        return [jax.ShapeDtypeStruct((n, ff), jnp.float32), jax.ShapeDtypeStruct((n, ff), jnp.bfloat16)]
-
-    def rows(n):
-        return [jax.ShapeDtypeStruct((n, width), jnp.bfloat16)]
-
-    full = [jax.ShapeDtypeStruct((2, 2, 2, n_mine, width), jnp.bfloat16)]
+    hbm = pl.BlockSpec(memory_space=pl.ANY)
+    scratch = [pltpu.VMEM(data_c.shape, jnp.bfloat16), pltpu.VMEM(data_t.shape, jnp.bfloat16), pltpu.SemaphoreType.DMA((2,))]
+    scratch += [pltpu.VMEM(data_c.shape, jnp.bfloat16), pltpu.VMEM((n_cand, 128), jnp.float32), pltpu.VMEM((n_cand, 128), jnp.int32)]
+    scratch += reduce_scratch(6, PIECE, width, jnp.bfloat16) + gather_sems() + softmax_scratch(n_cand, n_tok, width)
+    scratch += [pltpu.VMEM((n_cand, width), jnp.bfloat16)]
+    rows = [jax.ShapeDtypeStruct((n, width), jnp.bfloat16) for n in (n_mine, n_tok, n_tok, n_tok)]
     return pl.pallas_call(
-        fetch_body,
-        out_shape=tuple(rows(n_mine) + outs(n_mine) + full + rows(n_tok) + outs(n_tok) + rows(n_tok)),
-        in_specs=[vmem] * 4,
-        out_specs=(vmem,) * 8,
-        scratch_shapes=reduce_scratch(6, PIECE, width, jnp.bfloat16) + gather_sems(),
+        functools.partial(score_body, tok_total),
+        out_shape=(rows[0], rows[1], jax.ShapeDtypeStruct((8, 128), jnp.float32), rows[2], rows[3], jax.ShapeDtypeStruct((n_cand, width), jnp.float32)),
+        in_specs=[hbm, hbm] + [vmem] * 6,
+        out_specs=(vmem,) * 6,
+        scratch_shapes=scratch,
         compiler_params=pltpu.CompilerParams(vmem_limit_bytes=VMEM_LIMIT, collective_id=1, has_side_effects=True),
-        name="fetch_rows",
-    )(data_c, data_t, wi_one, wi_two)
-
-
-def back_body(d_part, loss_in, d_query, d_targ, tokens, q_pre, q_hid, w_two, targ_raw, t_pre, t_hid, cand_raw, c_pre, c_hid, wi_one, wi_two, back_t, back_c, dw_one_out, dw_two_out, dwi_one_out, dwi_two_out, loss_out, *scratch):
+        name="score",
+    )(data_c, data_t, wi_one, wi_two, query, log_q.reshape(-1, 128), cand_ids.reshape(-1, 128), targ_loc.reshape(1, n_tok))
+
+
+W_ROWS = 448
+
+
+def back_body(part_hbm, tok_hbm, loss_in, d_query, d_targ, w_one, w_two, targ_raw, cand_raw, wi_one, wi_two, back_t, back_c, w_first, w_rest, loss_out, *scratch):
     place = my_place()
     me, y, x, c = place
     rs_u, rs_w = scratch[0:10], scratch[10:20]
-    at_send, at_recv, ac_send, ac_recv, aw_send, aw_recv, l_send, l_recv, w_data, w_full, l_all = scratch[20:31]
+    at_send, at_recv, ac_send, ac_recv, l_send, l_recv, w_data, l_all, d_part, tokens, in_sem = scratch[20:31]
     width = d_query.shape[1]
     scale = SCORE_GAIN / math.sqrt(width)
+    in_copies = [pltpu.make_async_copy(part_hbm, d_part, in_sem.at[0]), pltpu.make_async_copy(tok_hbm, tokens, in_sem.at[1])]
+    for copy in in_copies:
+        copy.start()
     meet(place)
     red_u = []
     for k in range(2):
-        red_u.append(Reduce(place, d_part.at[:, :, :, pl.ds(k * PIECE, PIECE)], *[s.at[k] for s in rs_u]))
-    red_w = Reduce(place, w_data, *[s.at[0] for s in rs_w])
+        red_u.append(Reduce(place, d_part.at[:, :, :, pl.ds(k * PIECE, PIECE)], *[r.at[k] for r in rs_u]))
+    red_w = Reduce(place, w_data, *[r.at[0] for r in rs_w])
     ag_t = Gather(place, back_t, at_send, at_recv)
     ag_c = Gather(place, back_c, ac_send, ac_recv)
-    ag_w = Gather(place, w_full, aw_send, aw_recv)
+    in_copies[0].wait()
     red_u[0].one()
     red_u[1].one()
     l_all[me] = loss_in[...]
@@ -625,84 +608,76 @@
         for b in range(8):
             w_data[b // 4, (b // 2) % 2, b % 2, first : first + n, :] = value[b * n : (b + 1) * n, :]
 
-    dwi_two = over_rows(t_hid[...], d_targ[...])
+    t_q, t_hid = tower_back(targ_raw[...], wi_one[...], wi_two[...], d_targ[...])
     red_u[0].two()
     red_u[1].two()
-    t_q = grad_through(d_targ[...], wi_two[...], t_pre[...])
     back_t[y, x, c] = by_transpose(t_q, wi_one[...]).astype(jnp.bfloat16)
     ag_t.one()
-    dwi_one = over_rows(targ_raw[...], t_q)
-    _, dw_one, dw_two = tower_back(tokens[...], w_two[...], q_pre[...], q_hid[...], d_query[...])
-    dw_one_out[...] = dw_one
-    dw_two_out[...] = dw_two
+    in_copies[1].wait()
+    q_q, q_hid = tower_back(tokens[...], w_one[...], w_two[...], d_query[...])
     red_u[0].three()
     red_u[1].three()
     ag_t.two()
+    dw_one = over_rows(tokens[...], q_q)
+    put(0, dw_one[:, :width])
+    put(128, dw_one[:, width:])
+    put(256, over_rows(q_hid, d_query[...]))
     parts = []
     for k in range(2):
         first, second = red_u[k].last()
         parts += [first, second]
     d_cand = (jnp.concatenate(parts, axis=0) * scale).astype(jnp.bfloat16)
-    c_q, dwi_one_c, dwi_two_c = tower_back(cand_raw[...], wi_two[...], c_pre[...], c_hid[...], d_cand)
+    c_q, c_hid = tower_back(cand_raw[...], wi_one[...], wi_two[...], d_cand)
     back_c[y, x, c] = by_transpose(c_q, wi_one[...]).astype(jnp.bfloat16)
     ag_c.one()
-    dwi_one = dwi_one + dwi_one_c
-    put(0, dwi_one[:, :width])
-    put(32, dwi_one[:, width:])
-    put(64, dwi_two + dwi_two_c)
+    dwi_one = over_rows(targ_raw[...], t_q) + over_rows(cand_raw[...], c_q)
+    put(320, dwi_one[:, :width])
+    put(352, dwi_one[:, width:])
+    put(384, over_rows(t_hid, d_targ[...]) + over_rows(c_hid, d_cand))
     red_w.one()
     for copy in l_copies:
         copy.wait()
     loss_out[...] = jnp.sum(l_all[...], axis=0)
+    ag_c.two()
     red_w.two()
+    ag_t.three()
     red_w.three()
-    ag_c.two()
+    ag_c.three()
     first, second = red_w.last()
-    half = first.shape[0]
-    w_full[y, x, c, 0:half, :] = first
-    w_full[y, x, c, half : 2 * half, :] = second
-    ag_w.one()
-    ag_t.three()
-    ag_w.two()
-    ag_c.three()
-    ag_w.three()
+    w_mine = jnp.concatenate([first, second], axis=0)
+    w_first[:, :width] = w_mine[0:128]
+    w_first[:, width:] = w_mine[128:256]
+    w_rest[...] = w_mine[256:W_ROWS]
     ag_t.last()
     ag_c.last()
-    ag_w.last()
-    for b in range(8):
-        block = w_full.at[b // 4, (b // 2) % 2, b % 2]
-        dwi_one_out[b * 32 : (b + 1) * 32, :width] = block[0:32, :]
-        dwi_one_out[b * 32 : (b + 1) * 32, width:] = block[32:64, :]
-        dwi_two_out[b * 64 : (b + 1) * 64, :] = block[64:128, :]
-    for part in red_u + [red_w, ag_t, ag_c, ag_w]:
+    for part in red_u + [red_w, ag_t, ag_c]:
         part.drain()
 
 
-W_ROWS = 128
-
-
-def back_rows(d_part, loss_part, *rest):
+def back_rows(d_part, tokens, loss_part, d_query, d_targ, w_one, w_two, targ_raw, cand_raw, wi_one, wi_two):
     n_mine, width = d_part.shape[3:]
-    n_tok = rest[0].shape[0]
+    n_tok = d_query.shape[0]
     vmem = pl.BlockSpec(memory_space=pltpu.VMEM)
-    sems = [pltpu.SemaphoreType.DMA((8,)), pltpu.SemaphoreType.DMA((8,))]
+    hbm = pl.BlockSpec(memory_space=pl.ANY)
+    scratch = reduce_scratch(2, PIECE, width, jnp.float32) + reduce_scratch(1, W_ROWS, width, jnp.float32) + gather_sems() + gather_sems()
+    scratch += [pltpu.SemaphoreType.DMA((8,)), pltpu.SemaphoreType.DMA((8,))]
+    scratch += [pltpu.VMEM((2, 2, 2, W_ROWS, width), jnp.float32), pltpu.VMEM((8, 8, 128), jnp.float32)]
+    scratch += [pltpu.VMEM(d_part.shape, jnp.float32), pltpu.VMEM(tokens.shape, jnp.bfloat16), pltpu.SemaphoreType.DMA((2,))]
     return pl.pallas_call(
         back_body,
         out_shape=(
             jax.ShapeDtypeStruct((2, 2, 2, n_tok, width), jnp.bfloat16),
             jax.ShapeDtypeStruct((2, 2, 2, n_mine, width), jnp.bfloat16),
-            jax.ShapeDtypeStruct((rest[2].shape[1], rest[3].shape[1]), jnp.float32),
-            jax.ShapeDtypeStruct(rest[5].shape, jnp.float32),
-            jax.ShapeDtypeStruct(rest[12].shape, jnp.float32),
-            jax.ShapeDtypeStruct(rest[13].shape, jnp.float32),
+            jax.ShapeDtypeStruct((128, 2 * width), jnp.float32),
+            jax.ShapeDtypeStruct((W_ROWS - 256, width), jnp.float32),
             jax.ShapeDtypeStruct((8, 128), jnp.float32),
         ),
-        in_specs=[vmem] * 16,
-        out_specs=(vmem,) * 7,
-        scratch_shapes=reduce_scratch(2, PIECE, width, jnp.float32) + reduce_scratch(1, W_ROWS, width, jnp.float32) + gather_sems() + gather_sems() + gather_sems() + sems + [pltpu.VMEM((2, 2, 2, W_ROWS, width), jnp.float32), pltpu.VMEM((2, 2, 2, W_ROWS, width), jnp.float32), pltpu.VMEM((8, 8, 128), jnp.float32)],
+        in_specs=[hbm, hbm] + [vmem] * 9,
+        out_specs=(vmem,) * 5,
+        scratch_shapes=scratch,
         compiler_params=pltpu.CompilerParams(vmem_limit_bytes=VMEM_LIMIT, collective_id=2, has_side_effects=True),
         name="back_rows",
-    )(d_part, loss_part, *rest)
+    )(d_part, tokens, loss_part, d_query, d_targ, w_one, w_two, targ_raw, cand_raw, wi_one, wi_two)
 
 
 def solution(mesh):
@@ -713,7 +688,7 @@
         rows_loc, width = table_loc.shape
         n_cand = cand_ids.shape[0]
         tok_total = tokens.shape[0] * num_dev
-        targ_all, lq_b, cid_b, q_pre, q_hid, query = prepare(targ_loc, log_q, cand_ids, tokens, w_one, w_two)
+        targ_all, query = prepare(targ_loc, tokens, w_one, w_two)
         targ_all = targ_all.reshape(-1)
         local_ids = jnp.concatenate([cand_ids, targ_all]) - my_index * rows_loc
         spare = rows_loc + jnp.arange(local_ids.shape[0], dtype=jnp.int32) % SPARE
@@ -721,12 +696,14 @@
         data_c, data_t = pick_rows(ids_two, table_loc, n_cand)
         data_c = data_c.reshape(2, 2, 2, n_cand // 8, width)
         data_t = data_t.reshape(2, 2, 2, tokens.shape[0], width)
-        cand_mine, c_pre, c_hid, cand_vec, targ_raw, t_pre, t_hid, targ_vec = fetch_rows(data_c, data_t, wi_one, wi_two)
-        cand_vec = cand_vec.reshape(n_cand, width)
-        loss_part, d_query, d_targ_vec, d_part = softmax_grads(query, targ_vec, cand_vec, lq_b, cid_b, targ_loc, tok_total)
-        back_t, back_c, dw_one, dw_two, dwi_one, dwi_two, loss = back_rows(d_part.reshape(2, 2, 2, n_cand // 8, width), loss_part, d_query, d_targ_vec, tokens, q_pre, q_hid, w_two, targ_raw, t_pre, t_hid, cand_mine, c_pre, c_hid, wi_one, wi_two)
-        dw_one, dw_two = lax.psum((dw_one, dw_two), "dp")
+        cand_raw, targ_raw, loss_part, d_query, d_targ, d_part = score(tok_total, data_c, data_t, wi_one, wi_two, query, log_q, cand_ids, targ_loc)
+        back_t, back_c, w_first, w_rest, loss = back_rows(d_part.reshape(2, 2, 2, n_cand // 8, width), tokens, loss_part, d_query, d_targ, w_one, w_two, targ_raw, cand_raw, wi_one, wi_two)
+        dw_one = lax.all_gather(w_first, "dp", axis=0, tiled=True)
+        w_all = lax.all_gather(w_rest, "dp", axis=0)
         d_table = scatter_rows(ids_two, back_c.reshape(-1, width), back_t.reshape(-1, width), rows_loc)
+        dw_two = w_all[:, 0:64].reshape(-1, width)
+        dwi_one = jnp.concatenate([w_all[:, 64:96].reshape(-1, width), w_all[:, 96:128].reshape(-1, width)], axis=1)
+        dwi_two = w_all[:, 128:192].reshape(-1, width)
         return loss[0, 0] / tok_total, d_table, dw_one, dw_two, dwi_one, dwi_two
 
     return jax.shard_map(local_step, mesh=mesh, in_specs=(P("dp", None), P(), P(), P(), P(), P("dp", None), P(), P(), P("dp")), out_specs=(P(), P("dp", None), P(), P(), P(), P()), check_vma=False)

time: 254 us -> 235 us (0.925)
  Pallas kernels: 228 us -> 209 us
    pallas_call x2 -> x1, Pallas kernels: 66 us -> 55.6 us  [score(): pl.pallas_call(functools.partial(score_body, tok_total), out_shape=(rows[...]
    pallas_call x1, Pallas kernels: 53.6 us -> 47.8 us  [scatter_rows(): pl.pallas_call(scatter_body, out_shape=jax.ShapeDtypeStruct((rows_loc, wi...]
    unnamed x14 -> x9, local copies, waits for them, and re-layouts: 6.29 us -> 3.1 us
  transfers between devices with their start and end apart: 1 -> 2, of which waited for: 0 -> 0; matrix products, arithmetic and copies ran while one was open for 1% -> 2% of each run, Pallas kernels for 21% -> 20%
where the time goes in v5:
time: 235 us
  Pallas kernels  209 us (89%)
  between operations  15.9 us (7%)
  local copies, waits for them, and re-layouts  6.53 us (3%)
  other arithmetic  2.92 us (1%)
    pallas_call x1, Pallas kernels, back_rows(): pl.pallas_call(back_body, out_shape=(jax.ShapeDtypeStruct((2, 2, 2, n_tok...  71.9 us
    pallas_call x1, Pallas kernels, score(): pl.pallas_call(functools.partial(score_body, tok_total), out_shape=(rows[...  55.6 us
    pallas_call x1, Pallas kernels, scatter_rows(): pl.pallas_call(scatter_body, out_shape=jax.ShapeDtypeStruct((rows_loc, wi...  47.8 us
    pallas_call x1, Pallas kernels, pick_rows(): pl.pallas_call(pick_body, out_shape=(jax.ShapeDtypeStruct((n_cand, width)...  22.4 us
    pallas_call x1, Pallas kernels, prepare(): pl.pallas_call(prepare_body, out_shape=(jax.ShapeDtypeStruct((8, 8, 128),...  10.8 us
  transfers between devices with their start and end apart: 2, of which 0 were waited for; matrix products, arithmetic and copies ran while one was open for 2% of the time, Pallas kernels for 20%

profile of v5, /device:TPU:0, one launch (start us, length us, event | category | flops | bytes accessed | tf_op | source)
XLA Modules:
  0.0 234.7 jit_solution(10405374807217965660)
XLA Ops:
  7.2 0.0 copy-start.1
  7.2 0.0 all-gather.6.cloned.1.call-start
  7.2 10.8 %prepare.1 = (s32[8,8,128]{2,1,0:T(8,128)}, bf16[1024,256]{1,0:T(8,128)(2,1)}) custom-call(s32[8,128]{1,0:T(8,128)} %bitcast.39, bf16[1024,1024]{1,0:T(8,128)(2,1)} %tok_hbm.1, bf16[1024,512]{1,0:T(8,128)(2,1)} %w_one.3, bf16[512,256]{1,0:T(8,128)(2,1)} %w_two.3), custom_call_target="tpu_custom_call" | custom-call | tf_op jit(solution)/shard_map/prepare/pallas_call | solution.py:474
  18.0 0.0 copy-done.1
  18.0 1.4 fusion.2.ids_s
  19.4 22.4 %pick_rows.1 = (bf16[4096,256]{1,0:T(8,128)(2,1)}, bf16[8192,256]{1,0:T(8,128)(2,1)}) custom-call(s32[12288]{0:T(1024)} %fusion.2.ids_s, bf16[32768,256]{1,0:T(8,128)(2,1)} %table.1), custom_call_target="tpu_custom_call" | custom-call | tf_op jit(solution)/shard_map/pick_rows/pallas_call | solution.py:93
  41.9 55.6 %score.1 = (bf16[512,256]{1,0:T(8,128)(2,1)}, bf16[1024,256]{1,0:T(8,128)(2,1)}, f32[8,128]{1,0:T(8,128)}, bf16[1024,256]{1,0:T(8,128)(2,1)}, bf16[1024,256]{1,0:T(8,128)(2,1)}, /*index=5*/f32[4096,256]{1,0:T(8,128)}) custom-call(bf16[2,2,2,512,256]{4,3,2,1,0:T(8,128)(2,1)} %bitcast.28, bf16[2,2,2,1024,256]{4,3,2,1,0:T(8,128)(2,1)} %bitcast.27, ...), custom_call_target="tpu_custom_call" | custom-call | tf_op jit(solution)/shard_map/score/pallas_call | solution.py:567
  97.5 0.0 copy-start.2
  97.5 0.0 copy-start.3
  97.5 71.9 %back_rows.1 = (bf16[2,2,2,1024,256]{4,3,2,1,0:T(8,128)(2,1)}, bf16[2,2,2,512,256]{4,3,2,1,0:T(8,128)(2,1)}, f32[128,512]{1,0:T(8,128)}, f32[192,256]{1,0:T(8,128)}, f32[8,128]{1,0:T(8,128)}) custom-call(f32[2,2,2,512,256]{4,3,2,1,0:T(8,128)} %bitcast.26, bf16[1024,1024]{1,0:T(8,128)(2,1)} %tok_hbm.1, f32[8,128]{1,0:T(8,128)} %get-tuple-element.26.loss_in, ...), custom_call_target="tpu_custom_call" | custom-call | tf_op jit(solution)/shard_map/back_rows/pallas_call | solution.py:666
  169.4 0.0 all-gather.6.cloned.1.call-update
  169.4 0.0 all-gather.4.cloned.1.call-start
  169.5 0.7 all-gather.4.cloned.1.call-update
  170.2 0.0 copy-done.2
  170.2 0.0 copy-done.3
  170.2 0.7 fusion.6.ids_v
  170.8 1.2 slice.15
  172.7 47.8 %scatter_rows.1 = f32[32768,256]{1,0:T(8,128)} custom-call(s32[12288]{0:T(1024)} %fusion.2.ids_s, s32[96,128]{1,0:T(8,128)} %fusion.6.ids_v, bf16[4096,256]{1,0:T(8,128)(2,1)} %bitcast.42, bf16[8192,256]{1,0:T(8,128)(2,1)} %bitcast.41), custom_call_target="tpu_custom_call" | custom-call | flops 60000002048 | bytes 41943040 | tf_op jit(solution)/shard_map/scatter_rows/pallas_call | solution.py:179
  220.5 0.0 all-gather.6.cloned.1.call-done
  220.6 0.0 copy-start
  220.6 1.2 fusion.12
  221.8 0.9 pad_maximum_fusion
  222.6 0.0 copy-done
  222.6 1.1 fusion.11
  223.7 0.0 all-gather.4.cloned.1.call-done
  223.7 3.1 %copy.16 = f32[1024,512]{1,0:T(8,128)} copy(f32[1024,512]{1,0:T(8,128)} %all-gather.4.cloned.1.call-done) | data formatting | bytes 4194304
Async XLA Ops:
  7.2 10.9 %copy-start.1 = (s32[4096]{0:T(1024)S(1)}, s32[4096]{0:T(1024)}, u32[]{:S(2)}) copy-start(s32[4096]{0:T(1024)} %param.15) | copy-start | bytes 49156
  7.2 213.4 %all-gather.6.cloned.1.call-start = ((), (), s32[]{:S(2)}) async-start(), calls=%async_computation.1 | async-start | bytes 1769472 | tf_op jit(solution)/shard_map/all_gather | solution.py:702
  97.5 72.7 %copy-start.2 = (s32[4096]{0:T(1024)S(1)}, s32[4096]{0:T(1024)}, u32[]{:S(2)}) copy-start(s32[4096]{0:T(1024)} %param.15) | copy-start | bytes 49156
  97.5 72.7 %copy-start.3 = (s32[8,8,128]{2,1,0:T(8,128)S(1)}, s32[8,8,128]{2,1,0:T(8,128)}, u32[]{:S(2)}) copy-start(s32[8,8,128]{2,1,0:T(8,128)} %get-tuple-element.21) | copy-start | bytes 98308
  169.4 54.3 %all-gather.4.cloned.1.call-start = ((), (), s32[]{:S(2)}) async-start(), calls=%async_computation | async-start | bytes 2359296 | tf_op jit(solution)/shard_map/all_gather | solution.py:701
  220.6 2.1 copy-start
Sparse Core Ops, SparseCore 0:
  169.5 19.8 all-gather.5
  191.3 22.0 all-gather.3

commit v6 on v5

--- a/solution.py
+++ b/solution.py
@@ -40,7 +40,7 @@
 STAGE_ROWS = 2048
 OUT_ROWS = 1024
 IN_SLOTS = 12
-OUT_SLOTS = 12
+OUT_SLOTS = 8
 
 
 def pick_body(ids_s, table, cand_out, targ_out, wide, stage, rows_f, stage_sem):
@@ -106,29 +106,48 @@
     )(ids_two, table_loc)
 
 
-def scatter_body(ids_s, ids_v, cand_hbm, targ_hbm, out_ref, acc, g2, cand_ref, targ_ref, out_stage, sem, in_sem):
+def scatter_body(ids_s, ids_v, cand_hbm, targ_hbm, wa_hbm, wb_hbm, out_ref, dw_one, dw_two, dwi_one, dwi_two, acc, g2, cand_ref, targ_ref, wa, wb, flag_v, flag_s, out_stage, sem, in_sem, flag_sem, w_sem):
     rows, width = out_ref.shape
     lane = width // 2
     n_cand = cand_ref.shape[0]
     n_all = n_cand + targ_ref.shape[0]
-    in_copies = [pltpu.make_async_copy(cand_hbm, cand_ref, in_sem.at[0]), pltpu.make_async_copy(targ_hbm, targ_ref, in_sem.at[1])]
+    in_copies = [pltpu.make_async_copy(src, dst, in_sem.at[k]) for k, (src, dst) in enumerate([(cand_hbm, cand_ref), (targ_hbm, targ_ref), (wa_hbm, wa), (wb_hbm, wb)])]
     for copy in in_copies:
         copy.start()
+
+    ids = ids_v[...]
+    place = lax.broadcasted_iota(jnp.int32, ids.shape, 1) % GROUP
+    twice = jnp.zeros(ids.shape, jnp.int32)
+    for k in range(1, GROUP):
+        twice = jnp.where((ids == pltpu.roll(ids, k, 1)) & (place >= k), 1, twice)
+    flag_v[...] = jnp.broadcast_to(jnp.max(twice, axis=1, keepdims=True), ids.shape)
+    flag_copy = pltpu.make_async_copy(flag_v, flag_s, flag_sem)
+    flag_copy.start()
 
     @pl.loop(0, 2 * rows // 512)
     def _(i):
         acc[pl.ds(pl.multiple_of(i * 512, 512), 512), :] = jnp.zeros((512, lane), jnp.float32)
 
-    row_i = lax.broadcasted_iota(jnp.int32, (BATCH, BATCH), 0) // GROUP
-    col_i = lax.broadcasted_iota(jnp.int32, (BATCH, BATCH), 1) // GROUP
-    same_group = row_i == col_i
-
     def one_batch(b, src, src_base):
-        idr = jnp.broadcast_to(ids_v[pl.ds(b, 1), :], (BATCH, BATCH))
-        same = jnp.where((idr == idr.T) & same_group, 1.0, 0.0).astype(jnp.bfloat16)
-        part = jnp.dot(same, src[pl.ds(pl.multiple_of(b * BATCH - src_base, BATCH), BATCH), :], preferred_element_type=jnp.float32)
-        g2[pl.ds(0, BATCH, 2), :] = part[:, :lane]
-        g2[pl.ds(1, BATCH, 2), :] = part[:, lane:]
+        rows_b = pl.ds(pl.multiple_of(b * BATCH - src_base, BATCH), BATCH)
+        repeated = flag_s[b, 0]
+
+        @pl.when(repeated == 0)
+        def _():
+            part = src[rows_b, :].astype(jnp.float32)
+            g2[pl.ds(0, BATCH, 2), :] = part[:, :lane]
+            g2[pl.ds(1, BATCH, 2), :] = part[:, lane:]
+
+        @pl.when(repeated != 0)
+        def _():
+            row_i = lax.broadcasted_iota(jnp.int32, (BATCH, BATCH), 0) // GROUP
+            col_i = lax.broadcasted_iota(jnp.int32, (BATCH, BATCH), 1) // GROUP
+            idr = jnp.broadcast_to(ids_v[pl.ds(b, 1), :], (BATCH, BATCH))
+            same = jnp.where((idr == idr.T) & (row_i == col_i), 1.0, 0.0).astype(jnp.bfloat16)
+            part = jnp.dot(same, src[rows_b, :], preferred_element_type=jnp.float32)
+            g2[pl.ds(0, BATCH, 2), :] = part[:, :lane]
+            g2[pl.ds(1, BATCH, 2), :] = part[:, lane:]
+
         for g in range(BATCH // GROUP):
             at = [pl.multiple_of(ids_s[b * BATCH + g * GROUP + r], 2) for r in range(GROUP)]
             new = [acc[pl.ds(at[r], 2), :] + g2[pl.ds(2 * (g * GROUP + r), 2), :] for r in range(GROUP)]
@@ -137,6 +156,21 @@
 
     for copy in in_copies:
         copy.wait()
+    w_copies = []
+
+    def place_block(src, dst):
+        copy = pltpu.make_async_copy(src, dst, w_sem)
+        copy.start()
+        w_copies.append(copy)
+
+    for b in range(8):
+        place_block(wa.at[b, pl.ds(0, 128)], dw_one.at[pl.ds(b * 128, 128), pl.ds(0, width)])
+        place_block(wa.at[b, pl.ds(128, 128)], dw_one.at[pl.ds(b * 128, 128), pl.ds(width, width)])
+        place_block(wa.at[b, pl.ds(256, 64)], dw_two.at[pl.ds(b * 64, 64)])
+        place_block(wb.at[b, pl.ds(0, 32)], dwi_one.at[pl.ds(b * 32, 32), pl.ds(0, width)])
+        place_block(wb.at[b, pl.ds(32, 32)], dwi_one.at[pl.ds(b * 32, 32), pl.ds(width, width)])
+        place_block(wb.at[b, pl.ds(64, 64)], dwi_two.at[pl.ds(b * 64, 64)])
+    flag_copy.wait()
 
     @pl.loop(0, n_cand // BATCH)
     def _(b):
@@ -170,30 +204,41 @@
 
     for i in range(n_out - OUT_SLOTS, n_out):
         out_copy(i, i % OUT_SLOTS).wait()
-
-
-def scatter_rows(ids_two, back_cand, back_targ, rows_loc):
+    for copy in w_copies:
+        copy.wait()
+
+
+def scatter_rows(ids_two, back_cand, back_targ, wa, wb, rows_loc, din):
     n_all = ids_two.shape[0]
     width = back_cand.shape[1]
+    n_batch = n_all // BATCH
     vmem = pl.BlockSpec(memory_space=pltpu.VMEM)
+    hbm = pl.BlockSpec(memory_space=pl.ANY)
+    shapes = [(rows_loc, width), (din, 2 * width), (2 * width, width), (width, 2 * width), (2 * width, width)]
     return pl.pallas_call(
         scatter_body,
-        out_shape=jax.ShapeDtypeStruct((rows_loc, width), jnp.float32),
-        in_specs=[pl.BlockSpec(memory_space=pltpu.SMEM), vmem, pl.BlockSpec(memory_space=pl.ANY), pl.BlockSpec(memory_space=pl.ANY)],
-        out_specs=pl.BlockSpec(memory_space=pl.ANY),
+        out_shape=tuple(jax.ShapeDtypeStruct(shape, jnp.float32) for shape in shapes),
+        in_specs=[pl.BlockSpec(memory_space=pltpu.SMEM), vmem] + [hbm] * 4,
+        out_specs=(hbm,) * 5,
         scratch_shapes=[
             pltpu.VMEM((2 * (rows_loc + SPARE), width // 2), jnp.float32),
             pltpu.VMEM((2 * BATCH, width // 2), jnp.float32),
             pltpu.VMEM(back_cand.shape, jnp.bfloat16),
             pltpu.VMEM(back_targ.shape, jnp.bfloat16),
+            pltpu.VMEM(wa.shape, jnp.float32),
+            pltpu.VMEM(wb.shape, jnp.float32),
+            pltpu.VMEM((n_batch, BATCH), jnp.int32),
+            pltpu.SMEM((n_batch, BATCH), jnp.int32),
             pltpu.VMEM((OUT_SLOTS, OUT_ROWS, width), jnp.float32),
             pltpu.SemaphoreType.DMA((OUT_SLOTS,)),
-            pltpu.SemaphoreType.DMA((2,)),
+            pltpu.SemaphoreType.DMA((4,)),
+            pltpu.SemaphoreType.DMA,
+            pltpu.SemaphoreType.DMA,
         ],
         compiler_params=pltpu.CompilerParams(vmem_limit_bytes=VMEM_LIMIT),
         cost_estimate=pl.CostEstimate(flops=60_000_000_000, bytes_accessed=40 << 20, transcendentals=0),
         name="scatter_rows",
-    )(ids_two, ids_two.reshape(n_all // BATCH, BATCH), back_cand, back_targ)
+    )(ids_two, ids_two.reshape(n_batch, BATCH), back_cand, back_targ, wa, wb)
 
 
 CHUNK = 512
@@ -575,14 +620,15 @@
     )(data_c, data_t, wi_one, wi_two, query, log_q.reshape(-1, 128), cand_ids.reshape(-1, 128), targ_loc.reshape(1, n_tok))
 
 
-W_ROWS = 448
-
-
-def back_body(part_hbm, tok_hbm, loss_in, d_query, d_targ, w_one, w_two, targ_raw, cand_raw, wi_one, wi_two, back_t, back_c, w_first, w_rest, loss_out, *scratch):
+WA_ROWS = 320
+WB_ROWS = 128
+
+
+def back_body(part_hbm, tok_hbm, loss_in, d_query, d_targ, w_one, w_two, targ_raw, cand_raw, wi_one, wi_two, back_t, back_c, wa_full, wb_full, loss_out, *scratch):
     place = my_place()
     me, y, x, c = place
-    rs_u, rs_w = scratch[0:10], scratch[10:20]
-    at_send, at_recv, ac_send, ac_recv, l_send, l_recv, w_data, l_all, d_part, tokens, in_sem = scratch[20:31]
+    rs_u, rs_a, rs_b = scratch[0:10], scratch[10:20], scratch[20:30]
+    at_send, at_recv, ac_send, ac_recv, aa_send, aa_recv, ab_send, ab_recv, l_send, l_recv, wa_data, wb_data, l_all, d_part, tokens, in_sem = scratch[30:46]
     width = d_query.shape[1]
     scale = SCORE_GAIN / math.sqrt(width)
     in_copies = [pltpu.make_async_copy(part_hbm, d_part, in_sem.at[0]), pltpu.make_async_copy(tok_hbm, tokens, in_sem.at[1])]
@@ -592,7 +638,10 @@
     red_u = []
     for k in range(2):
         red_u.append(Reduce(place, d_part.at[:, :, :, pl.ds(k * PIECE, PIECE)], *[r.at[k] for r in rs_u]))
-    red_w = Reduce(place, w_data, *[r.at[0] for r in rs_w])
+    red_a = Reduce(place, wa_data, *[r.at[0] for r in rs_a])
+    red_b = Reduce(place, wb_data, *[r.at[0] for r in rs_b])
+    ag_a = Gather(place, wa_full, aa_send, aa_recv)
+    ag_b = Gather(place, wb_full, ab_send, ab_recv)
     ag_t = Gather(place, back_t, at_send, at_recv)
     ag_c = Gather(place, back_c, ac_send, ac_recv)
     in_copies[0].wait()
@@ -603,10 +652,16 @@
     for k in range(1, 8):
         l_copies.append(push(loss_in, l_all.at[me], l_send.at[k], l_recv.at[k], peer_of(place, k // 4, (k // 2) % 2, k % 2)))
 
-    def put(first, value):
+    def put(data, first, value):
         n = value.shape[0] // 8
         for b in range(8):
-            w_data[b // 4, (b // 2) % 2, b % 2, first : first + n, :] = value[b * n : (b + 1) * n, :]
+            data[b // 4, (b // 2) % 2, b % 2, first : first + n, :] = value[b * n : (b + 1) * n, :]
+
+    def own(red, full):
+        first, second = red.last()
+        half = first.shape[0]
+        full[y, x, c, 0:half, :] = first
+        full[y, x, c, half : 2 * half, :] = second
 
     t_q, t_hid = tower_back(targ_raw[...], wi_one[...], wi_two[...], d_targ[...])
     red_u[0].two()
@@ -615,13 +670,15 @@
     ag_t.one()
     in_copies[1].wait()
     q_q, q_hid = tower_back(tokens[...], w_one[...], w_two[...], d_query[...])
+    dw_one = over_rows(tokens[...], q_q)
+    put(wa_data, 0, dw_one[:, :width])
+    put(wa_data, 128, dw_one[:, width:])
+    put(wa_data, 256, over_rows(q_hid, d_query[...]))
+    red_a.one()
     red_u[0].three()
     red_u[1].three()
+    red_a.two()
     ag_t.two()
-    dw_one = over_rows(tokens[...], q_q)
-    put(0, dw_one[:, :width])
-    put(128, dw_one[:, width:])
-    put(256, over_rows(q_hid, d_query[...]))
     parts = []
     for k in range(2):
         first, second = red_u[k].last()
@@ -631,26 +688,30 @@
     back_c[y, x, c] = by_transpose(c_q, wi_one[...]).astype(jnp.bfloat16)
     ag_c.one()
     dwi_one = over_rows(targ_raw[...], t_q) + over_rows(cand_raw[...], c_q)
-    put(320, dwi_one[:, :width])
-    put(352, dwi_one[:, width:])
-    put(384, over_rows(t_hid, d_targ[...]) + over_rows(c_hid, d_cand))
-    red_w.one()
+    put(wb_data, 0, dwi_one[:, :width])
+    put(wb_data, 32, dwi_one[:, width:])
+    put(wb_data, 64, over_rows(t_hid, d_targ[...]) + over_rows(c_hid, d_cand))
+    red_b.one()
+    red_a.three()
+    red_b.two()
+    ag_c.two()
+    own(red_a, wa_full)
+    ag_a.one()
+    red_b.three()
+    ag_t.three()
+    ag_a.two()
+    own(red_b, wb_full)
+    ag_b.one()
+    ag_c.three()
+    ag_b.two()
     for copy in l_copies:
         copy.wait()
     loss_out[...] = jnp.sum(l_all[...], axis=0)
-    ag_c.two()
-    red_w.two()
-    ag_t.three()
-    red_w.three()
-    ag_c.three()
-    first, second = red_w.last()
-    w_mine = jnp.concatenate([first, second], axis=0)
-    w_first[:, :width] = w_mine[0:128]
-    w_first[:, width:] = w_mine[128:256]
-    w_rest[...] = w_mine[256:W_ROWS]
-    ag_t.last()
-    ag_c.last()
-    for part in red_u + [red_w, ag_t, ag_c]:
+    ag_a.three()
+    ag_b.three()
+    for part in (ag_t, ag_c, ag_a, ag_b):
+        part.last()
+    for part in red_u + [red_a, red_b, ag_t, ag_c, ag_a, ag_b]:
         part.drain()
 
 
@@ -659,17 +720,18 @@
     n_tok = d_query.shape[0]
     vmem = pl.BlockSpec(memory_space=pltpu.VMEM)
     hbm = pl.BlockSpec(memory_space=pl.ANY)
-    scratch = reduce_scratch(2, PIECE, width, jnp.float32) + reduce_scratch(1, W_ROWS, width, jnp.float32) + gather_sems() + gather_sems()
+    scratch = reduce_scratch(2, PIECE, width, jnp.float32) + reduce_scratch(1, WA_ROWS, width, jnp.float32) + reduce_scratch(1, WB_ROWS, width, jnp.float32)
+    scratch += gather_sems() + gather_sems() + gather_sems() + gather_sems()
     scratch += [pltpu.SemaphoreType.DMA((8,)), pltpu.SemaphoreType.DMA((8,))]
-    scratch += [pltpu.VMEM((2, 2, 2, W_ROWS, width), jnp.float32), pltpu.VMEM((8, 8, 128), jnp.float32)]
+    scratch += [pltpu.VMEM((2, 2, 2, WA_ROWS, width), jnp.float32), pltpu.VMEM((2, 2, 2, WB_ROWS, width), jnp.float32), pltpu.VMEM((8, 8, 128), jnp.float32)]
     scratch += [pltpu.VMEM(d_part.shape, jnp.float32), pltpu.VMEM(tokens.shape, jnp.bfloat16), pltpu.SemaphoreType.DMA((2,))]
     return pl.pallas_call(
         back_body,
         out_shape=(
             jax.ShapeDtypeStruct((2, 2, 2, n_tok, width), jnp.bfloat16),
             jax.ShapeDtypeStruct((2, 2, 2, n_mine, width), jnp.bfloat16),
-            jax.ShapeDtypeStruct((128, 2 * width), jnp.float32),
-            jax.ShapeDtypeStruct((W_ROWS - 256, width), jnp.float32),
+            jax.ShapeDtypeStruct((2, 2, 2, WA_ROWS, width), jnp.float32),
+            jax.ShapeDtypeStruct((2, 2, 2, WB_ROWS, width), jnp.float32),
             jax.ShapeDtypeStruct((8, 128), jnp.float32),
         ),
         in_specs=[hbm, hbm] + [vmem] * 9,
@@ -697,13 +759,8 @@
         data_c = data_c.reshape(2, 2, 2, n_cand // 8, width)
         data_t = data_t.reshape(2, 2, 2, tokens.shape[0], width)
         cand_raw, targ_raw, loss_part, d_query, d_targ, d_part = score(tok_total, data_c, data_t, wi_one, wi_two, query, log_q, cand_ids, targ_loc)
-        back_t, back_c, w_first, w_rest, loss = back_rows(d_part.reshape(2, 2, 2, n_cand // 8, width), tokens, loss_part, d_query, d_targ, w_one, w_two, targ_raw, cand_raw, wi_one, wi_two)
-        dw_one = lax.all_gather(w_first, "dp", axis=0, tiled=True)
-        w_all = lax.all_gather(w_rest, "dp", axis=0)
-        d_table = scatter_rows(ids_two, back_c.reshape(-1, width), back_t.reshape(-1, width), rows_loc)
-        dw_two = w_all[:, 0:64].reshape(-1, width)
-        dwi_one = jnp.concatenate([w_all[:, 64:96].reshape(-1, width), w_all[:, 96:128].reshape(-1, width)], axis=1)
-        dwi_two = w_all[:, 128:192].reshape(-1, width)
+        back_t, back_c, wa, wb, loss = back_rows(d_part.reshape(2, 2, 2, n_cand // 8, width), tokens, loss_part, d_query, d_targ, w_one, w_two, targ_raw, cand_raw, wi_one, wi_two)
+        d_table, dw_one, dw_two, dwi_one, dwi_two = scatter_rows(ids_two, back_c.reshape(-1, width), back_t.reshape(-1, width), wa.reshape(8, WA_ROWS, width), wb.reshape(8, WB_ROWS, width), rows_loc, tokens.shape[1])
         return loss[0, 0] / tok_total, d_table, dw_one, dw_two, dwi_one, dwi_two
 
     return jax.shard_map(local_step, mesh=mesh, in_specs=(P("dp", None), P(), P(), P(), P(), P("dp", None), P(), P(), P("dp")), out_specs=(P(), P("dp", None), P(), P(), P(), P()), check_vma=False)

time: 235 us -> 221 us (0.940)
  between operations: 15.9 us -> 2.46 us
  local copies, waits for them, and re-layouts: 6.53 us -> 1.19 us
  Pallas kernels: 209 us -> 214 us
    pallas_call x1, Pallas kernels: 71.9 us -> 90.3 us  [back_rows(): pl.pallas_call(back_body, out_shape=(jax.ShapeDtypeStruct((2, 2, 2, n_tok...]
    pallas_call x1, Pallas kernels: 47.8 us -> 34.6 us  [scatter_rows(): pl.pallas_call(scatter_body, out_shape=tuple((jax.ShapeDtypeStruct(shape,...]
    unnamed x9 -> x0, local copies, waits for them, and re-layouts: 3.1 us -> none
  transfers between devices with their start and end apart: 2 -> 0, of which waited for: 0 -> 0; matrix products, arithmetic and copies ran while one was open for 2% -> 0% of each run, Pallas kernels for 20% -> 0%
where the time goes in v6:
time: 221 us; the launch traced here: 220 us
  Pallas kernels  214 us (97%)
  other arithmetic  2.82 us (1%)
  between operations  2.46 us (1%)
    pallas_call x1, Pallas kernels, back_rows(): pl.pallas_call(back_body, out_shape=(jax.ShapeDtypeStruct((2, 2, 2, n_tok...  90.3 us
    pallas_call x1, Pallas kernels, score(): pl.pallas_call(functools.partial(score_body, tok_total), out_shape=(rows[...  55.5 us
    pallas_call x1, Pallas kernels, scatter_rows(): pl.pallas_call(scatter_body, out_shape=tuple((jax.ShapeDtypeStruct(shape,...  34.6 us
    pallas_call x1, Pallas kernels, pick_rows(): pl.pallas_call(pick_body, out_shape=(jax.ShapeDtypeStruct((n_cand, width)...  22.4 us
    pallas_call x1, Pallas kernels, prepare(): pl.pallas_call(prepare_body, out_shape=(jax.ShapeDtypeStruct((8, 8, 128),...  10.8 us

profile of v6, /device:TPU:0, one launch (start us, length us, event | category | flops | bytes accessed | tf_op | source)
XLA Modules:
  0.0 220.0 jit_solution(8442088788519209604)
XLA Ops:
  0.6 10.8 %prepare.1 = (s32[8,8,128]{2,1,0:T(8,128)}, bf16[1024,256]{1,0:T(8,128)(2,1)}) custom-call(s32[8,128]{1,0:T(8,128)} %bitcast.30, bf16[1024,1024]{1,0:T(8,128)(2,1)} %tok_hbm.1, bf16[1024,512]{1,0:T(8,128)(2,1)} %w_one.3, bf16[512,256]{1,0:T(8,128)(2,1)} %w_two.3), custom_call_target="tpu_custom_call" | custom-call | tf_op jit(solution)/shard_map/prepare/pallas_call | solution.py:519
  11.4 1.4 fusion.2.ids_s
  12.8 1.4 fusion.6.ids_v
  14.2 22.4 %pick_rows.1 = (bf16[4096,256]{1,0:T(8,128)(2,1)}, bf16[8192,256]{1,0:T(8,128)(2,1)}) custom-call(s32[12288]{0:T(1024)} %fusion.2.ids_s, bf16[32768,256]{1,0:T(8,128)(2,1)} %table.1), custom_call_target="tpu_custom_call" | custom-call | tf_op jit(solution)/shard_map/pick_rows/pallas_call | solution.py:93
  36.6 55.5 %score.1 = (bf16[512,256]{1,0:T(8,128)(2,1)}, bf16[1024,256]{1,0:T(8,128)(2,1)}, f32[8,128]{1,0:T(8,128)}, bf16[1024,256]{1,0:T(8,128)(2,1)}, bf16[1024,256]{1,0:T(8,128)(2,1)}, /*index=5*/f32[4096,256]{1,0:T(8,128)}) custom-call(bf16[2,2,2,512,256]{4,3,2,1,0:T(8,128)(2,1)} %bitcast.25, bf16[2,2,2,1024,256]{4,3,2,1,0:T(8,128)(2,1)} %bitcast.24, ...), custom_call_target="tpu_custom_call" | custom-call | tf_op jit(solution)/shard_map/score/pallas_call | solution.py:612
  92.1 90.3 %back_rows.1 = (bf16[2,2,2,1024,256]{4,3,2,1,0:T(8,128)(2,1)}, bf16[2,2,2,512,256]{4,3,2,1,0:T(8,128)(2,1)}, f32[2,2,2,320,256]{4,3,2,1,0:T(8,128)}, f32[2,2,2,128,256]{4,3,2,1,0:T(8,128)}, f32[8,128]{1,0:T(8,128)}) custom-call(f32[2,2,2,512,256]{4,3,2,1,0:T(8,128)} %bitcast.23, bf16[1024,1024]{1,0:T(8,128)(2,1)} %tok_hbm.1, ...), custom_call_target="tpu_custom_call" | custom-call | tf_op jit(solution)/shard_map/back_rows/pallas_call | solution.py:728
  182.5 1.2 slice.3
  184.3 34.6 %scatter_rows.1 = (f32[32768,256]{1,0:T(8,128)}, f32[1024,512]{1,0:T(8,128)}, f32[512,256]{1,0:T(8,128)}, f32[256,512]{1,0:T(8,128)}, f32[512,256]{1,0:T(8,128)}) custom-call(s32[12288]{0:T(1024)} %fusion.2.ids_s, s32[96,128]{1,0:T(8,128)} %fusion.6.ids_v, bf16[4096,256]{1,0:T(8,128)(2,1)} %bitcast.34, bf16[8192,256]{1,0:T(8,128)(2,1)} %bitcast.32, ...), custom_call_target="tpu_custom_call" | custom-call | flops 60000002048 | bytes 41943040 | tf_op jit(solution)/shard_map/scatter_rows/pallas_call | solution.py:218

commit v7 on v6

--- a/solution.py
+++ b/solution.py
@@ -76,19 +76,19 @@
         @pl.loop(0, out.shape[0] // BATCH)
         def _(b):
             for r in range(BATCH):
-                at = pl.multiple_of(ids_s[first + b * BATCH + r], 2)
+                at = pl.multiple_of(ids_s[first + b, r], 2)
                 rows_f[pl.ds(2 * r, 2), :] = wide[pl.ds(at, 2), :]
             rows = pl.ds(pl.multiple_of(b * BATCH, BATCH), BATCH)
             out[rows, :lane] = rows_f[pl.ds(0, BATCH, 2), :].astype(jnp.bfloat16)
             out[rows, lane:] = rows_f[pl.ds(1, BATCH, 2), :].astype(jnp.bfloat16)
 
     fill(cand_out, 0)
-    fill(targ_out, cand_out.shape[0])
+    fill(targ_out, cand_out.shape[0] // BATCH)
 
 
 def pick_rows(ids_two, table_loc, n_cand):
     rows_loc, width = table_loc.shape
-    n_targ = ids_two.shape[0] - n_cand
+    n_targ = ids_two.size - n_cand
     vmem = pl.BlockSpec(memory_space=pltpu.VMEM)
     return pl.pallas_call(
         pick_body,
@@ -149,7 +149,7 @@
             g2[pl.ds(1, BATCH, 2), :] = part[:, lane:]
 
         for g in range(BATCH // GROUP):
-            at = [pl.multiple_of(ids_s[b * BATCH + g * GROUP + r], 2) for r in range(GROUP)]
+            at = [pl.multiple_of(ids_s[b, g * GROUP + r], 2) for r in range(GROUP)]
             new = [acc[pl.ds(at[r], 2), :] + g2[pl.ds(2 * (g * GROUP + r), 2), :] for r in range(GROUP)]
             for r in range(GROUP):
                 acc[pl.ds(at[r], 2), :] = new[r]
@@ -209,9 +209,8 @@
 
 
 def scatter_rows(ids_two, back_cand, back_targ, wa, wb, rows_loc, din):
-    n_all = ids_two.shape[0]
     width = back_cand.shape[1]
-    n_batch = n_all // BATCH
+    n_batch = ids_two.shape[0]
     vmem = pl.BlockSpec(memory_space=pltpu.VMEM)
     hbm = pl.BlockSpec(memory_space=pl.ANY)
     shapes = [(rows_loc, width), (din, 2 * width), (2 * width, width), (width, 2 * width), (2 * width, width)]
@@ -238,26 +237,24 @@
         compiler_params=pltpu.CompilerParams(vmem_limit_bytes=VMEM_LIMIT),
         cost_estimate=pl.CostEstimate(flops=60_000_000_000, bytes_accessed=40 << 20, transcendentals=0),
         name="scatter_rows",
-    )(ids_two, ids_two.reshape(n_batch, BATCH), back_cand, back_targ, wa, wb)
+    )(ids_two, ids_two, back_cand, back_targ, wa, wb)
 
 
 CHUNK = 512
-SUB = 64
+SUB = 128
 COLS = 256
 
 
-def logits_pass(u_ref, h, lq_ref, cid_ref, tid, z_a, z_b, e_s, m_s, s_s):
-    n_cand, width = u_ref.shape
-    n_tok = h.shape[0]
+def logits_pass(u_at, n_cand, h, lq_ref, cid_ref, tid, z_a, z_b, e_s, m_s, s_s, between):
+    n_tok, width = h.shape
     scale = SCORE_GAIN / math.sqrt(width)
     ht = h.T
     n_chunk = n_cand // CHUNK
 
     def multiply(i, z_ref):
-        off = pl.multiple_of(jnp.minimum(i, n_chunk - 1) * CHUNK, CHUNK)
-        z_ref[...] = jnp.dot(u_ref[pl.ds(off, CHUNK), :], ht, preferred_element_type=jnp.float32)
-
-    def absorb(i, z_ref, first):
+        z_ref[...] = jnp.dot(u_at(jnp.minimum(i, n_chunk - 1)), ht, preferred_element_type=jnp.float32)
+
+    def absorb(i, z_ref):
         off = pl.multiple_of(i * CHUNK, CHUNK)
         for col in range(0, n_tok, COLS):
             cols = slice(col, col + COLS)
@@ -282,16 +279,19 @@
     s_s[...] = jnp.zeros_like(s_s)
     multiply(0, z_a)
 
-    @pl.loop(0, n_chunk // 2)
-    def _(i):
+    def two_chunks(i):
         multiply(2 * i + 1, z_b)
-        absorb(2 * i, z_a, 0)
+        absorb(2 * i, z_a)
         multiply(2 * i + 2, z_a)
-        absorb(2 * i + 1, z_b, 0)
-
-
-def loss_pass(tok_total, u_ref, ut_s, h, v, e_s, m_s, s_s, fac_s, dz_a, dz_b, dht_s, loss_ref, dh_ref, dv_ref, du_ref):
-    n_cand, width = u_ref.shape
+        absorb(2 * i + 1, z_b)
+
+    pl.loop(0, n_chunk // 4)(two_chunks)
+    between()
+    pl.loop(n_chunk // 4, n_chunk // 2)(two_chunks)
+
+
+def loss_pass(tok_total, u_at, ut_s, h, v, e_s, m_s, s_s, fac_s, dz_a, dz_b, dht_s, loss_ref, dh_ref, dv_ref, du_ref, dz_ref):
+    n_cand, width = du_ref.shape
     n_tok = h.shape[0]
     scale = SCORE_GAIN / math.sqrt(width)
     n_chunk = n_cand // CHUNK
@@ -309,10 +309,12 @@
     inv = 1.0 / den / tok_total
     fac_s[0:8, :] = jnp.broadcast_to(m, (8, n_tok))
     fac_s[8:16, :] = jnp.broadcast_to(inv, (8, n_tok))
-    for i in range(n_cand // 512):
-        ut_s[:, i * 512 : (i + 1) * 512] = u_ref[i * 512 : (i + 1) * 512, :].T
-
-    def gradient(i, dz_ref):
+    for i in range(n_chunk):
+        ut_s[:, i * CHUNK : (i + 1) * CHUNK] = u_at(i).T
+    for i in range(8):
+        dz_ref[i : i + 1, :] = dzt[:, i * 128 : (i + 1) * 128]
+
+    def gradient(i, out):
         i = jnp.minimum(i, n_chunk - 1)
         off = pl.multiple_of(i * CHUNK, CHUNK)
         for col in range(0, n_tok, COLS):
@@ -320,12 +322,12 @@
             for k in range(CHUNK // SUB):
                 rows = pl.ds(pl.multiple_of(off + k * SUB, SUB), SUB)
                 fac = jnp.exp(m_s[1 + i * (CHUNK // SUB) + k, :, cols] - fac_s[0:8, cols]) * fac_s[8:16, cols]
-                dz_ref[k * SUB : (k + 1) * SUB, cols] = (e_s[rows, cols].reshape(SUB // 8, 8, COLS) * fac[None]).reshape(SUB, COLS).astype(jnp.bfloat16)
-
-    def spread(i, dz_ref):
+                out[k * SUB : (k + 1) * SUB, cols] = (e_s[rows, cols].reshape(SUB // 8, 8, COLS) * fac[None]).reshape(SUB, COLS).astype(jnp.bfloat16)
+
+    def spread(i, dz_c):
         off = pl.multiple_of(i * CHUNK, CHUNK)
-        du_ref[pl.ds(off, CHUNK), :] = jnp.dot(dz_ref[...], h, preferred_element_type=jnp.float32)
-        dht_s[...] += jnp.dot(ut_s[:, pl.ds(off, CHUNK)], dz_ref[...], preferred_element_type=jnp.float32)
+        du_ref[pl.ds(off, CHUNK), :] = jnp.dot(dz_c[...], h, preferred_element_type=jnp.float32)
+        dht_s[...] += jnp.dot(ut_s[:, pl.ds(off, CHUNK)], dz_c[...], preferred_element_type=jnp.float32)
 
     dht_s[...] = jnp.zeros_like(dht_s)
     gradient(0, dz_a)
@@ -497,45 +499,55 @@
     return [pltpu.SemaphoreType.DMA((5,)), pltpu.SemaphoreType.DMA((5,))]
 
 
-def prepare_body(mine, tokens, w_one, w_two, full, query, send_sem, recv_sem):
+def prepare_body(rows_loc, mine, cand_ids, tokens, w_one, w_two, ids_two, query, full, send_sem, recv_sem):
     place = my_place()
+    me = place[0]
     greet(place)
     for i in range(tokens.shape[0] // 256):
         at = slice(i * 256, i * 256 + 256)
         query[at, :] = tower_fwd(tokens[at, :], w_one[...], w_two[...])
     pl.semaphore_wait(pltpu.get_barrier_semaphore(), 7)
-    full[place[0]] = mine[...]
+    full[me] = mine[...]
     copies = []
     for k in range(1, 8):
-        copies.append(push(mine, full.at[place[0]], send_sem.at[k], recv_sem.at[k], peer_of(place, k // 4, (k // 2) % 2, k % 2)))
-
+        copies.append(push(mine, full.at[me], send_sem.at[k], recv_sem.at[k], peer_of(place, k // 4, (k // 2) % 2, k % 2)))
+
+    def owned(ids):
+        local = ids - me * rows_loc
+        spare = rows_loc + (lax.broadcasted_iota(jnp.int32, ids.shape, 0) % 2) * 128 + lax.broadcasted_iota(jnp.int32, ids.shape, 1)
+        return 2 * jnp.where((local >= 0) & (local < rows_loc), local, spare)
+
+    n_c = cand_ids.shape[0]
+    ids_two[0:n_c, :] = owned(cand_ids[...])
     for copy in copies:
         copy.wait()
-
-
-def prepare(targ_loc, tokens, w_one, w_two):
+    ids_two[n_c : n_c + 64, :] = owned(full[...].reshape(64, 128))
+
+
+def prepare(targ_loc, cand_ids, tokens, w_one, w_two, rows_loc):
     n_tok = tokens.shape[0]
+    n_c = cand_ids.shape[0] // 128
     vmem = pl.BlockSpec(memory_space=pltpu.VMEM)
     return pl.pallas_call(
-        prepare_body,
-        out_shape=(jax.ShapeDtypeStruct((8, 8, 128), jnp.int32), jax.ShapeDtypeStruct((n_tok, w_two.shape[1]), jnp.bfloat16)),
-        in_specs=[vmem] * 4,
+        functools.partial(prepare_body, rows_loc),
+        out_shape=(jax.ShapeDtypeStruct((n_c + 64, 128), jnp.int32), jax.ShapeDtypeStruct((n_tok, w_two.shape[1]), jnp.bfloat16)),
+        in_specs=[vmem] * 5,
         out_specs=(vmem,) * 2,
-        scratch_shapes=[pltpu.SemaphoreType.DMA((8,)), pltpu.SemaphoreType.DMA((8,))],
+        scratch_shapes=[pltpu.VMEM((8, 8, 128), jnp.int32), pltpu.SemaphoreType.DMA((8,)), pltpu.SemaphoreType.DMA((8,))],
         compiler_params=pltpu.CompilerParams(vmem_limit_bytes=VMEM_LIMIT, collective_id=0, has_side_effects=True),
         name="prepare",
-    )(targ_loc.reshape(8, 128), tokens, w_one, w_two)
+    )(targ_loc.reshape(8, 128), cand_ids.reshape(n_c, 128), tokens, w_one, w_two)
 
 
 PIECE = 256
 
 
-def score_body(tok_total, c_hbm, t_hbm, wi_one, wi_two, h_ref, lq_ref, cid_ref, tid_ref, cand_raw, targ_raw, loss_ref, dh_ref, dv_ref, du_ref, *scratch):
+def score_body(tok_total, c_hbm, t_hbm, wi_one, wi_two, h_ref, lq_ref, cid_ref, tid_ref, cand_raw, targ_raw, loss_ref, dh_ref, dv_ref, du_ref, dz_ref, h_part, *scratch):
     place = my_place()
     me, y, x, c = place
     half = PIECE // 2
     data_c, data_t, in_sem, cand_vec, lq_b, cid_b, rs, ag_send, ag_recv = scratch[0:6] + (scratch[6:16],) + scratch[16:18]
-    z_a, z_b, e_s, m_s, s_s, ut_s, fac_s, dz_a, dz_b, dht_s, u_s = scratch[18:29]
+    z_a, z_b, e_s, m_s, s_s, ut_s, fac_s, dz_a, dz_b, dht_s, h_send, h_recv = scratch[18:30]
     n_cand, width = du_ref.shape
     in_copies = [pltpu.make_async_copy(c_hbm, data_c, in_sem.at[0]), pltpu.make_async_copy(t_hbm, data_t, in_sem.at[1])]
     for copy in in_copies:
@@ -546,6 +558,8 @@
         data = data_c.at[:, :, :, pl.ds(k * PIECE, PIECE)] if k < 2 else data_t.at[:, :, :, pl.ds((k - 2) * PIECE, PIECE)]
         reduces.append(Reduce(place, data, *[r.at[k] for r in rs]))
     ag = Gather(place, cand_vec, ag_send, ag_recv)
+    ag_h = Gather((me, y, x, 0), h_part, h_send, h_recv)
+    h_part[y, x, 0] = h_ref[...]
 
     def close(k, out, base):
         first, second = reduces[k].last()
@@ -579,23 +593,28 @@
     reduces[5].two()
     reduces[2].three()
     ag.two()
+    ag_h.one()
     reduces[3].three()
     reduces[4].three()
     ag.three()
     reduces[5].three()
     ag.last()
-    n_mine = n_cand // 8
-    for b in range(8):
-        u_s[b * n_mine : (b + 1) * n_mine, :] = cand_vec[b // 4, (b // 2) % 2, b % 2]
+
+    def u_at(i):
+        return cand_vec[i // 4, (i // 2) % 2, i % 2]
+
     h = h_ref[...]
-    logits_pass(u_s, h, lq_b, cid_b, tid_ref[...], z_a, z_b, e_s, m_s, s_s)
+    logits_pass(u_at, n_cand, h, lq_b, cid_b, tid_ref[...], z_a, z_b, e_s, m_s, s_s, ag_h.two)
     for k in range(4):
         close(k + 2, targ_raw, k * PIECE)
     v = tower_fwd(targ_raw[...], wi_one[...], wi_two[...])
-    loss_pass(tok_total, u_s, ut_s, h, v, e_s, m_s, s_s, fac_s, dz_a, dz_b, dht_s, loss_ref, dh_ref, dv_ref, du_ref)
+    loss_pass(tok_total, u_at, ut_s, h, v, e_s, m_s, s_s, fac_s, dz_a, dz_b, dht_s, loss_ref, dh_ref, dv_ref, du_ref, dz_ref)
+    ag_h.copies[2].wait_recv()
+    ag_h.copies[3].wait_recv()
     for red in reduces:
         red.drain()
     ag.drain()
+    ag_h.drain()
 
 
 def score(tok_total, data_c, data_t, wi_one, wi_two, query, log_q, cand_ids, targ_loc):
@@ -607,13 +626,13 @@
     scratch = [pltpu.VMEM(data_c.shape, jnp.bfloat16), pltpu.VMEM(data_t.shape, jnp.bfloat16), pltpu.SemaphoreType.DMA((2,))]
     scratch += [pltpu.VMEM(data_c.shape, jnp.bfloat16), pltpu.VMEM((n_cand, 128), jnp.float32), pltpu.VMEM((n_cand, 128), jnp.int32)]
     scratch += reduce_scratch(6, PIECE, width, jnp.bfloat16) + gather_sems() + softmax_scratch(n_cand, n_tok, width)
-    scratch += [pltpu.VMEM((n_cand, width), jnp.bfloat16)]
+    scratch += gather_sems()
     rows = [jax.ShapeDtypeStruct((n, width), jnp.bfloat16) for n in (n_mine, n_tok, n_tok, n_tok)]
     return pl.pallas_call(
         functools.partial(score_body, tok_total),
-        out_shape=(rows[0], rows[1], jax.ShapeDtypeStruct((8, 128), jnp.float32), rows[2], rows[3], jax.ShapeDtypeStruct((n_cand, width), jnp.float32)),
+        out_shape=(rows[0], rows[1], jax.ShapeDtypeStruct((8, 128), jnp.float32), rows[2], rows[3], jax.ShapeDtypeStruct((n_cand, width), jnp.float32), jax.ShapeDtypeStruct((8, 128), jnp.float32), jax.ShapeDtypeStruct((2, 2, 1, n_tok, width), jnp.bfloat16)),
         in_specs=[hbm, hbm] + [vmem] * 6,
-        out_specs=(vmem,) * 6,
+        out_specs=(vmem,) * 8,
         scratch_shapes=scratch,
         compiler_params=pltpu.CompilerParams(vmem_limit_bytes=VMEM_LIMIT, collective_id=1, has_side_effects=True),
         name="score",
@@ -624,14 +643,17 @@
 WB_ROWS = 128
 
 
-def back_body(part_hbm, tok_hbm, loss_in, d_query, d_targ, w_one, w_two, targ_raw, cand_raw, wi_one, wi_two, back_t, back_c, wa_full, wb_full, loss_out, *scratch):
+ROWS_BLK = 512
+
+
+def back_body(part_hbm, tok_hbm, raw_hbm, h_hbm, loss_in, dz_in, d_query, d_targ, w_one, w_two, targ_raw, cand_raw, wi_one, wi_two, rows_t, back_c, wa_full, wb_full, loss_out, *scratch):
     place = my_place()
     me, y, x, c = place
     rs_u, rs_a, rs_b = scratch[0:10], scratch[10:20], scratch[20:30]
-    at_send, at_recv, ac_send, ac_recv, aa_send, aa_recv, ab_send, ab_recv, l_send, l_recv, wa_data, wb_data, l_all, d_part, tokens, in_sem = scratch[30:46]
+    ac_send, ac_recv, aa_send, aa_recv, ab_send, ab_recv, l_send, l_recv, z_send, z_recv, h_sem, wa_data, wb_data, l_all, dz_all, d_part, tokens, raw_all, h_all, in_sem = scratch[30:50]
     width = d_query.shape[1]
     scale = SCORE_GAIN / math.sqrt(width)
-    in_copies = [pltpu.make_async_copy(part_hbm, d_part, in_sem.at[0]), pltpu.make_async_copy(tok_hbm, tokens, in_sem.at[1])]
+    in_copies = [pltpu.make_async_copy(src, dst, in_sem.at[k]) for k, (src, dst) in enumerate([(part_hbm, d_part), (h_hbm.at[:, :, 0], h_all.at[:, :, c]), (tok_hbm, tokens), (raw_hbm, raw_all)])]
     for copy in in_copies:
         copy.start()
     meet(place)
@@ -642,15 +664,37 @@
     red_b = Reduce(place, wb_data, *[r.at[0] for r in rs_b])
     ag_a = Gather(place, wa_full, aa_send, aa_recv)
     ag_b = Gather(place, wb_full, ab_send, ab_recv)
-    ag_t = Gather(place, back_t, at_send, at_recv)
     ag_c = Gather(place, back_c, ac_send, ac_recv)
     in_copies[0].wait()
     red_u[0].one()
     red_u[1].one()
     l_all[me] = loss_in[...]
+    dz_all[me] = dz_in[...]
     l_copies = []
     for k in range(1, 8):
-        l_copies.append(push(loss_in, l_all.at[me], l_send.at[k], l_recv.at[k], peer_of(place, k // 4, (k // 2) % 2, k % 2)))
+        peer = peer_of(place, k // 4, (k // 2) % 2, k % 2)
+        l_copies.append(push(loss_in, l_all.at[me], l_send.at[k], l_recv.at[k], peer))
+        l_copies.append(push(dz_in, dz_all.at[me], z_send.at[k], z_recv.at[k], peer))
+    in_copies[1].wait()
+    h_copy = push(h_all.at[:, :, c], h_all.at[:, :, c], h_sem.at[0], h_sem.at[1], peer_of(place, 0, 0, 1))
+
+    def rows_pass(first, last):
+        per = rows_t.shape[3] // ROWS_BLK
+
+        @pl.loop(first, last)
+        def _(i):
+            b = i // per
+            by, bx, bc = b // 4, (b // 2) % 2, b % 2
+            rows = pl.ds(pl.multiple_of((i % per) * ROWS_BLK, ROWS_BLK), ROWS_BLK)
+            columns = []
+            for k in range(ROWS_BLK // 128):
+                line = dz_all[b, pl.ds((i % per) * (ROWS_BLK // 128) + k, 1), :]
+                columns.append(jnp.broadcast_to(line, (128, 128)).T)
+            column = jnp.concatenate(columns, axis=0)
+            column = jnp.concatenate([column] * (width // 128), axis=1)
+            grad = (scale * column * h_all[by, bx, bc, rows, :].astype(jnp.float32)).astype(jnp.bfloat16)
+            q = tower_back(raw_all[by, bx, bc, rows, :], wi_one[...], wi_two[...], grad)[0]
+            rows_t[by, bx, bc, rows, :] = by_transpose(q, wi_one[...]).astype(jnp.bfloat16)
 
     def put(data, first, value):
         n = value.shape[0] // 8
@@ -666,9 +710,7 @@
     t_q, t_hid = tower_back(targ_raw[...], wi_one[...], wi_two[...], d_targ[...])
     red_u[0].two()
     red_u[1].two()
-    back_t[y, x, c] = by_transpose(t_q, wi_one[...]).astype(jnp.bfloat16)
-    ag_t.one()
-    in_copies[1].wait()
+    in_copies[2].wait()
     q_q, q_hid = tower_back(tokens[...], w_one[...], w_two[...], d_query[...])
     dw_one = over_rows(tokens[...], q_q)
     put(wa_data, 0, dw_one[:, :width])
@@ -678,7 +720,12 @@
     red_u[0].three()
     red_u[1].three()
     red_a.two()
-    ag_t.two()
+    in_copies[3].wait()
+    for copy in l_copies:
+        copy.wait()
+    h_copy.wait()
+    loss_out[...] = jnp.sum(l_all[...], axis=0)
+    rows_pass(0, 5)
     parts = []
     for k in range(2):
         first, second = red_u[k].last()
@@ -695,72 +742,67 @@
     red_a.three()
     red_b.two()
     ag_c.two()
+    rows_pass(5, 7)
     own(red_a, wa_full)
     ag_a.one()
     red_b.three()
-    ag_t.three()
+    rows_pass(7, 10)
     ag_a.two()
     own(red_b, wb_full)
     ag_b.one()
     ag_c.three()
+    rows_pass(10, 12)
     ag_b.two()
-    for copy in l_copies:
-        copy.wait()
-    loss_out[...] = jnp.sum(l_all[...], axis=0)
+    rows_pass(12, 16)
     ag_a.three()
     ag_b.three()
-    for part in (ag_t, ag_c, ag_a, ag_b):
+    for part in (ag_c, ag_a, ag_b):
         part.last()
-    for part in red_u + [red_a, red_b, ag_t, ag_c, ag_a, ag_b]:
+    for part in red_u + [red_a, red_b, ag_c, ag_a, ag_b]:
         part.drain()
 
 
-def back_rows(d_part, tokens, loss_part, d_query, d_targ, w_one, w_two, targ_raw, cand_raw, wi_one, wi_two):
+def back_rows(d_part, tokens, raw_all, h_part, loss_part, dz, d_query, d_targ, w_one, w_two, targ_raw, cand_raw, wi_one, wi_two):
     n_mine, width = d_part.shape[3:]
-    n_tok = d_query.shape[0]
     vmem = pl.BlockSpec(memory_space=pltpu.VMEM)
     hbm = pl.BlockSpec(memory_space=pl.ANY)
+    eight = pltpu.SemaphoreType.DMA((8,))
     scratch = reduce_scratch(2, PIECE, width, jnp.float32) + reduce_scratch(1, WA_ROWS, width, jnp.float32) + reduce_scratch(1, WB_ROWS, width, jnp.float32)
-    scratch += gather_sems() + gather_sems() + gather_sems() + gather_sems()
-    scratch += [pltpu.SemaphoreType.DMA((8,)), pltpu.SemaphoreType.DMA((8,))]
-    scratch += [pltpu.VMEM((2, 2, 2, WA_ROWS, width), jnp.float32), pltpu.VMEM((2, 2, 2, WB_ROWS, width), jnp.float32), pltpu.VMEM((8, 8, 128), jnp.float32)]
-    scratch += [pltpu.VMEM(d_part.shape, jnp.float32), pltpu.VMEM(tokens.shape, jnp.bfloat16), pltpu.SemaphoreType.DMA((2,))]
+    scratch += gather_sems() + gather_sems() + gather_sems() + [eight] * 4 + [pltpu.SemaphoreType.DMA((2,))]
+    scratch += [pltpu.VMEM((2, 2, 2, WA_ROWS, width), jnp.float32), pltpu.VMEM((2, 2, 2, WB_ROWS, width), jnp.float32), pltpu.VMEM((8, 8, 128), jnp.float32), pltpu.VMEM((8, 8, 128), jnp.float32)]
+    scratch += [pltpu.VMEM(d_part.shape, jnp.float32), pltpu.VMEM(tokens.shape, jnp.bfloat16), pltpu.VMEM(raw_all.shape, jnp.bfloat16), pltpu.VMEM(raw_all.shape, jnp.bfloat16), pltpu.SemaphoreType.DMA((4,))]
     return pl.pallas_call(
         back_body,
         out_shape=(
-            jax.ShapeDtypeStruct((2, 2, 2, n_tok, width), jnp.bfloat16),
+            jax.ShapeDtypeStruct(raw_all.shape, jnp.bfloat16),
             jax.ShapeDtypeStruct((2, 2, 2, n_mine, width), jnp.bfloat16),
             jax.ShapeDtypeStruct((2, 2, 2, WA_ROWS, width), jnp.float32),
             jax.ShapeDtypeStruct((2, 2, 2, WB_ROWS, width), jnp.float32),
             jax.ShapeDtypeStruct((8, 128), jnp.float32),
         ),
-        in_specs=[hbm, hbm] + [vmem] * 9,
+        in_specs=[hbm] * 4 + [vmem] * 10,
         out_specs=(vmem,) * 5,
         scratch_shapes=scratch,
         compiler_params=pltpu.CompilerParams(vmem_limit_bytes=VMEM_LIMIT, collective_id=2, has_side_effects=True),
         name="back_rows",
-    )(d_part, tokens, loss_part, d_query, d_targ, w_one, w_two, targ_raw, cand_raw, wi_one, wi_two)
+    )(d_part, tokens, raw_all, h_part, loss_part, dz, d_query, d_targ, w_one, w_two, targ_raw, cand_raw, wi_one, wi_two)
 
 
 def solution(mesh):
     num_dev = mesh.shape["dp"]
 
     def local_step(tokens, w_one, w_two, wi_one, wi_two, table_loc, cand_ids, log_q, targ_loc):
-        my_index = lax.axis_index("dp")
         rows_loc, width = table_loc.shape
         n_cand = cand_ids.shape[0]
-        tok_total = tokens.shape[0] * num_dev
-        targ_all, query = prepare(targ_loc, tokens, w_one, w_two)
-        targ_all = targ_all.reshape(-1)
-        local_ids = jnp.concatenate([cand_ids, targ_all]) - my_index * rows_loc
-        spare = rows_loc + jnp.arange(local_ids.shape[0], dtype=jnp.int32) % SPARE
-        ids_two = 2 * jnp.where((local_ids >= 0) & (local_ids < rows_loc), local_ids, spare)
+        n_tok = tokens.shape[0]
+        tok_total = n_tok * num_dev
+        ids_two, query = prepare(targ_loc, cand_ids, tokens, w_one, w_two, rows_loc)
         data_c, data_t = pick_rows(ids_two, table_loc, n_cand)
         data_c = data_c.reshape(2, 2, 2, n_cand // 8, width)
-        data_t = data_t.reshape(2, 2, 2, tokens.shape[0], width)
-        cand_raw, targ_raw, loss_part, d_query, d_targ, d_part = score(tok_total, data_c, data_t, wi_one, wi_two, query, log_q, cand_ids, targ_loc)
-        back_t, back_c, wa, wb, loss = back_rows(d_part.reshape(2, 2, 2, n_cand // 8, width), tokens, loss_part, d_query, d_targ, w_one, w_two, targ_raw, cand_raw, wi_one, wi_two)
-        d_table, dw_one, dw_two, dwi_one, dwi_two = scatter_rows(ids_two, back_c.reshape(-1, width), back_t.reshape(-1, width), wa.reshape(8, WA_ROWS, width), wb.reshape(8, WB_ROWS, width), rows_loc, tokens.shape[1])
+        data_t = data_t.reshape(2, 2, 2, n_tok, width)
+        cand_raw, targ_raw, loss_part, d_query, d_targ, d_part, dz, h_part = score(tok_total, data_c, data_t, wi_one, wi_two, query, log_q, cand_ids, targ_loc)
+        rows_t, back_c, wa, wb, loss = back_rows(d_part.reshape(2, 2, 2, n_cand // 8, width), tokens, data_t, h_part, loss_part, dz, d_query, d_targ, w_one, w_two, targ_raw, cand_raw, wi_one, wi_two)
+        d_table, dw_one, dw_two, dwi_one, dwi_two = scatter_rows(ids_two, back_c.reshape(-1, width), rows_t.reshape(-1, width), wa.reshape(8, WA_ROWS, width), wb.reshape(8, WB_ROWS, width), rows_loc, tokens.shape[1])
         return loss[0, 0] / tok_total, d_table, dw_one, dw_two, dwi_one, dwi_two
 
     return jax.shard_map(local_step, mesh=mesh, in_specs=(P("dp", None), P(), P(), P(), P(), P("dp", None), P(), P(), P("dp")), out_specs=(P(), P("dp", None), P(), P(), P(), P()), check_vma=False)

time: 221 us -> 207 us (0.937)
  Pallas kernels: 214 us -> 202 us
  other arithmetic: 2.82 us -> 0 us
    pallas_call x2, Pallas kernels: 101 us -> 84.4 us  [the longest x1 73.6 us: back_rows(): pl.pallas_call(back_body, out_shape=(jax.ShapeDtypeStruct(raw_all.shape,...]
    pallas_call x1, Pallas kernels: 55.5 us -> 60.8 us  [score(): pl.pallas_call(functools.partial(score_body, tok_total), out_shape=(rows[...]
    mul x2 -> x0, other arithmetic: 2.82 us -> none  [local_step(): 2 * jnp.where((local_ids >= 0) & (local_ids < rows_loc), local_ids, spare)]
where the time goes in v7:
time: 207 us; the launch traced here: 206 us
  Pallas kernels  202 us (98%)
  between operations  2.45 us (1%)
    pallas_call x1, Pallas kernels, back_rows(): pl.pallas_call(back_body, out_shape=(jax.ShapeDtypeStruct(raw_all.shape,...  73.6 us
    pallas_call x1, Pallas kernels, score(): pl.pallas_call(functools.partial(score_body, tok_total), out_shape=(rows[...  60.8 us
    pallas_call x1, Pallas kernels, scatter_rows(): pl.pallas_call(scatter_body, out_shape=tuple((jax.ShapeDtypeStruct(shape,...  34.5 us
    pallas_call x1, Pallas kernels, pick_rows(): pl.pallas_call(pick_body, out_shape=(jax.ShapeDtypeStruct((n_cand, width)...  22.6 us
    pallas_call x1, Pallas kernels, prepare(): pl.pallas_call(functools.partial(prepare_body, rows_loc), out_shape=(jax....  10.8 us

profile of v7, /device:TPU:0, one launch (start us, length us, event | category | flops | bytes accessed | tf_op | source)
XLA Modules:
  0.0 205.9 jit_solution(5056107517719850984)
XLA Ops:
  0.6 10.8 %prepare.1 = (s32[96,128]{1,0:T(8,128)}, bf16[1024,256]{1,0:T(8,128)(2,1)}) custom-call(s32[8,128]{1,0:T(8,128)} %bitcast.19, s32[32,128]{1,0:T(8,128)} %bitcast.16, bf16[1024,1024]{1,0:T(8,128)(2,1)} %tok_hbm.1, bf16[1024,512]{1,0:T(8,128)(2,1)} %w_one.3, bf16[512,256]{1,0:T(8,128)(2,1)} %w_two.3), custom_call_target="tpu_custom_call" | custom-call | tf_op jit(solution)/shard_map/prepare/pallas_call | solution.py:531
  11.5 22.6 %pick_rows.1 = (bf16[4096,256]{1,0:T(8,128)(2,1)}, bf16[8192,256]{1,0:T(8,128)(2,1)}) custom-call(s32[96,128]{1,0:T(8,128)} %get-tuple-element.28.ids_s.ids_v, bf16[32768,256]{1,0:T(8,128)(2,1)} %table.1), custom_call_target="tpu_custom_call" | custom-call | tf_op jit(solution)/shard_map/pick_rows/pallas_call | solution.py:93
  34.1 60.8 %score.1 = (bf16[512,256]{1,0:T(8,128)(2,1)}, bf16[1024,256]{1,0:T(8,128)(2,1)}, f32[8,128]{1,0:T(8,128)}, bf16[1024,256]{1,0:T(8,128)(2,1)}, bf16[1024,256]{1,0...) custom-call(bf16[2,2,2,512,256]{4,3,2,1,0:T(8,128)(2,1)} %bitcast.15, ...), custom_call_target="tpu_custom_call" | custom-call | tf_op jit(solution)/shard_map/score/pallas_call | solution.py:631
  94.9 73.6 %back_rows.1 = (bf16[2,2,2,1024,256]{4,3,2,1,0:T(8,128)(2,1)}, bf16[2,2,2,512,256]{4,3,2,1,0:T(8,128)(2,1)}, f32[2,2,2,320,256]{4,3,2,1,0:T(8,128)}, f32[2,2,2,128,256]{4,3,2,1,0:T(8,128)}, f32[8,128]{1,0:T(8,128)}) custom-call(f32[2,2,2,512,256]{4,3,2,1,0:T(8,128)} %bitcast.14, bf16[1024,1024]{1,0:T(8,128)(2,1)} %tok_hbm.1, ...), custom_call_target="tpu_custom_call" | custom-call | tf_op jit(solution)/shard_map/back_rows/pallas_call | solution.py:774
  168.4 1.2 slice.3
  170.3 34.5 %scatter_rows.1 = (f32[32768,256]{1,0:T(8,128)}, f32[1024,512]{1,0:T(8,128)}, f32[512,256]{1,0:T(8,128)}, f32[256,512]{1,0:T(8,128)}, f32[512,256]{1,0:T(8,128)}) custom-call(s32[96,128]{1,0:T(8,128)} %get-tuple-element.28.ids_s.ids_v, s32[96,128]{1,0:T(8,128)} %get-tuple-element.28.ids_s.ids_v, bf16[4096,256]{1,0:T(8,128)(2,1)} %bitcast.23, ...), custom_call_target="tpu_custom_call" | custom-call | flops 60000002048 | bytes 41943040 | tf_op jit(solution)/shard_map/scatter_rows/pallas_call | solution.py:217

commit v8 on v7

--- a/solution.py
+++ b/solution.py
@@ -43,7 +43,7 @@
 OUT_SLOTS = 8
 
 
-def pick_body(ids_s, table, cand_out, targ_out, wide, stage, rows_f, stage_sem):
+def pick_body(ids_s, table, cand_hbm, targ_hbm, wide, stage, rows_f, cand_out, targ_out, stage_sem, out_sem):
     rows_loc, width = table.shape
     lane = width // 2
     n_stage = rows_loc // STAGE_ROWS
@@ -72,44 +72,59 @@
             wide[pl.ds(base, 128, 2), :] = block[:, :lane]
             wide[pl.ds(base + 1, 128, 2), :] = block[:, lane:]
 
-    def fill(out, first):
-        @pl.loop(0, out.shape[0] // BATCH)
+    copies = []
+
+    def fill(out, hbm, first, count, ids_row):
+        @pl.loop(0, count // BATCH)
         def _(b):
             for r in range(BATCH):
-                at = pl.multiple_of(ids_s[first + b, r], 2)
+                at = pl.multiple_of(ids_s[ids_row + b, r], 2)
                 rows_f[pl.ds(2 * r, 2), :] = wide[pl.ds(at, 2), :]
-            rows = pl.ds(pl.multiple_of(b * BATCH, BATCH), BATCH)
+            rows = pl.ds(pl.multiple_of(first + b * BATCH, BATCH), BATCH)
             out[rows, :lane] = rows_f[pl.ds(0, BATCH, 2), :].astype(jnp.bfloat16)
             out[rows, lane:] = rows_f[pl.ds(1, BATCH, 2), :].astype(jnp.bfloat16)
 
-    fill(cand_out, 0)
-    fill(targ_out, cand_out.shape[0] // BATCH)
+        copy = pltpu.make_async_copy(out.at[pl.ds(first, count)], hbm.at[pl.ds(first, count)], out_sem.at[len(copies)])
+        copy.start()
+        copies.append(copy)
+
+    n_cand = cand_out.shape[0]
+    part = targ_out.shape[0] // 4
+    fill(cand_out, cand_hbm, 0, n_cand, 0)
+    for k in range(4):
+        fill(targ_out, targ_hbm, k * part, part, (n_cand + k * part) // BATCH)
+    for copy in copies:
+        copy.wait()
 
 
 def pick_rows(ids_two, table_loc, n_cand):
     rows_loc, width = table_loc.shape
     n_targ = ids_two.size - n_cand
-    vmem = pl.BlockSpec(memory_space=pltpu.VMEM)
+    hbm = pl.BlockSpec(memory_space=pl.ANY)
     return pl.pallas_call(
         pick_body,
         out_shape=(jax.ShapeDtypeStruct((n_cand, width), jnp.bfloat16), jax.ShapeDtypeStruct((n_targ, width), jnp.bfloat16)),
-        in_specs=[pl.BlockSpec(memory_space=pltpu.SMEM), pl.BlockSpec(memory_space=pl.ANY)],
-        out_specs=(vmem, vmem),
+        in_specs=[pl.BlockSpec(memory_space=pltpu.SMEM), hbm],
+        out_specs=(hbm, hbm),
         scratch_shapes=[
             pltpu.VMEM((2 * (rows_loc + SPARE), width // 2), jnp.float32),
             pltpu.VMEM((IN_SLOTS, STAGE_ROWS, width), jnp.bfloat16),
             pltpu.VMEM((2 * BATCH, width // 2), jnp.float32),
+            pltpu.VMEM((n_cand, width), jnp.bfloat16),
+            pltpu.VMEM((n_targ, width), jnp.bfloat16),
             pltpu.SemaphoreType.DMA((IN_SLOTS,)),
+            pltpu.SemaphoreType.DMA((5,)),
         ],
         compiler_params=pltpu.CompilerParams(vmem_limit_bytes=VMEM_LIMIT),
         name="pick_rows",
     )(ids_two, table_loc)
 
 
-def scatter_body(ids_s, ids_v, cand_hbm, targ_hbm, wa_hbm, wb_hbm, out_ref, dw_one, dw_two, dwi_one, dwi_two, acc, g2, cand_ref, targ_ref, wa, wb, flag_v, flag_s, out_stage, sem, in_sem, flag_sem, w_sem):
+def scatter_body(tok_total, ids_s, ids_v, loss_s, cand_hbm, targ_hbm, wa_hbm, wb_hbm, out_ref, dw_one, dw_two, dwi_one, dwi_two, loss_out, acc, g2, cand_ref, targ_ref, wa, wb, flag_v, flag_s, out_stage, sem, in_sem, flag_sem, w_sem):
     rows, width = out_ref.shape
     lane = width // 2
     n_cand = cand_ref.shape[0]
+    loss_out[0, 0] = loss_s[0, 0] * (1.0 / tok_total)
     n_all = n_cand + targ_ref.shape[0]
     in_copies = [pltpu.make_async_copy(src, dst, in_sem.at[k]) for k, (src, dst) in enumerate([(cand_hbm, cand_ref), (targ_hbm, targ_ref), (wa_hbm, wa), (wb_hbm, wb)])]
     for copy in in_copies:
@@ -208,17 +223,18 @@
         copy.wait()
 
 
-def scatter_rows(ids_two, back_cand, back_targ, wa, wb, rows_loc, din):
+def scatter_rows(tok_total, ids_two, loss, back_cand, back_targ, wa, wb, rows_loc, din):
     width = back_cand.shape[1]
     n_batch = ids_two.shape[0]
     vmem = pl.BlockSpec(memory_space=pltpu.VMEM)
     hbm = pl.BlockSpec(memory_space=pl.ANY)
-    shapes = [(rows_loc, width), (din, 2 * width), (2 * width, width), (width, 2 * width), (2 * width, width)]
+    smem = pl.BlockSpec(memory_space=pltpu.SMEM)
+    shapes = [(rows_loc, width), (din, 2 * width), (2 * width, width), (width, 2 * width), (2 * width, width), (1, 1)]
     return pl.pallas_call(
-        scatter_body,
+        functools.partial(scatter_body, tok_total),
         out_shape=tuple(jax.ShapeDtypeStruct(shape, jnp.float32) for shape in shapes),
-        in_specs=[pl.BlockSpec(memory_space=pltpu.SMEM), vmem] + [hbm] * 4,
-        out_specs=(hbm,) * 5,
+        in_specs=[smem, vmem, smem] + [hbm] * 4,
+        out_specs=(hbm,) * 5 + (smem,),
         scratch_shapes=[
             pltpu.VMEM((2 * (rows_loc + SPARE), width // 2), jnp.float32),
             pltpu.VMEM((2 * BATCH, width // 2), jnp.float32),
@@ -237,7 +253,7 @@
         compiler_params=pltpu.CompilerParams(vmem_limit_bytes=VMEM_LIMIT),
         cost_estimate=pl.CostEstimate(flops=60_000_000_000, bytes_accessed=40 << 20, transcendentals=0),
         name="scatter_rows",
-    )(ids_two, ids_two, back_cand, back_targ, wa, wb)
+    )(ids_two, ids_two, loss, back_cand, back_targ, wa, wb)
 
 
 CHUNK = 512
@@ -503,9 +519,8 @@
     place = my_place()
     me = place[0]
     greet(place)
-    for i in range(tokens.shape[0] // 256):
-        at = slice(i * 256, i * 256 + 256)
-        query[at, :] = tower_fwd(tokens[at, :], w_one[...], w_two[...])
+    half = tokens.shape[0] // 2
+    query[0:half, :] = tower_fwd(tokens[0:half, :], w_one[...], w_two[...])
     pl.semaphore_wait(pltpu.get_barrier_semaphore(), 7)
     full[me] = mine[...]
     copies = []
@@ -519,6 +534,7 @@
 
     n_c = cand_ids.shape[0]
     ids_two[0:n_c, :] = owned(cand_ids[...])
+    query[half : 2 * half, :] = tower_fwd(tokens[half : 2 * half, :], w_one[...], w_two[...])
     for copy in copies:
         copy.wait()
     ids_two[n_c : n_c + 64, :] = owned(full[...].reshape(64, 128))
@@ -646,11 +662,11 @@
 ROWS_BLK = 512
 
 
-def back_body(part_hbm, tok_hbm, raw_hbm, h_hbm, loss_in, dz_in, d_query, d_targ, w_one, w_two, targ_raw, cand_raw, wi_one, wi_two, rows_t, back_c, wa_full, wb_full, loss_out, *scratch):
+def back_body(part_hbm, tok_hbm, raw_hbm, h_hbm, loss_in, dz_in, d_query, d_targ, w_one, w_two, targ_raw, cand_raw, wi_one, wi_two, rows_out, cand_out, wa_out, wb_out, loss_out, *scratch):
     place = my_place()
     me, y, x, c = place
     rs_u, rs_a, rs_b = scratch[0:10], scratch[10:20], scratch[20:30]
-    ac_send, ac_recv, aa_send, aa_recv, ab_send, ab_recv, l_send, l_recv, z_send, z_recv, h_sem, wa_data, wb_data, l_all, dz_all, d_part, tokens, raw_all, h_all, in_sem = scratch[30:50]
+    ac_send, ac_recv, aa_send, aa_recv, ab_send, ab_recv, l_send, l_recv, z_send, z_recv, h_sem, wa_data, wb_data, l_all, dz_all, d_part, tokens, raw_all, h_all, in_sem, rows_t, back_c, wa_full, wb_full, rows_sem, out_sem = scratch[30:56]
     width = d_query.shape[1]
     scale = SCORE_GAIN / math.sqrt(width)
     in_copies = [pltpu.make_async_copy(src, dst, in_sem.at[k]) for k, (src, dst) in enumerate([(part_hbm, d_part), (h_hbm.at[:, :, 0], h_all.at[:, :, c]), (tok_hbm, tokens), (raw_hbm, raw_all)])]
@@ -678,8 +694,14 @@
     in_copies[1].wait()
     h_copy = push(h_all.at[:, :, c], h_all.at[:, :, c], h_sem.at[0], h_sem.at[1], peer_of(place, 0, 0, 1))
 
+    per = rows_t.shape[3] // ROWS_BLK
+
+    def rows_copy(i):
+        b = i // per
+        here = (b // 4, (b // 2) % 2, b % 2, pl.ds(pl.multiple_of((i % per) * ROWS_BLK, ROWS_BLK), ROWS_BLK))
+        return pltpu.make_async_copy(rows_t.at[here], rows_out.at[here], rows_sem.at[i])
+
     def rows_pass(first, last):
-        per = rows_t.shape[3] // ROWS_BLK
 
         @pl.loop(first, last)
         def _(i):
@@ -695,6 +717,7 @@
             grad = (scale * column * h_all[by, bx, bc, rows, :].astype(jnp.float32)).astype(jnp.bfloat16)
             q = tower_back(raw_all[by, bx, bc, rows, :], wi_one[...], wi_two[...], grad)[0]
             rows_t[by, bx, bc, rows, :] = by_transpose(q, wi_one[...]).astype(jnp.bfloat16)
+            rows_copy(i).start()
 
     def put(data, first, value):
         n = value.shape[0] // 8
@@ -717,15 +740,16 @@
     put(wa_data, 128, dw_one[:, width:])
     put(wa_data, 256, over_rows(q_hid, d_query[...]))
     red_a.one()
-    red_u[0].three()
-    red_u[1].three()
-    red_a.two()
     in_copies[3].wait()
     for copy in l_copies:
         copy.wait()
     h_copy.wait()
     loss_out[...] = jnp.sum(l_all[...], axis=0)
-    rows_pass(0, 5)
+    rows_pass(0, 3)
+    red_u[0].three()
+    red_u[1].three()
+    red_a.two()
+    rows_pass(3, 6)
     parts = []
     for k in range(2):
         first, second = red_u[k].last()
@@ -742,24 +766,34 @@
     red_a.three()
     red_b.two()
     ag_c.two()
-    rows_pass(5, 7)
+    rows_pass(6, 8)
     own(red_a, wa_full)
     ag_a.one()
     red_b.three()
-    rows_pass(7, 10)
+    rows_pass(8, 13)
     ag_a.two()
     own(red_b, wb_full)
     ag_b.one()
     ag_c.three()
-    rows_pass(10, 12)
+    rows_pass(13, 16)
     ag_b.two()
-    rows_pass(12, 16)
+    ag_c.last()
+    out_copies = [pltpu.make_async_copy(back_c, cand_out, out_sem.at[0])]
+    out_copies[0].start()
     ag_a.three()
     ag_b.three()
-    for part in (ag_c, ag_a, ag_b):
-        part.last()
+    ag_a.last()
+    out_copies.append(pltpu.make_async_copy(wa_full, wa_out, out_sem.at[1]))
+    out_copies[1].start()
+    ag_b.last()
+    out_copies.append(pltpu.make_async_copy(wb_full, wb_out, out_sem.at[2]))
+    out_copies[2].start()
     for part in red_u + [red_a, red_b, ag_c, ag_a, ag_b]:
         part.drain()
+    for i in range(rows_sem.shape[0]):
+        rows_copy(i).wait()
+    for copy in out_copies:
+        copy.wait()
 
 
 def back_rows(d_part, tokens, raw_all, h_part, loss_part, dz, d_query, d_targ, w_one, w_two, targ_raw, cand_raw, wi_one, wi_two):
@@ -771,6 +805,8 @@
     scratch += gather_sems() + gather_sems() + gather_sems() + [eight] * 4 + [pltpu.SemaphoreType.DMA((2,))]
     scratch += [pltpu.VMEM((2, 2, 2, WA_ROWS, width), jnp.float32), pltpu.VMEM((2, 2, 2, WB_ROWS, width), jnp.float32), pltpu.VMEM((8, 8, 128), jnp.float32), pltpu.VMEM((8, 8, 128), jnp.float32)]
     scratch += [pltpu.VMEM(d_part.shape, jnp.float32), pltpu.VMEM(tokens.shape, jnp.bfloat16), pltpu.VMEM(raw_all.shape, jnp.bfloat16), pltpu.VMEM(raw_all.shape, jnp.bfloat16), pltpu.SemaphoreType.DMA((4,))]
+    scratch += [pltpu.VMEM(raw_all.shape, jnp.bfloat16), pltpu.VMEM((2, 2, 2, n_mine, width), jnp.bfloat16), pltpu.VMEM((2, 2, 2, WA_ROWS, width), jnp.float32), pltpu.VMEM((2, 2, 2, WB_ROWS, width), jnp.float32)]
+    scratch += [pltpu.SemaphoreType.DMA((8 * raw_all.shape[3] // ROWS_BLK,)), pltpu.SemaphoreType.DMA((3,))]
     return pl.pallas_call(
         back_body,
         out_shape=(
@@ -781,7 +817,7 @@
             jax.ShapeDtypeStruct((8, 128), jnp.float32),
         ),
         in_specs=[hbm] * 4 + [vmem] * 10,
-        out_specs=(vmem,) * 5,
+        out_specs=(hbm,) * 4 + (vmem,),
         scratch_shapes=scratch,
         compiler_params=pltpu.CompilerParams(vmem_limit_bytes=VMEM_LIMIT, collective_id=2, has_side_effects=True),
         name="back_rows",
@@ -802,7 +838,7 @@
         data_t = data_t.reshape(2, 2, 2, n_tok, width)
         cand_raw, targ_raw, loss_part, d_query, d_targ, d_part, dz, h_part = score(tok_total, data_c, data_t, wi_one, wi_two, query, log_q, cand_ids, targ_loc)
         rows_t, back_c, wa, wb, loss = back_rows(d_part.reshape(2, 2, 2, n_cand // 8, width), tokens, data_t, h_part, loss_part, dz, d_query, d_targ, w_one, w_two, targ_raw, cand_raw, wi_one, wi_two)
-        d_table, dw_one, dw_two, dwi_one, dwi_two = scatter_rows(ids_two, back_c.reshape(-1, width), rows_t.reshape(-1, width), wa.reshape(8, WA_ROWS, width), wb.reshape(8, WB_ROWS, width), rows_loc, tokens.shape[1])
-        return loss[0, 0] / tok_total, d_table, dw_one, dw_two, dwi_one, dwi_two
+        d_table, dw_one, dw_two, dwi_one, dwi_two, loss = scatter_rows(tok_total, ids_two, loss, back_c.reshape(-1, width), rows_t.reshape(-1, width), wa.reshape(8, WA_ROWS, width), wb.reshape(8, WB_ROWS, width), rows_loc, tokens.shape[1])
+        return loss.reshape(()), d_table, dw_one, dw_two, dwi_one, dwi_two
 
     return jax.shard_map(local_step, mesh=mesh, in_specs=(P("dp", None), P(), P(), P(), P(), P("dp", None), P(), P(), P("dp")), out_specs=(P(), P("dp", None), P(), P(), P(), P()), check_vma=False)

time: 207 us -> 198 us (0.957)
  Pallas kernels: 202 us -> 196 us
    pallas_call x1, Pallas kernels: 73.6 us -> 68.8 us  [back_rows(): pl.pallas_call(back_body, out_shape=(jax.ShapeDtypeStruct(raw_all.shape,...]
where the time goes in v8:
time: 198 us; the launch traced here: 197 us
  Pallas kernels  196 us (99%)
    pallas_call x1, Pallas kernels, back_rows(): pl.pallas_call(back_body, out_shape=(jax.ShapeDtypeStruct(raw_all.shape,...  68.8 us
    pallas_call x1, Pallas kernels, score(): pl.pallas_call(functools.partial(score_body, tok_total), out_shape=(rows[...  61.1 us
    pallas_call x1, Pallas kernels, scatter_rows(): pl.pallas_call(functools.partial(scatter_body, tok_total), out_shape=tupl...  35.5 us
    pallas_call x1, Pallas kernels, pick_rows(): pl.pallas_call(pick_body, out_shape=(jax.ShapeDtypeStruct((n_cand, width)...  21 us
    pallas_call x1, Pallas kernels, prepare(): pl.pallas_call(functools.partial(prepare_body, rows_loc), out_shape=(jax....  10.1 us

profile of v8, /device:TPU:0, one launch (start us, length us, event | category | flops | bytes accessed | tf_op | source)
XLA Modules:
  0.0 197.3 jit_solution(2712994084087775810)
XLA Ops:
  0.6 10.1 %prepare.1 = (s32[96,128]{1,0:T(8,128)}, bf16[1024,256]{1,0:T(8,128)(2,1)}) custom-call(s32[8,128]{1,0:T(8,128)} %bitcast.19, s32[32,128]{1,0:T(8,128)} %bitcast.16, bf16[1024,1024]{1,0:T(8,128)(2,1)} %tok_hbm.1, bf16[1024,512]{1,0:T(8,128)(2,1)} %w_one.3, bf16[512,256]{1,0:T(8,128)(2,1)} %w_two.3), custom_call_target="tpu_custom_call" | custom-call | tf_op jit(solution)/shard_map/prepare/pallas_call | solution.py:547
  10.7 21.0 %pick_rows.1 = (bf16[4096,256]{1,0:T(8,128)(2,1)}, bf16[8192,256]{1,0:T(8,128)(2,1)}) custom-call(s32[96,128]{1,0:T(8,128)} %get-tuple-element.29.ids_s.ids_v, bf16[32768,256]{1,0:T(8,128)(2,1)} %table.1), custom_call_target="tpu_custom_call" | custom-call | tf_op jit(solution)/shard_map/pick_rows/pallas_call | solution.py:104
  31.7 61.1 %score.1 = (bf16[512,256]{1,0:T(8,128)(2,1)}, bf16[1024,256]{1,0:T(8,128)(2,1)}, f32[8,128]{1,0:T(8,128)}, bf16[1024,256]{1,0:T(8,128)(2,1)}, bf16[1024,256]{1,0...) custom-call(bf16[2,2,2,512,256]{4,3,2,1,0:T(8,128)(2,1)} %bitcast.15, ...), custom_call_target="tpu_custom_call" | custom-call | tf_op jit(solution)/shard_map/score/pallas_call | solution.py:647
  92.8 68.8 %back_rows.1 = (bf16[2,2,2,1024,256]{4,3,2,1,0:T(8,128)(2,1)}, bf16[2,2,2,512,256]{4,3,2,1,0:T(8,128)(2,1)}, f32[2,2,2,320,256]{4,3,2,1,0:T(8,128)}, f32[2,2,2,128,256]{4,3,2,1,0:T(8,128)}, f32[8,128]{1,0:T(8,128)}) custom-call(f32[2,2,2,512,256]{4,3,2,1,0:T(8,128)} %bitcast.14, bf16[1024,1024]{1,0:T(8,128)(2,1)} %tok_hbm.1, ...), custom_call_target="tpu_custom_call" | custom-call | tf_op jit(solution)/shard_map/back_rows/pallas_call | solution.py:810
  161.6 35.5 %scatter_rows.1 = (f32[32768,256]{1,0:T(8,128)}, f32[1024,512]{1,0:T(8,128)}, f32[512,256]{1,0:T(8,128)}, f32[256,512]{1,0:T(8,128)}, f32[512,256]{1,0:T(8,128)}, /*index=5*/f32[1,1]{1,0:T(1,128)}) custom-call(s32[96,128]{1,0:T(8,128)} %get-tuple-element.29.ids_s.ids_v, s32[96,128]{1,0:T(8,128)} %get-tuple-element.29.ids_s.ids_v, ...), custom_call_target="tpu_custom_call" | custom-call | flops 60000002048 | bytes 41943040 | tf_op jit(solution)/shard_map/scatter_rows/pallas_call | solution.py:233

commit v9 on v8

--- a/solution.py
+++ b/solution.py
@@ -261,7 +261,7 @@
 COLS = 256
 
 
-def logits_pass(u_at, n_cand, h, lq_ref, cid_ref, tid, z_a, z_b, e_s, m_s, s_s, between):
+def logits_pass(u_at, n_cand, h, lq_ref, cid_ref, tid, z_a, z_b, e_s, m_s, s_s):
     n_tok, width = h.shape
     scale = SCORE_GAIN / math.sqrt(width)
     ht = h.T
@@ -301,12 +301,10 @@
         multiply(2 * i + 2, z_a)
         absorb(2 * i + 1, z_b)
 
-    pl.loop(0, n_chunk // 4)(two_chunks)
-    between()
-    pl.loop(n_chunk // 4, n_chunk // 2)(two_chunks)
-
-
-def loss_pass(tok_total, u_at, ut_s, h, v, e_s, m_s, s_s, fac_s, dz_a, dz_b, dht_s, loss_ref, dh_ref, dv_ref, du_ref, dz_ref):
+    pl.loop(0, n_chunk // 2)(two_chunks)
+
+
+def loss_pass(tok_total, u_at, ut_s, h, v, e_s, m_s, s_s, fac_s, dz_a, dz_b, dht_s, loss_ref, dh_ref, dv_ref, du_ref, dz_ref, du_copy):
     n_cand, width = du_ref.shape
     n_tok = h.shape[0]
     scale = SCORE_GAIN / math.sqrt(width)
@@ -343,6 +341,7 @@
     def spread(i, dz_c):
         off = pl.multiple_of(i * CHUNK, CHUNK)
         du_ref[pl.ds(off, CHUNK), :] = jnp.dot(dz_c[...], h, preferred_element_type=jnp.float32)
+        du_copy(i).start()
         dht_s[...] += jnp.dot(ut_s[:, pl.ds(off, CHUNK)], dz_c[...], preferred_element_type=jnp.float32)
 
     dht_s[...] = jnp.zeros_like(dht_s)
@@ -558,24 +557,25 @@
 PIECE = 256
 
 
-def score_body(tok_total, c_hbm, t_hbm, wi_one, wi_two, h_ref, lq_ref, cid_ref, tid_ref, cand_raw, targ_raw, loss_ref, dh_ref, dv_ref, du_ref, dz_ref, h_part, *scratch):
+def score_body(tok_total, c_hbm, t_hbm, wi_one, wi_two, h_ref, lq_ref, cid_ref, tid_ref, cand_raw, targ_raw, loss_ref, dh_ref, dv_ref, du_hbm, dz_ref, h_part, *scratch):
     place = my_place()
     me, y, x, c = place
     half = PIECE // 2
     data_c, data_t, in_sem, cand_vec, lq_b, cid_b, rs, ag_send, ag_recv = scratch[0:6] + (scratch[6:16],) + scratch[16:18]
-    z_a, z_b, e_s, m_s, s_s, ut_s, fac_s, dz_a, dz_b, dht_s, h_send, h_recv = scratch[18:30]
+    z_a, z_b, e_s, m_s, s_s, ut_s, fac_s, dz_a, dz_b, dht_s, h_send, h_recv, du_ref, du_sem = scratch[18:32]
     n_cand, width = du_ref.shape
     in_copies = [pltpu.make_async_copy(c_hbm, data_c, in_sem.at[0]), pltpu.make_async_copy(t_hbm, data_t, in_sem.at[1])]
     for copy in in_copies:
         copy.start()
+    ag_h = Gather((me, y, x, 0), h_part, h_send, h_recv)
+    h_part[y, x, 0] = h_ref[...]
     meet(place)
+    ag_h.one()
     reduces = []
     for k in range(6):
         data = data_c.at[:, :, :, pl.ds(k * PIECE, PIECE)] if k < 2 else data_t.at[:, :, :, pl.ds((k - 2) * PIECE, PIECE)]
         reduces.append(Reduce(place, data, *[r.at[k] for r in rs]))
     ag = Gather(place, cand_vec, ag_send, ag_recv)
-    ag_h = Gather((me, y, x, 0), h_part, h_send, h_recv)
-    h_part[y, x, 0] = h_ref[...]
 
     def close(k, out, base):
         first, second = reduces[k].last()
@@ -609,22 +609,28 @@
     reduces[5].two()
     reduces[2].three()
     ag.two()
-    ag_h.one()
     reduces[3].three()
     reduces[4].three()
     ag.three()
     reduces[5].three()
+    ag_h.two()
     ag.last()
+
+    def du_copy(i):
+        rows = pl.ds(pl.multiple_of(i * CHUNK, CHUNK), CHUNK)
+        return pltpu.make_async_copy(du_ref.at[rows], du_hbm.at[rows], du_sem.at[i])
 
     def u_at(i):
         return cand_vec[i // 4, (i // 2) % 2, i % 2]
 
     h = h_ref[...]
-    logits_pass(u_at, n_cand, h, lq_b, cid_b, tid_ref[...], z_a, z_b, e_s, m_s, s_s, ag_h.two)
+    logits_pass(u_at, n_cand, h, lq_b, cid_b, tid_ref[...], z_a, z_b, e_s, m_s, s_s)
     for k in range(4):
         close(k + 2, targ_raw, k * PIECE)
     v = tower_fwd(targ_raw[...], wi_one[...], wi_two[...])
-    loss_pass(tok_total, u_at, ut_s, h, v, e_s, m_s, s_s, fac_s, dz_a, dz_b, dht_s, loss_ref, dh_ref, dv_ref, du_ref, dz_ref)
+    loss_pass(tok_total, u_at, ut_s, h, v, e_s, m_s, s_s, fac_s, dz_a, dz_b, dht_s, loss_ref, dh_ref, dv_ref, du_ref, dz_ref, du_copy)
+    for i in range(n_cand // CHUNK):
+        du_copy(i).wait()
     ag_h.copies[2].wait_recv()
     ag_h.copies[3].wait_recv()
     for red in reduces:
@@ -642,13 +648,13 @@
     scratch = [pltpu.VMEM(data_c.shape, jnp.bfloat16), pltpu.VMEM(data_t.shape, jnp.bfloat16), pltpu.SemaphoreType.DMA((2,))]
     scratch += [pltpu.VMEM(data_c.shape, jnp.bfloat16), pltpu.VMEM((n_cand, 128), jnp.float32), pltpu.VMEM((n_cand, 128), jnp.int32)]
     scratch += reduce_scratch(6, PIECE, width, jnp.bfloat16) + gather_sems() + softmax_scratch(n_cand, n_tok, width)
-    scratch += gather_sems()
+    scratch += gather_sems() + [pltpu.VMEM((n_cand, width), jnp.float32), pltpu.SemaphoreType.DMA((n_cand // CHUNK,))]
     rows = [jax.ShapeDtypeStruct((n, width), jnp.bfloat16) for n in (n_mine, n_tok, n_tok, n_tok)]
     return pl.pallas_call(
         functools.partial(score_body, tok_total),
         out_shape=(rows[0], rows[1], jax.ShapeDtypeStruct((8, 128), jnp.float32), rows[2], rows[3], jax.ShapeDtypeStruct((n_cand, width), jnp.float32), jax.ShapeDtypeStruct((8, 128), jnp.float32), jax.ShapeDtypeStruct((2, 2, 1, n_tok, width), jnp.bfloat16)),
         in_specs=[hbm, hbm] + [vmem] * 6,
-        out_specs=(vmem,) * 8,
+        out_specs=(vmem,) * 5 + (hbm,) + (vmem,) * 2,
         scratch_shapes=scratch,
         compiler_params=pltpu.CompilerParams(vmem_limit_bytes=VMEM_LIMIT, collective_id=1, has_side_effects=True),
         name="score",
@@ -662,17 +668,23 @@
 ROWS_BLK = 512
 
 
-def back_body(part_hbm, tok_hbm, raw_hbm, h_hbm, loss_in, dz_in, d_query, d_targ, w_one, w_two, targ_raw, cand_raw, wi_one, wi_two, rows_out, cand_out, wa_out, wb_out, loss_out, *scratch):
+def back_body(part_hbm, tok_hbm, raw_hbm, h_hbm, *rest):
+    operands, (loss_in, dz_in, rows_out, cand_out, wa_out, wb_out, loss_out), scratch = rest[0:8], rest[8:15], rest[15:]
     place = my_place()
     me, y, x, c = place
     rs_u, rs_a, rs_b = scratch[0:10], scratch[10:20], scratch[20:30]
     ac_send, ac_recv, aa_send, aa_recv, ab_send, ab_recv, l_send, l_recv, z_send, z_recv, h_sem, wa_data, wb_data, l_all, dz_all, d_part, tokens, raw_all, h_all, in_sem, rows_t, back_c, wa_full, wb_full, rows_sem, out_sem = scratch[30:56]
+    d_targ, targ_raw, wi_one, wi_two, d_query, w_one, w_two, cand_raw = scratch[56:64]
     width = d_query.shape[1]
     scale = SCORE_GAIN / math.sqrt(width)
-    in_copies = [pltpu.make_async_copy(src, dst, in_sem.at[k]) for k, (src, dst) in enumerate([(part_hbm, d_part), (h_hbm.at[:, :, 0], h_all.at[:, :, c]), (tok_hbm, tokens), (raw_hbm, raw_all)])]
-    for copy in in_copies:
+    pairs = [(part_hbm, d_part), (h_hbm.at[:, :, 0], h_all.at[:, :, c]), (tok_hbm, tokens), (raw_hbm, raw_all)] + list(zip(operands, scratch[56:64]))
+    in_copies = [pltpu.make_async_copy(src, dst, in_sem.at[k]) for k, (src, dst) in enumerate(pairs)]
+    in_copies[0].start()
+    for copy in in_copies[4:]:
         copy.start()
     meet(place)
+    for copy in in_copies[1:4]:
+        copy.start()
     red_u = []
     for k in range(2):
         red_u.append(Reduce(place, d_part.at[:, :, :, pl.ds(k * PIECE, PIECE)], *[r.at[k] for r in rs_u]))
@@ -730,6 +742,8 @@
         full[y, x, c, 0:half, :] = first
         full[y, x, c, half : 2 * half, :] = second
 
+    for copy in in_copies[4:]:
+        copy.wait()
     t_q, t_hid = tower_back(targ_raw[...], wi_one[...], wi_two[...], d_targ[...])
     red_u[0].two()
     red_u[1].two()
@@ -796,7 +810,7 @@
         copy.wait()
 
 
-def back_rows(d_part, tokens, raw_all, h_part, loss_part, dz, d_query, d_targ, w_one, w_two, targ_raw, cand_raw, wi_one, wi_two):
+def back_rows(d_part, tokens, raw_all, h_part, operands, loss_part, dz):
     n_mine, width = d_part.shape[3:]
     vmem = pl.BlockSpec(memory_space=pltpu.VMEM)
     hbm = pl.BlockSpec(memory_space=pl.ANY)
@@ -804,9 +818,10 @@
     scratch = reduce_scratch(2, PIECE, width, jnp.float32) + reduce_scratch(1, WA_ROWS, width, jnp.float32) + reduce_scratch(1, WB_ROWS, width, jnp.float32)
     scratch += gather_sems() + gather_sems() + gather_sems() + [eight] * 4 + [pltpu.SemaphoreType.DMA((2,))]
     scratch += [pltpu.VMEM((2, 2, 2, WA_ROWS, width), jnp.float32), pltpu.VMEM((2, 2, 2, WB_ROWS, width), jnp.float32), pltpu.VMEM((8, 8, 128), jnp.float32), pltpu.VMEM((8, 8, 128), jnp.float32)]
-    scratch += [pltpu.VMEM(d_part.shape, jnp.float32), pltpu.VMEM(tokens.shape, jnp.bfloat16), pltpu.VMEM(raw_all.shape, jnp.bfloat16), pltpu.VMEM(raw_all.shape, jnp.bfloat16), pltpu.SemaphoreType.DMA((4,))]
+    scratch += [pltpu.VMEM(d_part.shape, jnp.float32), pltpu.VMEM(tokens.shape, jnp.bfloat16), pltpu.VMEM(raw_all.shape, jnp.bfloat16), pltpu.VMEM(raw_all.shape, jnp.bfloat16), pltpu.SemaphoreType.DMA((4 + len(operands),))]
     scratch += [pltpu.VMEM(raw_all.shape, jnp.bfloat16), pltpu.VMEM((2, 2, 2, n_mine, width), jnp.bfloat16), pltpu.VMEM((2, 2, 2, WA_ROWS, width), jnp.float32), pltpu.VMEM((2, 2, 2, WB_ROWS, width), jnp.float32)]
     scratch += [pltpu.SemaphoreType.DMA((8 * raw_all.shape[3] // ROWS_BLK,)), pltpu.SemaphoreType.DMA((3,))]
+    scratch += [pltpu.VMEM(operand.shape, operand.dtype) for operand in operands]
     return pl.pallas_call(
         back_body,
         out_shape=(
@@ -816,12 +831,12 @@
             jax.ShapeDtypeStruct((2, 2, 2, WB_ROWS, width), jnp.float32),
             jax.ShapeDtypeStruct((8, 128), jnp.float32),
         ),
-        in_specs=[hbm] * 4 + [vmem] * 10,
+        in_specs=[hbm] * 12 + [vmem] * 2,
         out_specs=(hbm,) * 4 + (vmem,),
         scratch_shapes=scratch,
         compiler_params=pltpu.CompilerParams(vmem_limit_bytes=VMEM_LIMIT, collective_id=2, has_side_effects=True),
         name="back_rows",
-    )(d_part, tokens, raw_all, h_part, loss_part, dz, d_query, d_targ, w_one, w_two, targ_raw, cand_raw, wi_one, wi_two)
+    )(d_part, tokens, raw_all, h_part, *operands, loss_part, dz)
 
 
 def solution(mesh):
@@ -837,7 +852,7 @@
         data_c = data_c.reshape(2, 2, 2, n_cand // 8, width)
         data_t = data_t.reshape(2, 2, 2, n_tok, width)
         cand_raw, targ_raw, loss_part, d_query, d_targ, d_part, dz, h_part = score(tok_total, data_c, data_t, wi_one, wi_two, query, log_q, cand_ids, targ_loc)
-        rows_t, back_c, wa, wb, loss = back_rows(d_part.reshape(2, 2, 2, n_cand // 8, width), tokens, data_t, h_part, loss_part, dz, d_query, d_targ, w_one, w_two, targ_raw, cand_raw, wi_one, wi_two)
+        rows_t, back_c, wa, wb, loss = back_rows(d_part.reshape(2, 2, 2, n_cand // 8, width), tokens, data_t, h_part, (d_targ, targ_raw, wi_one, wi_two, d_query, w_one, w_two, cand_raw), loss_part, dz)
         d_table, dw_one, dw_two, dwi_one, dwi_two, loss = scatter_rows(tok_total, ids_two, loss, back_c.reshape(-1, width), rows_t.reshape(-1, width), wa.reshape(8, WA_ROWS, width), wb.reshape(8, WB_ROWS, width), rows_loc, tokens.shape[1])
         return loss.reshape(()), d_table, dw_one, dw_two, dwi_one, dwi_two
 

time: 198 us -> 198 us (level)
    pallas_call x1, Pallas kernels: 68.8 us -> 71.5 us  [back_rows(): pl.pallas_call(back_body, out_shape=(jax.ShapeDtypeStruct(raw_all.shape,...]
    pallas_call x1, Pallas kernels: 61.1 us -> 58.6 us  [score(): pl.pallas_call(functools.partial(score_body, tok_total), out_shape=(rows[...]
where the time goes in v9:
time: 198 us; the launch traced here: 197 us
  Pallas kernels  196 us (99%)
    pallas_call x1, Pallas kernels, back_rows(): pl.pallas_call(back_body, out_shape=(jax.ShapeDtypeStruct(raw_all.shape,...  71.5 us
    pallas_call x1, Pallas kernels, score(): pl.pallas_call(functools.partial(score_body, tok_total), out_shape=(rows[...  58.6 us
    pallas_call x1, Pallas kernels, scatter_rows(): pl.pallas_call(functools.partial(scatter_body, tok_total), out_shape=tupl...  35.3 us
    pallas_call x1, Pallas kernels, pick_rows(): pl.pallas_call(pick_body, out_shape=(jax.ShapeDtypeStruct((n_cand, width)...  21 us
    pallas_call x1, Pallas kernels, prepare(): pl.pallas_call(functools.partial(prepare_body, rows_loc), out_shape=(jax....  10.1 us

profile of v9, /device:TPU:0, one launch (start us, length us, event | category | flops | bytes accessed | tf_op | source)
XLA Modules:
  0.0 197.3 jit_solution(4684895062920539035)
XLA Ops:
  0.6 10.1 %prepare.1 = (s32[96,128]{1,0:T(8,128)}, bf16[1024,256]{1,0:T(8,128)(2,1)}) custom-call(s32[8,128]{1,0:T(8,128)} %bitcast.19, s32[32,128]{1,0:T(8,128)} %bitcast.16, bf16[1024,1024]{1,0:T(8,128)(2,1)} %tok_hbm.1, bf16[1024,512]{1,0:T(8,128)(2,1)} %rest_5_.1, bf16[512,256]{1,0:T(8,128)(2,1)} %rest_6_.1), custom_call_target="tpu_custom_call" | custom-call | tf_op jit(solution)/shard_map/prepare/pallas_call | solution.py:546
  10.7 21.0 %pick_rows.1 = (bf16[4096,256]{1,0:T(8,128)(2,1)}, bf16[8192,256]{1,0:T(8,128)(2,1)}) custom-call(s32[96,128]{1,0:T(8,128)} %get-tuple-element.29.ids_s.ids_v, bf16[32768,256]{1,0:T(8,128)(2,1)} %table.1), custom_call_target="tpu_custom_call" | custom-call | tf_op jit(solution)/shard_map/pick_rows/pallas_call | solution.py:104
  31.7 58.6 %score.1 = (bf16[512,256]{1,0:T(8,128)(2,1)}, bf16[1024,256]{1,0:T(8,128)(2,1)}, f32[8,128]{1,0:T(8,128)}, bf16[1024,256]{1,0:T(8,128)(2,1)}, bf16[1024,256]{1,0...) custom-call(bf16[2,2,2,512,256]{4,3,2,1,0:T(8,128)(2,1)} %bitcast.15, ...), custom_call_target="tpu_custom_call" | custom-call | tf_op jit(solution)/shard_map/score/pallas_call | solution.py:653
  90.4 71.5 %back_rows.1 = (bf16[2,2,2,1024,256]{4,3,2,1,0:T(8,128)(2,1)}, bf16[2,2,2,512,256]{4,3,2,1,0:T(8,128)(2,1)}, f32[2,2,2,320,256]{4,3,2,1,0:T(8,128)}, f32[2,2,2,128,256]{4,3,2,1,0:T(8,128)}, f32[8,128]{1,0:T(8,128)}) custom-call(f32[2,2,2,512,256]{4,3,2,1,0:T(8,128)} %bitcast.14, bf16[1024,1024]{1,0:T(8,128)(2,1)} %tok_hbm.1, ...), custom_call_target="tpu_custom_call" | custom-call | tf_op jit(solution)/shard_map/back_rows/pallas_call | solution.py:825
  161.8 35.3 %scatter_rows.1 = (f32[32768,256]{1,0:T(8,128)}, f32[1024,512]{1,0:T(8,128)}, f32[512,256]{1,0:T(8,128)}, f32[256,512]{1,0:T(8,128)}, f32[512,256]{1,0:T(8,128)}, /*index=5*/f32[1,1]{1,0:T(1,128)}) custom-call(s32[96,128]{1,0:T(8,128)} %get-tuple-element.29.ids_s.ids_v, s32[96,128]{1,0:T(8,128)} %get-tuple-element.29.ids_s.ids_v, ...), custom_call_target="tpu_custom_call" | custom-call | flops 60000002048 | bytes 41943040 | tf_op jit(solution)/shard_map/scatter_rows/pallas_call | solution.py:233

commit v10 on v9

--- a/solution.py
+++ b/solution.py
@@ -606,9 +606,9 @@
     cand_vec[y, x, c] = tower_fwd(cand_raw[...], wi_one[...], wi_two[...])
     ag.one()
     reduces[4].two()
+    ag.two()
     reduces[5].two()
     reduces[2].three()
-    ag.two()
     reduces[3].three()
     reduces[4].three()
     ag.three()

time: 198 us -> 194 us (0.980)
  Pallas kernels: 196 us -> 192 us
    pallas_call x1, Pallas kernels: 71.5 us -> 67.5 us  [back_rows(): pl.pallas_call(back_body, out_shape=(jax.ShapeDtypeStruct(raw_all.shape,...]
where the time goes in v10:
time: 194 us; the launch traced here: 193 us
  Pallas kernels  192 us (99%)
    pallas_call x1, Pallas kernels, back_rows(): pl.pallas_call(back_body, out_shape=(jax.ShapeDtypeStruct(raw_all.shape,...  67.5 us
    pallas_call x1, Pallas kernels, score(): pl.pallas_call(functools.partial(score_body, tok_total), out_shape=(rows[...  58 us
    pallas_call x1, Pallas kernels, scatter_rows(): pl.pallas_call(functools.partial(scatter_body, tok_total), out_shape=tupl...  35.5 us
    pallas_call x1, Pallas kernels, pick_rows(): pl.pallas_call(pick_body, out_shape=(jax.ShapeDtypeStruct((n_cand, width)...  21 us
    pallas_call x1, Pallas kernels, prepare(): pl.pallas_call(functools.partial(prepare_body, rows_loc), out_shape=(jax....  10.1 us

profile of v10, /device:TPU:0, one launch (start us, length us, event | category | flops | bytes accessed | tf_op | source)
XLA Modules:
  0.0 192.9 jit_solution(4045327923637093869)
XLA Ops:
  0.6 10.1 %prepare.1 = (s32[96,128]{1,0:T(8,128)}, bf16[1024,256]{1,0:T(8,128)(2,1)}) custom-call(s32[8,128]{1,0:T(8,128)} %bitcast.19, s32[32,128]{1,0:T(8,128)} %bitcast.16, bf16[1024,1024]{1,0:T(8,128)(2,1)} %tok_hbm.1, bf16[1024,512]{1,0:T(8,128)(2,1)} %rest_5_.1, bf16[512,256]{1,0:T(8,128)(2,1)} %rest_6_.1), custom_call_target="tpu_custom_call" | custom-call | tf_op jit(solution)/shard_map/prepare/pallas_call | solution.py:546
  10.7 21.0 %pick_rows.1 = (bf16[4096,256]{1,0:T(8,128)(2,1)}, bf16[8192,256]{1,0:T(8,128)(2,1)}) custom-call(s32[96,128]{1,0:T(8,128)} %get-tuple-element.29.ids_s.ids_v, bf16[32768,256]{1,0:T(8,128)(2,1)} %table.1), custom_call_target="tpu_custom_call" | custom-call | tf_op jit(solution)/shard_map/pick_rows/pallas_call | solution.py:104
  31.7 58.0 %score.1 = (bf16[512,256]{1,0:T(8,128)(2,1)}, bf16[1024,256]{1,0:T(8,128)(2,1)}, f32[8,128]{1,0:T(8,128)}, bf16[1024,256]{1,0:T(8,128)(2,1)}, bf16[1024,256]{1,0...) custom-call(bf16[2,2,2,512,256]{4,3,2,1,0:T(8,128)(2,1)} %bitcast.15, ...), custom_call_target="tpu_custom_call" | custom-call | tf_op jit(solution)/shard_map/score/pallas_call | solution.py:653
  89.7 67.5 %back_rows.1 = (bf16[2,2,2,1024,256]{4,3,2,1,0:T(8,128)(2,1)}, bf16[2,2,2,512,256]{4,3,2,1,0:T(8,128)(2,1)}, f32[2,2,2,320,256]{4,3,2,1,0:T(8,128)}, f32[2,2,2,128,256]{4,3,2,1,0:T(8,128)}, f32[8,128]{1,0:T(8,128)}) custom-call(f32[2,2,2,512,256]{4,3,2,1,0:T(8,128)} %bitcast.14, bf16[1024,1024]{1,0:T(8,128)(2,1)} %tok_hbm.1, ...), custom_call_target="tpu_custom_call" | custom-call | tf_op jit(solution)/shard_map/back_rows/pallas_call | solution.py:825
  157.2 35.5 %scatter_rows.1 = (f32[32768,256]{1,0:T(8,128)}, f32[1024,512]{1,0:T(8,128)}, f32[512,256]{1,0:T(8,128)}, f32[256,512]{1,0:T(8,128)}, f32[512,256]{1,0:T(8,128)}, /*index=5*/f32[1,1]{1,0:T(1,128)}) custom-call(s32[96,128]{1,0:T(8,128)} %get-tuple-element.29.ids_s.ids_v, s32[96,128]{1,0:T(8,128)} %get-tuple-element.29.ids_s.ids_v, ...), custom_call_target="tpu_custom_call" | custom-call | flops 60000002048 | bytes 41943040 | tf_op jit(solution)/shard_map/scatter_rows/pallas_call | solution.py:233

commit v11 on v10

--- a/solution.py
+++ b/solution.py
@@ -590,9 +590,9 @@
         reduces[k].one()
     reduces[0].two()
     reduces[1].two()
-    reduces[2].two()
     reduces[0].three()
     reduces[1].three()
+    reduces[2].two()
     reduces[3].two()
 
     @pl.loop(0, n_cand // 128)

time: 194 us -> 195 us (level)
  no operation moved by 1% of the time
where the time goes in v11:
time: 195 us; the launch traced here: 194 us
  Pallas kernels  193 us (99%)
    pallas_call x1, Pallas kernels, back_rows(): pl.pallas_call(back_body, out_shape=(jax.ShapeDtypeStruct(raw_all.shape,...  68.3 us
    pallas_call x1, Pallas kernels, score(): pl.pallas_call(functools.partial(score_body, tok_total), out_shape=(rows[...  58.5 us
    pallas_call x1, Pallas kernels, scatter_rows(): pl.pallas_call(functools.partial(scatter_body, tok_total), out_shape=tupl...  35.3 us
    pallas_call x1, Pallas kernels, pick_rows(): pl.pallas_call(pick_body, out_shape=(jax.ShapeDtypeStruct((n_cand, width)...  21 us
    pallas_call x1, Pallas kernels, prepare(): pl.pallas_call(functools.partial(prepare_body, rows_loc), out_shape=(jax....  10.1 us

profile of v11, /device:TPU:0, one launch (start us, length us, event | category | flops | bytes accessed | tf_op | source)
XLA Modules:
  0.0 194.0 jit_solution(15057592923370008692)
XLA Ops:
  0.6 10.1 %prepare.1 = (s32[96,128]{1,0:T(8,128)}, bf16[1024,256]{1,0:T(8,128)(2,1)}) custom-call(s32[8,128]{1,0:T(8,128)} %bitcast.19, s32[32,128]{1,0:T(8,128)} %bitcast.16, bf16[1024,1024]{1,0:T(8,128)(2,1)} %tok_hbm.1, bf16[1024,512]{1,0:T(8,128)(2,1)} %rest_5_.1, bf16[512,256]{1,0:T(8,128)(2,1)} %rest_6_.1), custom_call_target="tpu_custom_call" | custom-call | tf_op jit(solution)/shard_map/prepare/pallas_call | solution.py:546
  10.7 21.0 %pick_rows.1 = (bf16[4096,256]{1,0:T(8,128)(2,1)}, bf16[8192,256]{1,0:T(8,128)(2,1)}) custom-call(s32[96,128]{1,0:T(8,128)} %get-tuple-element.29.ids_s.ids_v, bf16[32768,256]{1,0:T(8,128)(2,1)} %table.1), custom_call_target="tpu_custom_call" | custom-call | tf_op jit(solution)/shard_map/pick_rows/pallas_call | solution.py:104
  31.7 58.5 %score.1 = (bf16[512,256]{1,0:T(8,128)(2,1)}, bf16[1024,256]{1,0:T(8,128)(2,1)}, f32[8,128]{1,0:T(8,128)}, bf16[1024,256]{1,0:T(8,128)(2,1)}, bf16[1024,256]{1,0...) custom-call(bf16[2,2,2,512,256]{4,3,2,1,0:T(8,128)(2,1)} %bitcast.15, ...), custom_call_target="tpu_custom_call" | custom-call | tf_op jit(solution)/shard_map/score/pallas_call | solution.py:653
  90.2 68.3 %back_rows.1 = (bf16[2,2,2,1024,256]{4,3,2,1,0:T(8,128)(2,1)}, bf16[2,2,2,512,256]{4,3,2,1,0:T(8,128)(2,1)}, f32[2,2,2,320,256]{4,3,2,1,0:T(8,128)}, f32[2,2,2,128,256]{4,3,2,1,0:T(8,128)}, f32[8,128]{1,0:T(8,128)}) custom-call(f32[2,2,2,512,256]{4,3,2,1,0:T(8,128)} %bitcast.14, bf16[1024,1024]{1,0:T(8,128)(2,1)} %tok_hbm.1, ...), custom_call_target="tpu_custom_call" | custom-call | tf_op jit(solution)/shard_map/back_rows/pallas_call | solution.py:825
  158.5 35.3 %scatter_rows.1 = (f32[32768,256]{1,0:T(8,128)}, f32[1024,512]{1,0:T(8,128)}, f32[512,256]{1,0:T(8,128)}, f32[256,512]{1,0:T(8,128)}, f32[512,256]{1,0:T(8,128)}, /*index=5*/f32[1,1]{1,0:T(1,128)}) custom-call(s32[96,128]{1,0:T(8,128)} %get-tuple-element.29.ids_s.ids_v, s32[96,128]{1,0:T(8,128)} %get-tuple-element.29.ids_s.ids_v, ...), custom_call_target="tpu_custom_call" | custom-call | flops 60000002048 | bytes 41943040 | tf_op jit(solution)/shard_map/scatter_rows/pallas_call | solution.py:233
